TPU v7x, 128 devices: a whole 4x4x4 slice. The times are simulated.
128 devices in a mesh: sp: 2 (over core), dp: 64 (over z, y, x).
Axes of the slice: x: 4, y: 4, z: 4, core: 2. Of those that a mesh axis runs over, the one named last changes fastest.
Arguments:
- node_lat: bfloat16 [64, 512, 512], P('dp', 'sp')
- edge_lat: bfloat16 [64, 4096, 512], P('dp', 'sp')
- senders: int32 [4096], P('sp')
- edge_mask: int32 [4096], P('sp')
- node_cot: bfloat16 [64, 512, 512], P('dp', 'sp')
- edge_cot: bfloat16 [64, 4096, 512], P('dp', 'sp')
- w_edge1: float32 [2, 1536, 512], P(None, 'dp')
- w_edge2: float32 [2, 512, 512], P(None, 'dp')
- w_node1: float32 [2, 1024, 512], P(None, 'dp')
- w_node2: float32 [2, 512, 512], P(None, 'dp')
- norm_par: float32 [2, 4, 512], P(None, None, 'dp')
- mom_edge1: float32 [2, 1536, 512], P(None, 'dp')
- mom_edge2: float32 [2, 512, 512], P(None, 'dp')
- mom_node1: float32 [2, 1024, 512], P(None, 'dp')
- mom_node2: float32 [2, 512, 512], P(None, 'dp')
- mom_norm: float32 [2, 4, 512], P(None, None, 'dp')
- vel_edge1: float32 [2, 1536, 512], P(None, 'dp')
- vel_edge2: float32 [2, 512, 512], P(None, 'dp')
- vel_node1: float32 [2, 1024, 512], P(None, 'dp')
- vel_node2: float32 [2, 512, 512], P(None, 'dp')
- vel_norm: float32 [2, 4, 512], P(None, None, 'dp')
Outputs:
- output 1: float32 [2, 1536, 512], P(None, 'dp')
- output 2: float32 [2, 512, 512], P(None, 'dp')
- output 3: float32 [2, 1024, 512], P(None, 'dp')
- output 4: float32 [2, 512, 512], P(None, 'dp')
- output 5: float32 [2, 4, 512], P(None, None, 'dp')
- output 6: float32 [2, 1536, 512], P(None, 'dp')
- output 7: float32 [2, 512, 512], P(None, 'dp')
- output 8: float32 [2, 1024, 512], P(None, 'dp')
- output 9: float32 [2, 512, 512], P(None, 'dp')
- output 10: float32 [2, 4, 512], P(None, None, 'dp')
- output 11: float32 [2, 1536, 512], P(None, 'dp')
- output 12: float32 [2, 512, 512], P(None, 'dp')
- output 13: float32 [2, 1024, 512], P(None, 'dp')
- output 14: float32 [2, 512, 512], P(None, 'dp')
- output 15: float32 [2, 4, 512], P(None, None, 'dp')
- output 16: bfloat16 [64, 512, 512], P('dp', 'sp')
- output 17: bfloat16 [64, 4096, 512], P('dp', 'sp')
All inputs are finite; a program needn't handle non-finite values.
Results may differ from a plain program's by a relative error of at most 0.02.
Values are sent between devices in bfloat16 or wider.
A program may use at most 1 GiB of HBM per device.

v0:
```python
import jax
import jax.numpy as jnp
from jax import lax
from jax.sharding import PartitionSpec as P

NORM_EPS = 1e-5
LEARN_RATE = 1e-3
BETA_ONE = 0.9
BETA_TWO = 0.95
ADAM_EPS = 1e-8
DECAY = 0.1
STEP = 10


def contract(left_op, right_op, left_dims, right_dims):
    return lax.dot_general(left_op, right_op, ((left_dims, right_dims), ((), ())), preferred_element_type=jnp.float32)


def norm_forward(out_b, norm_gain, norm_bias):
    values = out_b.astype(jnp.float32)
    centered = values - jnp.mean(values, axis=-1, keepdims=True)
    inv_std = lax.rsqrt(jnp.mean(centered * centered, axis=-1, keepdims=True) + NORM_EPS)
    normed = centered * inv_std
    return normed * norm_gain + norm_bias, normed, inv_std


def mlp_tail(pre_act, w_two, norm_gain, norm_bias):
    pre_b = pre_act.astype(jnp.bfloat16)
    hidden_act = jax.nn.silu(pre_b.astype(jnp.float32)).astype(jnp.bfloat16)
    last_dim = hidden_act.ndim - 1
    out_b = contract(hidden_act, w_two, (last_dim,), (0,)).astype(jnp.bfloat16)
    branch, normed, inv_std = norm_forward(out_b, norm_gain, norm_bias)
    return branch, (pre_b, hidden_act, normed, inv_std)


def mlp_back(d_branch, saved, w_one, w_two, norm_gain):
    pre_b, hidden_act, normed, inv_std = saved
    last_dim = hidden_act.ndim - 1
    lead_dims = tuple(range(last_dim))
    d_gain = jnp.sum(d_branch * normed, axis=lead_dims)
    d_bias = jnp.sum(d_branch, axis=lead_dims)
    d_norm = d_branch * norm_gain
    d_out = (inv_std * (d_norm - jnp.mean(d_norm, axis=-1, keepdims=True) - normed * jnp.mean(d_norm * normed, axis=-1, keepdims=True))).astype(jnp.bfloat16)
    d_two = contract(hidden_act, d_out, lead_dims, lead_dims)
    d_act = contract(d_out, w_two, (last_dim,), (1,)).astype(jnp.bfloat16)
    pre_f = pre_b.astype(jnp.float32)
    gate_sig = jax.nn.sigmoid(pre_f)
    d_pre = (d_act.astype(jnp.float32) * gate_sig * (1.0 + pre_f * (1.0 - gate_sig))).astype(jnp.bfloat16)
    d_in = contract(d_pre, w_one, (last_dim,), (1,))
    return d_pre, d_in, d_two, d_gain, d_bias


def layer_forward(node_x, node_all, edge_x, senders, mask_b, layer_wts):
    w_e1, w_e2, w_n1, w_n2, norm_rows = layer_wts
    lat_width = node_x.shape[-1]
    sender_lat = jnp.take(node_all, senders, axis=1).reshape(edge_x.shape)
    pre_e = (contract(edge_x, w_e1[:lat_width], (3,), (0,))
             + contract(sender_lat, w_e1[lat_width:2 * lat_width], (3,), (0,))
             + contract(node_x, w_e1[2 * lat_width:], (2,), (0,))[:, :, None, :])
    branch_e, saved_e = mlp_tail(pre_e, w_e2, norm_rows[0], norm_rows[1])
    edge_new = (edge_x.astype(jnp.float32) + branch_e).astype(jnp.bfloat16)
    node_sum = jnp.einsum('bngd,ng->bnd', edge_new, mask_b, preferred_element_type=jnp.float32).astype(jnp.bfloat16)
    pre_n = contract(node_x, w_n1[:lat_width], (2,), (0,)) + contract(node_sum, w_n1[lat_width:], (2,), (0,))
    branch_n, saved_n = mlp_tail(pre_n, w_n2, norm_rows[2], norm_rows[3])
    node_new = (node_x.astype(jnp.float32) + branch_n).astype(jnp.bfloat16)
    return node_new, edge_new, (sender_lat, node_sum, saved_e, saved_n)


def layer_backward(d_node_new, d_edge_new, node_x, edge_x, senders, mask_f, saved, layer_wts, total_nodes):
    w_e1, w_e2, w_n1, w_n2, norm_rows = layer_wts
    sender_lat, node_sum, saved_e, saved_n = saved
    batch_size, tile_nodes, degree, lat_width = edge_x.shape
    d_res_n = d_node_new.astype(jnp.float32)
    d_pre_n, d_in_n, d_wn2, d_gain_n, d_bias_n = mlp_back(d_res_n, saved_n, w_n1, w_n2, norm_rows[2])
    d_wn1 = jnp.concatenate([contract(node_x, d_pre_n, (0, 1), (0, 1)), contract(node_sum, d_pre_n, (0, 1), (0, 1))], axis=0)
    d_sum = d_in_n[..., lat_width:].astype(jnp.bfloat16)
    d_res_e = (d_edge_new.astype(jnp.float32) + d_sum.astype(jnp.float32)[:, :, None, :] * mask_f[None, :, :, None]).astype(jnp.bfloat16).astype(jnp.float32)
    d_pre_e, d_in_e, d_we2, d_gain_e, d_bias_e = mlp_back(d_res_e, saved_e, w_e1, w_e2, norm_rows[0])
    recv_grad = contract(node_x, d_pre_e.reshape(batch_size, tile_nodes, -1), (0, 1), (0, 1))
    d_we1 = jnp.concatenate([contract(edge_x, d_pre_e, (0, 1, 2), (0, 1, 2)), contract(sender_lat, d_pre_e, (0, 1, 2), (0, 1, 2)), recv_grad.reshape(lat_width, degree, -1).sum(axis=1)], axis=0)
    d_edge_x = (d_res_e + d_in_e[..., :lat_width]).astype(jnp.bfloat16)
    d_sender = d_in_e[..., lat_width:2 * lat_width].reshape(batch_size, tile_nodes * degree, lat_width)
    scattered = jnp.zeros((batch_size, total_nodes, lat_width), jnp.float32).at[:, senders].add(d_sender)
    d_local = d_res_n + d_in_n[..., :lat_width] + d_in_e[..., 2 * lat_width:].sum(axis=2)
    grads = (d_we1, d_we2, d_wn1, d_wn2, jnp.stack([d_gain_e, d_bias_e, d_gain_n, d_bias_n]))
    return d_local, scattered, d_edge_x, grads


def adamw_update(master, grad_sum, moment_one, moment_two):
    corr_one = 1.0 - BETA_ONE ** STEP
    corr_two = 1.0 - BETA_TWO ** STEP
    one_new = BETA_ONE * moment_one + (1.0 - BETA_ONE) * grad_sum
    two_new = BETA_TWO * moment_two + (1.0 - BETA_TWO) * grad_sum * grad_sum
    direction = (one_new / corr_one) / (jnp.sqrt(two_new / corr_two) + ADAM_EPS)
    return master - LEARN_RATE * (direction + DECAY * master), one_new, two_new


def update_all(masters, moments_one, moments_two, layer_grads):
    new_master = []
    new_one = []
    new_two = []
    for slot in range(len(masters)):
        grad_sum = jnp.stack([per_layer[slot] for per_layer in layer_grads], axis=0)
        master_new, one_new, two_new = adamw_update(masters[slot], grad_sum, moments_one[slot], moments_two[slot])
        new_master.append(master_new)
        new_one.append(one_new)
        new_two.append(two_new)
    return tuple(new_master) + tuple(new_one) + tuple(new_two)


def gather_weights(masters, layer_idx):
    mat_list = [lax.all_gather(master[layer_idx].astype(jnp.bfloat16), 'dp', axis=0, tiled=True) for master in masters[:4]]
    norm_rows = lax.all_gather(masters[4][layer_idx].astype(jnp.bfloat16), 'dp', axis=1, tiled=True).astype(jnp.float32)
    return mat_list[0], mat_list[1], mat_list[2], mat_list[3], norm_rows


def reduce_grads(grads):
    mat_list = [lax.psum(lax.psum_scatter(grad_full, 'dp', scatter_dimension=0, tiled=True), 'sp') for grad_full in grads[:4]]
    norm_grad = lax.psum(lax.psum_scatter(grads[4], 'dp', scatter_dimension=1, tiled=True), 'sp')
    return mat_list[0], mat_list[1], mat_list[2], mat_list[3], norm_grad


def solution(mesh):
    lat_spec = P('dp', 'sp', None)
    edge_spec = P('sp')
    mat_spec = P(None, 'dp', None)
    norm_spec = P(None, None, 'dp')
    param_specs = (mat_spec, mat_spec, mat_spec, mat_spec, norm_spec)
    tile_count = mesh.shape['sp']

    def train_step(node_lat, edge_lat, senders, edge_mask, node_cot, edge_cot, w_edge1, w_edge2, w_node1, w_node2, norm_par, mom_edge1, mom_edge2, mom_node1, mom_node2, mom_norm, vel_edge1, vel_edge2, vel_node1, vel_node2, vel_norm):
        masters = (w_edge1, w_edge2, w_node1, w_node2, norm_par)
        moments_one = (mom_edge1, mom_edge2, mom_node1, mom_node2, mom_norm)
        moments_two = (vel_edge1, vel_edge2, vel_node1, vel_node2, vel_norm)
        batch_size, tile_nodes, lat_width = node_lat.shape
        degree = edge_lat.shape[1] // tile_nodes
        total_nodes = tile_nodes * tile_count
        layers = w_edge1.shape[0]
        mask_f = edge_mask.astype(jnp.float32).reshape(tile_nodes, degree)
        mask_b = mask_f.astype(jnp.bfloat16)
        node_x = node_lat
        edge_x = edge_lat.reshape(batch_size, tile_nodes, degree, lat_width)
        records = []
        for layer_idx in range(layers):
            layer_wts = gather_weights(masters, layer_idx)
            node_all = lax.all_gather(node_x, 'sp', axis=1, tiled=True)
            node_new, edge_new, saved = layer_forward(node_x, node_all, edge_x, senders, mask_b, layer_wts)
            records.append((node_x, edge_x, saved))
            node_x = node_new
            edge_x = edge_new
        d_node = node_cot
        d_edge = edge_cot.reshape(batch_size, tile_nodes, degree, lat_width)
        grads_rev = []
        for layer_idx in reversed(range(layers)):
            layer_wts = gather_weights(masters, layer_idx)
            node_in, edge_in, saved = records[layer_idx]
            d_local, scattered, d_edge, grads = layer_backward(d_node, d_edge, node_in, edge_in, senders, mask_f, saved, layer_wts, total_nodes)
            returned = lax.psum_scatter(scattered, 'sp', scatter_dimension=1, tiled=True)
            d_node = (d_local + returned).astype(jnp.bfloat16)
            grads_rev.append(reduce_grads(grads))
        new_state = update_all(masters, moments_one, moments_two, grads_rev[::-1])
        return new_state + (d_node, d_edge.reshape(edge_lat.shape))

    return jax.shard_map(train_step, mesh=mesh, in_specs=(lat_spec, lat_spec, edge_spec, edge_spec, lat_spec, lat_spec) + param_specs + param_specs + param_specs, out_specs=param_specs + param_specs + param_specs + (lat_spec, lat_spec), check_vma=False)
```

profile of v0, /device:TPU:1, one launch (start us, length us, event | category | flops | bytes accessed | tf_op | source)
XLA Modules:
  0.0 3829.2 jit_solution(12434027982458576818)
XLA Ops:
  17.7 152.4 %all-gather.8 = bf16[1,4,512]{1,0,2:T(2,128)(2,1)S(1)} all-gather(bf16[1,4,8]{1,0,2:T(2,128)(2,1)S(1)} %get-tuple-element.88), channel_id=10, replica_groups=mesh['sp'=2,'dp'=64] {'dp'}, dimensions={2}, use_global_device_ids=true | all-gather | bytes 4160 | tf_op jit(solution)/shard_map/all_gather | solution.py:113
  170.3 4.8 slice_reduce_fusion.2
  175.1 143.3 %all-gather.3 = bf16[1,4,512]{1,0,2:T(2,128)(2,1)S(1)} all-gather(bf16[1,4,8]{1,0,2:T(2,128)(2,1)S(1)} %get-tuple-element.89), channel_id=5, replica_groups=mesh['sp'=2,'dp'=64] {'dp'}, dimensions={2}, use_global_device_ids=true | all-gather | bytes 4160 | tf_op jit(solution)/shard_map/all_gather | solution.py:113
  318.7 6.7 slice_reduce_fusion.6
  325.4 145.9 %all-gather.9 = bf16[1,512,512]{2,1,0:T(8,128)(2,1)} all-gather(bf16[1,8,512]{2,1,0:T(8,128)(2,1)S(1)} %get-tuple-element.82), channel_id=11, replica_groups=mesh['sp'=2,'dp'=64] {'dp'}, dimensions={1}, use_global_device_ids=true | all-gather | bytes 532480 | tf_op jit(solution)/shard_map/all_gather | solution.py:112
  471.3 145.1 %all-gather.7 = bf16[1,512,512]{2,1,0:T(8,128)(2,1)} all-gather(bf16[1,8,512]{2,1,0:T(8,128)(2,1)S(1)} %get-tuple-element.84), channel_id=9, replica_groups=mesh['sp'=2,'dp'=64] {'dp'}, dimensions={1}, use_global_device_ids=true | all-gather | bytes 532480 | tf_op jit(solution)/shard_map/all_gather | solution.py:112
  616.4 145.5 %all-gather.4 = bf16[1,512,512]{2,1,0:T(8,128)(2,1)} all-gather(bf16[1,8,512]{2,1,0:T(8,128)(2,1)S(1)} %get-tuple-element.83), channel_id=6, replica_groups=mesh['sp'=2,'dp'=64] {'dp'}, dimensions={1}, use_global_device_ids=true | all-gather | bytes 532480 | tf_op jit(solution)/shard_map/all_gather | solution.py:112
  761.9 145.4 %all-gather.1 = bf16[1,512,512]{2,1,0:T(8,128)(2,1)S(1)} all-gather(bf16[1,8,512]{2,1,0:T(8,128)(2,1)S(1)} %get-tuple-element.85), channel_id=3, replica_groups=mesh['sp'=2,'dp'=64] {'dp'}, dimensions={1}, use_global_device_ids=true | all-gather | bytes 532480 | tf_op jit(solution)/shard_map/all_gather | solution.py:112
  907.3 167.9 %all_gather.47 = bf16[1,512,512]{2,1,0:T(8,128)(2,1)S(1)} all-gather(bf16[1,256,512]{2,1,0:T(8,128)(2,1)S(1)} %copy-done.15), channel_id=1, replica_groups=mesh['sp'=2,'dp'=64] {'sp'}, dimensions={1}, use_global_device_ids=true | all-gather | bytes 786432 | tf_op jit(solution)/shard_map/all_gather | solution.py:146
  1075.2 4.4 convert_bitcast_fusion.1
  1079.6 9.2 gather_fusion
  1088.8 2.9 fusion.66
  1095.2 2.7 fusion.79
  1097.9 2.9 add_convert_fusion.2
  1107.7 2.4 all_gather.54
  1110.1 9.2 gather_fusion.1
  1119.3 2.9 fusion.65
  1126.1 2.9 add_convert_fusion.1
  1146.2 6.7 fusion.30
  1154.3 3.6 fusion.46
  1159.2 3.5 convolution_bitcast_fusion.1
  1162.7 4.8 slice_reduce_fusion.1
  1168.6 17.5 scatter_custom_fusion
  1186.2 2.4 fusion.176
  1188.9 6.1 convolution_bitcast_fusion.3
  1209.1 8.0 fusion.48
  1218.4 4.0 fusion.88
  1222.7 4.7 fusion.94
  1227.4 3.9 copy.111
  1231.3 3.1 convolution_reduce_fusion
  1237.8 5.9 fusion.39
  1243.7 4.0 copy.107
  1250.0 4.0 convolution_reduce_fusion.1
  1255.6 4.1 fusion.85
  1263.5 5.5 convolution_bitcast_fusion
  1269.0 6.6 fusion.49
  1275.7 17.7 scatter_custom_fusion.1
  1295.4 2.5 copy.186
  1298.7 291.8 %all-reduce.2 = (f32[4,512]{1,0:T(4,128)S(1)}, f32[4,512]{1,0:T(4,128)S(1)}) all-reduce(f32[4,512]{1,0:T(4,128)S(1)} %pad_maximum_fusion.4, f32[4,512]{1,0:T(4,128)S(1)} %pad_maximum_fusion.5), channel_id=21, replica_groups=mesh['sp'=2,'dp'=64] {'dp'}, use_global_device_ids=true, to_apply=%region_41.43.clone | all-reduce | flops 4096 | bytes 32768
  1591.8 260.6 %reduce-scatter.21.cloned.1.call-done = f32[8,512]{1,0:T(8,128)} async-done(((f32[512,512]{1,0:T(8,128)}), f32[8,512]{1,0:T(8,128)}) %reduce-scatter.21.cloned.1.call-update) | async-done | bytes 16400 | tf_op jit(solution)/shard_map/reduce_scatter | solution.py:118
  1852.4 354.4 %reduce-scatter.25.cloned.1.call-done = f32[16,512]{1,0:T(8,128)} async-done(((f32[1024,512]{1,0:T(8,128)}), f32[16,512]{1,0:T(8,128)}) %reduce-scatter.25.cloned.1.call-update) | async-done | bytes 32784 | tf_op jit(solution)/shard_map/reduce_scatter | solution.py:118
  2206.9 352.7 %reduce-scatter.27.cloned.1.call-done = f32[8,512]{1,0:T(8,128)} async-done(((f32[512,512]{1,0:T(8,128)}), f32[8,512]{1,0:T(8,128)}) %reduce-scatter.27.cloned.1.call-update) | async-done | bytes 16400 | tf_op jit(solution)/shard_map/reduce_scatter | solution.py:118
  2559.5 352.4 %reduce-scatter.19.cloned.1.call-done = f32[8,512]{1,0:T(8,128)} async-done(((f32[512,512]{1,0:T(8,128)}), f32[8,512]{1,0:T(8,128)}) %reduce-scatter.19.cloned.1.call-update) | async-done | bytes 16400 | tf_op jit(solution)/shard_map/reduce_scatter | solution.py:118
  2912.0 272.0 %reduce-scatter.17.cloned.1.call-done = f32[24,512]{1,0:T(8,128)} async-done(((f32[1536,512]{1,0:T(8,128)}), f32[24,512]{1,0:T(8,128)}) %reduce-scatter.17.cloned.1.call-update) | async-done | bytes 49168 | tf_op jit(solution)/shard_map/reduce_scatter | solution.py:118
  3183.9 307.7 %reduce-scatter.23.cloned.1.call-done = f32[16,512]{1,0:T(8,128)} async-done(((f32[1024,512]{1,0:T(8,128)}), f32[16,512]{1,0:T(8,128)}) %reduce-scatter.23.cloned.1.call-update) | async-done | bytes 32784 | tf_op jit(solution)/shard_map/reduce_scatter | solution.py:118
  3491.6 272.5 %reduce-scatter.15.cloned.1.call-done = f32[24,512]{1,0:T(8,128)} async-done(((f32[1536,512]{1,0:T(8,128)}), f32[24,512]{1,0:T(8,128)}) %reduce-scatter.15.cloned.1.call-update) | async-done | bytes 49168 | tf_op jit(solution)/shard_map/reduce_scatter | solution.py:118
  3764.2 13.4 reduce-scatter.31.cloned.1.call-done
  3779.6 27.7 all-reduce.6.cloned.1.call-done
  (301 shorter events, 92.6 us)
Async XLA Ops:
  7.2 900.1 %copy-start.15 = (bf16[1,256,512]{2,1,0:T(8,128)(2,1)S(1)}, bf16[1,256,512]{2,1,0:T(8,128)(2,1)}, u32[]{:S(2)}) copy-start(bf16[1,256,512]{2,1,0:T(8,128)(2,1)} %param.23) | copy-start | bytes 786436
  7.2 1068.0 %copy-start.10 = (bf16[1,2048,512]{2,1,0:T(8,128)(2,1)S(1)}, bf16[1,2048,512]{2,1,0:T(8,128)(2,1)}, u32[]{:S(2)}) copy-start(bf16[1,2048,512]{2,1,0:T(8,128)(2,1)} %param.28) | copy-start | bytes 6291460
  7.2 1084.5 %all-gather.17.cloned.1.call-start = ((), (), s32[]{:S(2)}) async-start(), calls=%async_computation.21 | async-start | bytes 1064960 | tf_op jit(solution)/shard_map/all_gather | solution.py:112
  8.9 1084.9 %all-gather.15.cloned.1.call-start = ((), (), s32[]{:S(2)}) async-start(), calls=%async_computation.20 | async-start | bytes 1597440 | tf_op jit(solution)/shard_map/all_gather | solution.py:112
  10.5 1111.8 %all-gather.21.cloned.1.call-start = ((), (), s32[]{:S(2)}) async-start(), calls=%async_computation.23 | async-start | bytes 1597440 | tf_op jit(solution)/shard_map/all_gather | solution.py:112
  11.2 1123.4 %all-gather.19.cloned.1.call-start = ((), (), s32[]{:S(2)}) async-start(), calls=%async_computation.22 | async-start | bytes 1064960 | tf_op jit(solution)/shard_map/all_gather | solution.py:112
  11.8 1187.7 %reduce-scatter.13.cloned.1.call-start = ((), (), s32[]{:S(2)}) async-start(), calls=%async_computation.10 | async-start | bytes 1572864 | tf_op jit(solution)/shard_map/reduce_scatter | solution.py:158
  14.6 747.4 %copy-start.57 = (f32[2048]{0:T(1024)}, f32[2048]{0:T(1024)S(1)}, u32[]{:S(2)}) copy-start(f32[2048]{0:T(1024)S(1)} %convert_element_type.345) | copy-start | bytes 24580
  175.1 956.4 %copy-start.64 = (f32[512]{0:T(512)}, f32[512]{0:T(512)S(1)}, u32[]{:S(2)}) copy-start(f32[512]{0:T(512)S(1)} %get-tuple-element.36) | copy-start | bytes 6148
  175.1 963.1 %copy-start.73 = (f32[512]{0:T(512)}, f32[512]{0:T(512)S(1)}, u32[]{:S(2)}) copy-start(f32[512]{0:T(512)S(1)} %get-tuple-element.34) | copy-start | bytes 6148
  325.4 777.9 %copy-start.71 = (f32[512]{0:T(512)}, f32[512]{0:T(512)S(1)}, u32[]{:S(2)}) copy-start(f32[512]{0:T(512)S(1)} %get-tuple-element.39) | copy-start | bytes 6148
  325.4 782.1 %copy-start.62 = (f32[512]{0:T(512)}, f32[512]{0:T(512)S(1)}, u32[]{:S(2)}) copy-start(f32[512]{0:T(512)S(1)} %get-tuple-element.37) | copy-start | bytes 6148
  907.3 193.4 %copy-start.43 = (bf16[1,512,512]{2,1,0:T(8,128)(2,1)}, bf16[1,512,512]{2,1,0:T(8,128)(2,1)S(1)}, u32[]{:S(2)}) copy-start(bf16[1,512,512]{2,1,0:T(8,128)(2,1)S(1)} %all-gather.1) | copy-start | bytes 1572868
  1088.8 6.4 copy-start
  1107.2 12.1 copy-start.67
  1107.4 11.9 copy-start.69
  1107.7 27.0 copy-start.17
  1134.7 5.4 copy-start.51
  1140.1 6.1 copy-start.8
  1146.1 8.1 copy-start.49
  1146.1 8.1 copy-start.61
  1146.1 8.1 copy-start.66
  1146.1 8.1 copy-start.76
  1146.1 8.1 copy-start.82
  1162.6 6.0 copy-start.9
  1186.2 405.6 %reduce-scatter.29.cloned.1.call-start = ((), (), s32[]{:S(2)}) async-start(), calls=%async_computation.18 | async-start | bytes 1064960 | tf_op jit(solution)/shard_map/reduce_scatter | solution.py:118
  1188.6 7.8 copy-start.18
  1188.7 663.8 %reduce-scatter.21.cloned.1.call-start = ((), (), s32[]{:S(2)}) async-start(), calls=%async_computation.14 | async-start | bytes 1064960 | tf_op jit(solution)/shard_map/reduce_scatter | solution.py:118
  1195.0 1011.9 %reduce-scatter.25.cloned.1.call-start = ((), (), s32[]{:S(2)}) async-start(), calls=%async_computation.16 | async-start | bytes 2129920 | tf_op jit(solution)/shard_map/reduce_scatter | solution.py:118
  1199.5 1360.1 %reduce-scatter.27.cloned.1.call-start = ((), (), s32[]{:S(2)}) async-start(), calls=%async_computation.17 | async-start | bytes 1064960 | tf_op jit(solution)/shard_map/reduce_scatter | solution.py:118
  1201.6 6.0 copy-start.41
  1203.9 5.1 copy-start.3
  1209.0 1703.0 %reduce-scatter.19.cloned.1.call-start = ((), (), s32[]{:S(2)}) async-start(), calls=%async_computation.13 | async-start | bytes 1064960 | tf_op jit(solution)/shard_map/reduce_scatter | solution.py:118
  1209.1 9.3 copy-start.80
  1222.4 1961.5 %reduce-scatter.17.cloned.1.call-start = ((), (), s32[]{:S(2)}) async-start(), calls=%async_computation.12 | async-start | bytes 3194880 | tf_op jit(solution)/shard_map/reduce_scatter | solution.py:118
  1237.7 2253.9 %reduce-scatter.23.cloned.1.call-start = ((), (), s32[]{:S(2)}) async-start(), calls=%async_computation.15 | async-start | bytes 2129920 | tf_op jit(solution)/shard_map/reduce_scatter | solution.py:118
  1249.9 5.6 copy-start.1
  1250.0 2514.2 %reduce-scatter.15.cloned.1.call-start = ((), (), s32[]{:S(2)}) async-start(), calls=%async_computation.11 | async-start | bytes 3194880 | tf_op jit(solution)/shard_map/reduce_scatter | solution.py:118
  1263.2 2514.3 %reduce-scatter.31.cloned.1.call-start = ((), (), s32[]{:S(2)}) async-start(), calls=%async_computation.19 | async-start | bytes 1572864 | tf_op jit(solution)/shard_map/reduce_scatter | solution.py:158
  1275.7 17.8 copy-start.78
  1275.7 19.0 copy-start.75
  1275.7 19.8 copy-start.13
  1275.7 2501.9 %copy-start.22 = (f32[1,256,1024]{2,1,0:T(8,128)S(1)}, f32[1,256,1024]{2,1,0:T(8,128)}, u32[]{:S(2)}) copy-start(f32[1,256,1024]{2,1,0:T(8,128)} %copy-done.21) | copy-start | bytes 3145732
  1275.7 2501.9 %copy-start.28 = (bf16[1,256,512]{2,1,0:T(8,128)(2,1)S(1)}, bf16[1,256,512]{2,1,0:T(8,128)(2,1)}, u32[]{:S(2)}) copy-start(bf16[1,256,512]{2,1,0:T(8,128)(2,1)} %copy-done.27) | copy-start | bytes 786436
  1293.3 2521.4 %copy-start.74 = (f32[2,4,8]{2,1,0:T(4,128)S(1)}, f32[2,4,8]{2,1,0:T(4,128)}, u32[]{:S(2)}) copy-start(f32[2,4,8]{2,1,0:T(4,128)} %param.33) | copy-start | bytes 772
  1293.3 2522.7 %copy-start.54 = (f32[2,8,512]{2,1,0:T(8,128)S(1)}, f32[2,8,512]{2,1,0:T(8,128)}, u32[]{:S(2)}) copy-start(f32[2,8,512]{2,1,0:T(8,128)} %param.32) | copy-start | bytes 98308
  1293.4 2527.2 %copy-start.53 = (f32[2,24,512]{2,1,0:T(8,128)S(1)}, f32[2,24,512]{2,1,0:T(8,128)}, u32[]{:S(2)}) copy-start(f32[2,24,512]{2,1,0:T(8,128)} %param.29) | copy-start | bytes 294916
  1293.4 2514.0 %all-reduce.6.cloned.1.call-start = ((), (), s32[]{:S(2)}) async-start(), calls=%async_computation.24 | async-start | bytes 466944 | tf_op jit(solution)/shard_map/psum | solution.py:118
  (50 other events, 145.4 us)
Sparse Core Ops, SparseCore 0:
  11.5 65.4 all-gather.16
  80.3 61.7 all-gather.14
  145.4 61.6 all-gather.20
  210.4 61.5 all-gather.18
  1186.3 6.4 reduce-scatter.12
  1195.0 304.5 reduce-scatter.28
  1501.9 350.4 reduce-scatter.20
  1854.8 352.0 reduce-scatter.24
  2209.2 350.2 reduce-scatter.26
  2561.7 350.2 reduce-scatter.18
  2916.4 267.5 reduce-scatter.16
  3186.2 305.4 reduce-scatter.22
  3496.0 268.1 reduce-scatter.14
  3766.3 11.1 reduce-scatter.30
  3781.2 26.1 all-reduce.5
where the time goes:
time: 3840 us; the launch traced here: 3830 us
  waiting for transfers between devices  2210 us (58%)
  blocking collectives  1340 us (35%)
  other arithmetic  109 us (3%)
  matrix products  84.4 us (2%)
  local copies, waits for them, and re-layouts  64.2 us (2%)
    reduce_scatter x8, waiting for transfers between devices, reduce_grads(): lax.psum_scatter(grad_full, 'dp', scatter_dimension=0, tiled=True)  2170 us
    all_gather x4, blocking collectives, gather_weights(): lax.all_gather(master[layer_idx].astype(jnp.bfloat16), 'dp', axis=0, tile...  582 us
    all_gather x2, blocking collectives, gather_weights(): lax.all_gather(masters[4][layer_idx].astype(jnp.bfloat16), 'dp', axis=1,...  296 us
    unnamed x1, blocking collectives  292 us
    all_gather x2, blocking collectives, train_step(): node_all = lax.all_gather(node_x, 'sp', axis=1, tiled=True)  170 us
    dot_general x36, matrix products, contract(): lax.dot_general(left_op, right_op, ((left_dims, right_dims), ((), ())), p...  81.5 us
  transfers between devices with their start and end apart: 15, of which 9 were waited for; matrix products, arithmetic and copies ran while one was open for 5% of the time, Pallas kernels for 0%

commit v1 on v0

--- a/solution.py
+++ b/solution.py
@@ -1,6 +1,10 @@
+import functools
+
 import jax
 import jax.numpy as jnp
 from jax import lax
+from jax.experimental import pallas as pl
+from jax.experimental.pallas import tpu as pltpu
 from jax.sharding import PartitionSpec as P
 
 NORM_EPS = 1e-5
@@ -108,16 +112,332 @@
     return tuple(new_master) + tuple(new_one) + tuple(new_two)
 
 
-def gather_weights(masters, layer_idx):
-    mat_list = [lax.all_gather(master[layer_idx].astype(jnp.bfloat16), 'dp', axis=0, tiled=True) for master in masters[:4]]
-    norm_rows = lax.all_gather(masters[4][layer_idx].astype(jnp.bfloat16), 'dp', axis=1, tiled=True).astype(jnp.float32)
-    return mat_list[0], mat_list[1], mat_list[2], mat_list[3], norm_rows
-
-
-def reduce_grads(grads):
-    mat_list = [lax.psum(lax.psum_scatter(grad_full, 'dp', scatter_dimension=0, tiled=True), 'sp') for grad_full in grads[:4]]
-    norm_grad = lax.psum(lax.psum_scatter(grads[4], 'dp', scatter_dimension=1, tiled=True), 'sp')
-    return mat_list[0], mat_list[1], mat_list[2], mat_list[3], norm_grad
+MESH_ID = pl.DeviceIdType.MESH
+ORDERS = ((0, 1, 2), (1, 2, 0), (2, 0, 1))
+RING = 4
+
+
+class Place:
+    def __init__(self):
+        chip = lax.axis_index('dp')
+        self.core = lax.axis_index('sp')
+        self.at = (lax.rem(chip // 16, 4), lax.rem(chip // 4, 4), lax.rem(chip, 4))
+
+    def step(self, dim, delta):
+        return lax.rem(self.at[dim] + (delta + RING), RING)
+
+    def chip(self, dim, delta):
+        pos = list(self.at)
+        pos[dim] = self.step(dim, delta)
+        return {'dp': pos[0] * 16 + pos[1] * 4 + pos[2]}
+
+    def partner(self):
+        return {'sp': 1 - self.core}
+
+    def barrier(self):
+        sem = pltpu.get_barrier_semaphore()
+        for dim in range(3):
+            for delta in (1, -1):
+                pl.semaphore_signal(sem, inc=1, device_id=self.chip(dim, delta), device_id_type=MESH_ID)
+        pl.semaphore_signal(sem, inc=1, device_id=self.partner(), device_id_type=MESH_ID)
+        pl.semaphore_wait(sem, 7)
+
+
+def split_groups(count):
+    base, extra = divmod(count, 3)
+    sizes = [base + (1 if g < extra else 0) for g in range(3)]
+    starts = [sum(sizes[:g]) for g in range(3)]
+    return list(zip(starts, sizes))
+
+
+def gather_kernel(tiles, src_ref, out_ref, send_sem, recv_sem):
+    place = Place()
+    half = tiles // 2
+    first = place.core * half
+    out_ref[place.at[0], place.at[1], place.at[2]] = src_ref[...]
+    place.barrier()
+    pending = []
+    from_partner = []
+    counter = [0]
+
+    def send(src, dst, where):
+        slot = counter[0]
+        counter[0] += 1
+        copy = pltpu.make_async_remote_copy(src_ref=src, dst_ref=dst, send_sem=send_sem.at[slot], recv_sem=recv_sem.at[slot], device_id=where, device_id_type=MESH_ID)
+        copy.start()
+        pending.append(copy)
+        return copy
+
+    groups = split_groups(half)
+
+    def region(g, phase, j, side=None):
+        order = ORDERS[g]
+        start, size = groups[g]
+        index = list(place.at)
+        for q in range(phase):
+            index[order[q]] = pl.ds(0, RING)
+        index[order[phase]] = j
+        lo, n = start, size
+        if side is not None:
+            if phase == 0:
+                cut = (size + 1) // 2
+                lo, n = (start, cut) if side == 0 else (start + cut, size - cut)
+            else:
+                index[order[0]] = pl.ds(2 * side, 2)
+        return out_ref.at[index[0], index[1], index[2], pl.ds(first + lo, n)]
+
+    def share(g, phase, j, side=None):
+        piece = region(g, phase, j, side)
+        from_partner.append(send(piece, piece, place.partner()))
+
+    flight = {}
+    for phase in range(3):
+        for g in range(3):
+            dim = ORDERS[g][phase]
+            piece = region(g, phase, place.at[dim])
+            origin = piece
+            if phase == 0:
+                origin = src_ref.at[pl.ds(first + groups[g][0], groups[g][1])]
+            flight[g] = (send(origin, piece, place.chip(dim, 1)), send(origin, piece, place.chip(dim, -1)))
+        for g in range(3):
+            dim = ORDERS[g][phase]
+            from_left, from_right = flight[g]
+            from_left.wait_recv()
+            piece = region(g, phase, place.step(dim, -1), 0)
+            onward_right = send(piece, piece, place.chip(dim, 1))
+            from_right.wait_recv()
+            piece = region(g, phase, place.step(dim, 1), 1)
+            onward_left = send(piece, piece, place.chip(dim, -1))
+            flight[g] = (onward_right, onward_left)
+            share(g, phase, place.step(dim, -1))
+            share(g, phase, place.step(dim, 1))
+        for g in range(3):
+            dim = ORDERS[g][phase]
+            far = place.step(dim, 2)
+            flight[g][0].wait_recv()
+            flight[g][1].wait_recv()
+            share(g, phase, far)
+    for copy in from_partner:
+        copy.wait_recv()
+    for copy in pending:
+        copy.wait_send()
+
+
+def gather_tiles(shard, collective_id):
+    tiles = shard.shape[0]
+    copies = 3 * 3 * (4 + 3)
+    return pl.pallas_call(
+        functools.partial(gather_kernel, tiles),
+        out_shape=jax.ShapeDtypeStruct((RING, RING, RING) + shard.shape, shard.dtype),
+        in_specs=[pl.BlockSpec(memory_space=pltpu.VMEM)],
+        out_specs=pl.BlockSpec(memory_space=pltpu.VMEM),
+        scratch_shapes=[pltpu.SemaphoreType.DMA((copies,)), pltpu.SemaphoreType.DMA((copies,))],
+        compiler_params=pltpu.CompilerParams(collective_id=collective_id, has_side_effects=True, vmem_limit_bytes=40 * 2 ** 20),
+        name='gather_tiles',
+    )(shard)
+
+
+def reduce_kernel(tiles, src_ref, out_ref, own, theirs, *rest):
+    boxes = rest[:9]
+    load_sem, send_sem, recv_sem = rest[9:]
+    place = Place()
+    half = tiles // 2
+    first = place.core * half
+    other = (1 - place.core) * half
+    groups = split_groups(half)
+    pending = []
+    counter = [0]
+
+    def send(src, dst, where):
+        slot = counter[0]
+        counter[0] += 1
+        copy = pltpu.make_async_remote_copy(src_ref=src, dst_ref=dst, send_sem=send_sem.at[slot], recv_sem=recv_sem.at[slot], device_id=where, device_id_type=MESH_ID)
+        copy.start()
+        pending.append(copy)
+        return copy
+
+    def index_of(g, phase, j, side=None):
+        order = ORDERS[g]
+        start, size = groups[g]
+        index = [pl.ds(0, RING)] * 3
+        for q in range(phase):
+            index[order[q]] = place.at[order[q]]
+        index[order[phase]] = j
+        lo, n = start, size
+        if side is not None:
+            if phase < 2:
+                index[order[phase + 1]] = pl.ds(2 * side, 2)
+            else:
+                cut = (size + 1) // 2
+                lo, n = (start, cut) if side == 0 else (start + cut, size - cut)
+        return index, lo, n
+
+    def in_own(ref, g, phase, j, side=None):
+        index, lo, n = index_of(g, phase, j, side)
+        return ref.at[index[0], index[1], index[2], pl.ds(lo, n)]
+
+    loads = {}
+    for turn, delta in enumerate((2, 1, -1, 0)):
+        for g in range(3):
+            j = place.step(ORDERS[g][0], delta)
+            index, lo, n = index_of(g, 0, j)
+            load = pltpu.make_async_copy(src_ref.at[index[0], index[1], index[2], pl.ds(first + lo, n)], in_own(own, g, 0, j), load_sem.at[turn * 3 + g])
+            load.start()
+            loads[turn, g] = load
+    place.barrier()
+    swaps = {}
+    for turn, delta in enumerate((2, 1, -1, 0)):
+        for g in range(3):
+            j = place.step(ORDERS[g][0], delta)
+            index, lo, n = index_of(g, 0, j)
+            swaps[turn, g] = send(src_ref.at[index[0], index[1], index[2], pl.ds(other + lo, n)], in_own(theirs, g, 0, j), place.partner())
+
+    def add_into(target, addend):
+        target[...] = target[...] + addend[...]
+
+    def ready(turn, g):
+        delta = (2, 1, -1, 0)[turn]
+        loads[turn, g].wait()
+        swaps[turn, g].wait_recv()
+        j = place.step(ORDERS[g][0], delta)
+        add_into(in_own(own, g, 0, j), in_own(theirs, g, 0, j))
+
+    def box(g, phase, slot, side):
+        ref = boxes[g * 3 + phase]
+        if phase < 2:
+            return ref.at[slot]
+        size = groups[g][1]
+        cut = (size + 1) // 2
+        return ref.at[slot, pl.ds(0, cut if side == 0 else size - cut)]
+
+    for phase in range(3):
+        flight = {}
+        dims = [ORDERS[g][phase] for g in range(3)]
+
+        def start(g, name, j_delta, side, slot, toward):
+            j = place.step(dims[g], j_delta)
+            flight[g, name] = send(in_own(own, g, phase, j, side), box(g, phase, slot, side), place.chip(dims[g], toward))
+
+        for g in range(3):
+            if phase == 0:
+                ready(0, g)
+            start(g, 'far_right', 2, 0, 0, 1)
+            start(g, 'far_left', 2, 1, 2, -1)
+        for g in range(3):
+            if phase == 0:
+                ready(1, g)
+            start(g, 'near_right', 1, 1, 1, 1)
+            if phase == 0:
+                ready(2, g)
+            start(g, 'near_left', -1, 0, 3, -1)
+        for g in range(3):
+            flight[g, 'far_right'].wait_recv()
+            add_into(in_own(own, g, phase, place.step(dims[g], 1), 0), box(g, phase, 0, 0))
+            start(g, 'sum_right', 1, 0, 4, 1)
+            flight[g, 'far_left'].wait_recv()
+            add_into(in_own(own, g, phase, place.step(dims[g], -1), 1), box(g, phase, 2, 1))
+            start(g, 'sum_left', -1, 1, 5, -1)
+        if phase == 0:
+            for g in range(3):
+                ready(3, g)
+        for g in range(3):
+            here = place.at[dims[g]]
+            for name, slot, side in (('near_left', 3, 0), ('near_right', 1, 1)):
+                flight[g, name].wait_recv()
+                add_into(in_own(own, g, phase, here, side), box(g, phase, slot, side))
+            for name, slot, side in (('sum_right', 4, 0), ('sum_left', 5, 1)):
+                flight[g, name].wait_recv()
+                add_into(in_own(own, g, phase, here, side), box(g, phase, slot, side))
+    out_ref[pl.ds(first, half)] = own[place.at[0], place.at[1], place.at[2]]
+    piece = out_ref.at[pl.ds(first, half)]
+    send(piece, piece, place.partner()).wait_recv()
+    for copy in pending:
+        copy.wait_send()
+
+
+def reduce_tiles(partials, collective_id):
+    tiles = partials.shape[3]
+    half = tiles // 2
+    groups = split_groups(half)
+    box_shapes = []
+    for g in range(3):
+        order = ORDERS[g]
+        size = groups[g][1]
+        dims = {dim: RING for dim in range(3) if dim != order[0]}
+        dims[order[1]] = 2
+        box_shapes.append((6,) + tuple(dims[dim] for dim in sorted(dims)) + (size, 8, 128))
+        box_shapes.append((6, 2, size, 8, 128))
+        box_shapes.append((6, (size + 1) // 2, 8, 128))
+    copies = 12 + 3 * 3 * 6 + 1
+    return pl.pallas_call(
+        functools.partial(reduce_kernel, tiles),
+        out_shape=jax.ShapeDtypeStruct((tiles, 8, 128), jnp.float32),
+        in_specs=[pl.BlockSpec(memory_space=pl.ANY)],
+        out_specs=pl.BlockSpec(memory_space=pltpu.VMEM),
+        scratch_shapes=[pltpu.VMEM((RING, RING, RING, half, 8, 128), jnp.float32)] * 2 + [pltpu.VMEM(shape, jnp.float32) for shape in box_shapes] + [pltpu.SemaphoreType.DMA((12,)), pltpu.SemaphoreType.DMA((copies,)), pltpu.SemaphoreType.DMA((copies,))],
+        compiler_params=pltpu.CompilerParams(collective_id=collective_id, has_side_effects=True, vmem_limit_bytes=56 * 2 ** 20),
+        name='reduce_tiles',
+    )(partials)
+
+
+SHARD_ROWS = (24, 8, 16, 8)
+
+
+def rows_to_tiles(values, sub):
+    lead = values.shape[:-2]
+    rows = values.shape[-2]
+    cut = values.reshape(lead + (rows // sub, sub, 4, 128))
+    n = len(lead)
+    return jnp.moveaxis(cut, n + 2, n + 1).reshape(lead + (rows // sub * 4, sub, 128))
+
+
+def tiles_to_rows(tiles):
+    lead = tiles.shape[:-3]
+    count, sub = tiles.shape[-3:-1]
+    n = len(lead)
+    cut = tiles.reshape(lead + (count // 4, 4, sub, 128))
+    return jnp.moveaxis(cut, n + 1, n + 2).reshape(lead + (count // 4 * sub, 512))
+
+
+def gather_weights(masters):
+    rows = jnp.concatenate([masters[slot][layer] for layer in range(2) for slot in range(4)], axis=0).astype(jnp.bfloat16)
+    norms = jnp.pad(masters[4].astype(jnp.bfloat16).reshape(1, 64), ((0, 15), (0, 64)))[None]
+    shard = jnp.concatenate([rows_to_tiles(rows, 16), norms, jnp.zeros_like(norms)], axis=0)
+    full = gather_tiles(shard, 1).reshape(64, 30, 16, 128)
+    rows = tiles_to_rows(full[:, :28])
+    norms = full[:, 28, 0, :64].reshape(64, 2, 4, 8).transpose(1, 2, 0, 3).reshape(2, 4, 512).astype(jnp.float32)
+    layers = []
+    first = 0
+    for layer in range(2):
+        mats = []
+        for size in SHARD_ROWS:
+            mats.append(rows[:, first:first + size].reshape(64 * size, 512))
+            first += size
+        layers.append(tuple(mats) + (norms[layer],))
+    return layers
+
+
+def reduce_grads(layer_grads):
+    parts = []
+    for grads in layer_grads:
+        for slot, size in enumerate(SHARD_ROWS):
+            parts.append(rows_to_tiles(grads[slot].reshape(64, size, 512), 8))
+    norms = jnp.stack([grads[4] for grads in layer_grads]).reshape(8, 64, 8).transpose(1, 0, 2).reshape(64, 1, 64)
+    norms = jnp.pad(norms, ((0, 0), (0, 7), (0, 64)))[:, None]
+    parts += [norms, jnp.zeros_like(norms)]
+    partials = jnp.concatenate(parts, axis=1).reshape(4, 4, 4, 58, 8, 128)
+    total = reduce_tiles(partials, 2)
+    rows = tiles_to_rows(total[:56])
+    norms = total[56, 0, :64].reshape(2, 4, 8)
+    out = []
+    first = 0
+    for layer in range(2):
+        mats = []
+        for size in SHARD_ROWS:
+            mats.append(rows[first:first + size])
+            first += size
+        out.append(tuple(mats) + (norms[layer],))
+    return out
 
 
 def solution(mesh):
@@ -141,8 +461,9 @@
         node_x = node_lat
         edge_x = edge_lat.reshape(batch_size, tile_nodes, degree, lat_width)
         records = []
+        weights = gather_weights(masters)
         for layer_idx in range(layers):
-            layer_wts = gather_weights(masters, layer_idx)
+            layer_wts = weights[layer_idx]
             node_all = lax.all_gather(node_x, 'sp', axis=1, tiled=True)
             node_new, edge_new, saved = layer_forward(node_x, node_all, edge_x, senders, mask_b, layer_wts)
             records.append((node_x, edge_x, saved))
@@ -152,13 +473,13 @@
         d_edge = edge_cot.reshape(batch_size, tile_nodes, degree, lat_width)
         grads_rev = []
         for layer_idx in reversed(range(layers)):
-            layer_wts = gather_weights(masters, layer_idx)
+            layer_wts = weights[layer_idx]
             node_in, edge_in, saved = records[layer_idx]
             d_local, scattered, d_edge, grads = layer_backward(d_node, d_edge, node_in, edge_in, senders, mask_f, saved, layer_wts, total_nodes)
             returned = lax.psum_scatter(scattered, 'sp', scatter_dimension=1, tiled=True)
             d_node = (d_local + returned).astype(jnp.bfloat16)
-            grads_rev.append(reduce_grads(grads))
-        new_state = update_all(masters, moments_one, moments_two, grads_rev[::-1])
+            grads_rev.append(grads)
+        new_state = update_all(masters, moments_one, moments_two, reduce_grads(grads_rev[::-1]))
         return new_state + (d_node, d_edge.reshape(edge_lat.shape))
 
     return jax.shard_map(train_step, mesh=mesh, in_specs=(lat_spec, lat_spec, edge_spec, edge_spec, lat_spec, lat_spec) + param_specs + param_specs + param_specs, out_specs=param_specs + param_specs + param_specs + (lat_spec, lat_spec), check_vma=False)

time: 3840 us -> 422 us (0.11)
  waiting for transfers between devices: 2210 us -> 0.04 us
  blocking collectives: 1340 us -> 4.74 us
  Pallas kernels: 0 us -> 87.4 us
  local copies, waits for them, and re-layouts: 64.2 us -> 119 us
    reduce_scatter x8 -> x0, waiting for transfers between devices: 2170 us -> none  [reduce_grads(): lax.psum_scatter(grad_full, 'dp', scatter_dimension=0, tiled=True)]
    all_gather x6 -> x0, blocking collectives: 878 us -> none  [the longest x4 582 us: gather_weights(): lax.all_gather(master[layer_idx].astype(jnp.bfloat16), 'dp', axis=0, tile...]
    unnamed x1 -> x0, blocking collectives: 292 us -> none
    all_gather x2, blocking collectives: 170 us -> 4.74 us  [train_step(): node_all = lax.all_gather(node_x, 'sp', axis=1, tiled=True)]
    pallas_call x0 -> x2, Pallas kernels: none -> 87.4 us  [the longest x1 47.9 us: reduce_tiles(): pl.pallas_call(functools.partial(reduce_kernel, tiles), out_shape=jax.Sha...]
  transfers between devices with their start and end apart: 15 -> 2, of which waited for: 9 -> 0; matrix products, arithmetic and copies ran while one was open for 5% -> 17% of each run, Pallas kernels for 0% -> 12%
where the time goes in v1:
time: 422 us; the launch traced here: 414 us
  local copies, waits for them, and re-layouts  119 us (28%)
  other arithmetic  97.7 us (23%)
  matrix products  88.6 us (21%)
  Pallas kernels  87.4 us (21%)
  between operations  16.1 us (4%)
  blocking collectives  4.74 us (1%)
    dot_general x36, matrix products, contract(): lax.dot_general(left_op, right_op, ((left_dims, right_dims), ((), ())), p...  85.6 us
    pallas_call x1, Pallas kernels, reduce_tiles(): pl.pallas_call(functools.partial(reduce_kernel, tiles), out_shape=jax.Sha...  47.9 us
    pallas_call x1, Pallas kernels, gather_tiles(): pl.pallas_call(functools.partial(gather_kernel, tiles), out_shape=jax.Sha...  39.4 us
    scatter-add x2, other arithmetic, layer_backward(): jnp.zeros((batch_size, total_nodes, lat_width), jnp.float32).at[:, senders]  35.2 us
    unnamed x240, local copies, waits for them, and re-layouts  26.4 us
    dot_general x7, local copies, waits for them, and re-layouts, contract(): lax.dot_general(left_op, right_op, ((left_dims, right_dims), ((), ())), p...  18.2 us
    gather x2, local copies, waits for them, and re-layouts, layer_forward(): sender_lat = jnp.take(node_all, senders, axis=1).reshape(edge_x.shape)  16.7 us
    reduce_sum x4, other arithmetic, mlp_back(): d_gain = jnp.sum(d_branch * normed, axis=lead_dims)  15.4 us
  transfers between devices with their start and end apart: 2, of which 0 were waited for; matrix products, arithmetic and copies ran while one was open for 17% of the time, Pallas kernels for 12%

profile of v1, /device:TPU:1, one launch (start us, length us, event | category | flops | bytes accessed | tf_op | source)
XLA Modules:
  0.0 413.8 jit_solution(16671520377765475975)
XLA Ops:
  15.1 39.4 %gather_tiles.1 = bf16[4,4,4,30,16,128]{5,4,3,2,1,0:T(8,128)(2,1)S(1)} custom-call(bf16[30,16,128]{2,1,0:T(8,128)(2,1)S(1)} %maximum_maximum_fusion.src_ref), custom_call_target="tpu_custom_call" | custom-call | tf_op jit(solution)/shard_map/gather_tiles/pallas_call | solution.py:229
  54.6 5.5 %slice.304 = bf16[64,28,16,128]{3,2,1,0:T(8,128)(2,1)} slice(bf16[64,30,16,128]{3,2,1,0:T(8,128)(2,1)S(1)} %bitcast.493), slice={[0:64], [0:28], [0:16], [0:128]} | slice | bytes 14680064 | tf_op jit(solution)/shard_map/slice | solution.py:407
  60.1 9.8 %copy.236 = bf16[64,7,16,4,128]{4,3,2,1,0:T(4,128)(2,1)} copy(bf16[64,7,16,4,128]{4,2,3,1,0:T(8,128)(2,1)} %bitcast.496) | data formatting | bytes 14680064 | tf_op jit(solution)/shard_map/transpose | solution.py:399
  69.8 11.6 %reshape.767 = bf16[64,112,512]{2,1,0:T(8,128)(2,1)} reshape(bf16[64,7,16,4,128]{4,3,2,1,0:T(4,128)(2,1)} %copy.236) | data formatting | bytes 14680064 | tf_op jit(solution)/shard_map/reshape | solution.py:399
  81.5 2.9 fusion.225
  84.3 3.0 fusion.224
  87.4 4.0 fusion.226
  91.4 2.3 all_gather.6
  95.5 2.4 fusion.160
  97.9 4.4 %fusion.109 = f32[512,256,8]{1,0,2:T(8,128)} fusion(bf16[256,8,512]{2,1,0:T(8,128)(2,1)S(1)} %bitcast.497, bf16[1536,512]{1,0:T(8,128)(2,1)} %bitcast.505), kind=kOutput, calls=%fused_computation.153 | convolution fusion | flops 1073741824 | bytes 6815744 | tf_op jit(solution)/shard_map/dot_general | solution.py:20
  102.3 7.5 %gather_fusion = bf16[2048,512]{1,0:T(8,128)(2,1)S(1)} fusion(bf16[512,512]{1,0:T(8,128)(2,1)S(1)} %bitcast.494, s32[2048]{0:T(1024)S(1)} %get-tuple-element.86), kind=kCustom, calls=%fused_computation.clone | custom fusion | bytes 4202496 | tf_op jit(solution)/shard_map/jit(_take)/gather | solution.py:60
  110.3 2.5 copy-done.3
  112.8 4.9 %fusion.67 = (bf16[256,8,512]{0,2,1:T(8,128)(2,1)S(1)}, f32[256,8,512]{0,2,1:T(8,128)}) fusion(f32[512,256,8]{1,0,2:T(8,128)S(1)} %copy-done.3, f32[256,512]{0,1:T(8,128)} %bitcast.523, bf16[1536,512]{1,0:T(8,128)(2,1)} %bitcast.506, bf16[256,8,512]{2,1,0:T(8,128)(2,1)S(1)} %fusion.87), kind=kOutput, calls=%fused_computation.105 | convolution fusion | flops 1076887552 | bytes 13631488 | tf_op jit(solution)/shard_map/dot_general | solution.py:20
  117.7 3.4 convert_reduce_fusion.3
  128.2 2.4 all_gather.7
  131.8 3.3 fusion.159
  136.2 2.1 copy.250
  138.3 9.2 %gather_fusion.1 = bf16[2048,512]{1,0:T(8,128)(2,1)} fusion(bf16[512,512]{1,0:T(8,128)(2,1)S(1)} %bitcast.495, s32[2048]{0:T(1024)S(1)} %get-tuple-element.86), kind=kCustom, calls=%fused_computation.1.clone | custom fusion | bytes 4202496 | tf_op jit(solution)/shard_map/jit(_take)/gather | solution.py:60
  150.3 2.9 convolution_add_fusion
  153.3 3.4 convert_reduce_fusion.2
  167.9 4.3 %convert_bitcast_fusion.1 = (f32[1,256,8,512]{3,2,1,0:T(8,128)}, f32[256,8,512]{2,1,0:T(8,128)}) fusion(bf16[1,2048,512]{2,1,0:T(8,128)(2,1)S(1)} %copy-done.15), kind=kLoop, calls=%fused_computation.12 | loop fusion | flops 1048576 | bytes 10485760 | tf_op jit(solution)/shard_map/convert_element_type | solution.py:81
  176.1 6.4 %fusion.30 = (f32[512]{0:T(512)S(1)}, f32[256,8]{0,1:T(8,128)S(1)}, bf16[256,8,512]{2,0,1:T(8,128)(2,1)S(1)}) fusion(bf16[256,8,512]{2,0,1:T(8,128)(2,1)} %copy-done, f32[256,8]{0,1:T(8,128)} %copy-done.83, f32[256,8]{0,1:T(8,128)} %copy-done.79, f32[512]{0:T(512)} %bitcast.542, f32[256,8]{0,1:T(8,128)} %copy.255, f32[256,512]{1,0:T(8,128)S(1)} %fusion.173, ...), kind=kLoop, calls=%fused_computation.61 | loop fusion | flops 12580352 | bytes 8949760 | tf_op jit(solution)/shard_map/reduce_sum | solution.py:44
  182.7 4.8 %fusion.54 = bf16[256,8,512]{0,2,1:T(8,128)(2,1)S(1)} fusion(f32[256,8,512]{0,2,1:T(8,128)S(1)} %copy-done.32, f32[256,512]{0,1:T(8,128)S(1)} %copy-done.69, bf16[64,112,512]{2,1,0:T(8,128)(2,1)} %reshape.767, bf16[256,8,512]{2,0,1:T(8,128)(2,1)S(1)} %get-tuple-element.53, bf16[256,8,512]{2,0,1:T(8,128)(2,1)S(1)} %copy-done.1, ...), kind=kOutput, calls=%fused_computation.85 | convolution fusion | flops 1098907648 | bytes 11569152 | tf_op jit(solution)/shard_map/dot_general | solution.py:20
  187.6 3.5 convolution_bitcast_fusion.1
  191.1 4.8 %slice_reduce_fusion.1 = (f32[256,512]{1,0:T(8,128)}, f32[1,256,8,512]{3,1,2,0:T(8,128)}) fusion(f32[1,256,8,1536]{3,1,2,0:T(8,128)S(1)} %convolution_bitcast_fusion.1), kind=kLoop, calls=%fused_computation.90 | loop fusion | flops 917504 | bytes 13107200 | tf_op jit(solution)/shard_map/reduce_sum | solution.py:88
  197.1 17.5 %scatter_custom_fusion = f32[512,512]{1,0:T(8,128)} fusion(s32[2048]{0:T(1024)} %get-tuple-element.85, f32[1,256,8,512]{3,1,2,0:T(8,128)} %get-tuple-element.58, f32[]{:T(128)} %constant.39.clone.1), kind=kCustom, calls=%fused_computation.100 | custom fusion | flops 1048576 | bytes 5243392 | tf_op jit(solution)/shard_map/scatter-add | solution.py:87
  214.6 2.7 fusion.201
  217.3 2.3 fusion.184
  219.7 4.6 %fusion.213 = bf16[512,256,8]{0,1,2:T(8,128)(2,1)} fusion(f32[256,8]{0,1:T(8,128)S(1)} %broadcast_multiply_fusion.3, f32[256,8]{0,1:T(8,128)S(1)} %copy-done.80, bf16[256,8,512]{2,0,1:T(8,128)(2,1)S(1)} %copy-done.2, f32[256,8]{0,1:T(8,128)S(1)} %copy-done.94, f32[512]{0:T(512)S(1)} %bitcast.544, bf16[256,8,512]{2,0,1:T(8,128)(2,1)} %copy-done.21, ...), kind=kLoop, calls=%fused_computation.382 | loop fusion | flops 10485760 | bytes 6326272 | tf_op jit(solution)/shard_map/dot_general | solution.py:20
  224.2 4.5 %copy.277 = bf16[256,8,512]{2,1,0:T(8,128)(2,1)} copy(bf16[256,8,512]{0,2,1:T(8,128)(2,1)} %copy-done.48) | data formatting | bytes 4194304 | tf_op jit(solution)/shard_map/convert_element_type | solution.py:52
  232.6 2.5 fusion.176
  235.1 4.0 dot_general.222
  239.0 4.2 %copy.281 = bf16[4,128,256,8]{2,1,3,0:T(8,128)(2,1)} copy(bf16[4,128,256,8]{1,0,2,3:T(4,128)(2,1)} %dot_general.222) | data formatting | bytes 4194304 | tf_op jit(solution)/shard_map/dot_general | solution.py:20
  243.3 3.7 convolution_bitcast_fusion.6
  256.1 2.3 fusion.78
  266.4 6.3 %fusion.56 = (f32[512]{0:T(512)S(1)}, f32[256,8]{0,1:T(8,128)S(1)}, f32[256,8]{0,1:T(8,128)S(1)}, f32[512]{0:T(512)S(1)}, bf16[1,256,8,512]{3,1,2,0:T(8,128)(2,1)S(1)}) fusion(bf16[256,8,512]{2,0,1:T(8,128)(2,1)S(1)} %get-tuple-element.90, f32[256,8]{0,1:T(8,128)S(1)} %add_rsqrt_fusion.1, f32[256,8]{0,1:T(8,128)S(1)} %broadcast_multiply_fusion.5, ...), kind=kLoop, calls=%fused_computation.87 | loop fusion | flops 22014976 | bytes 13678592 | tf_op jit(solution)/shard_map/reduce_sum | solution.py:44
  272.7 5.8 %fusion.47 = bf16[256,8,512]{0,2,1:T(8,128)(2,1)S(1)} fusion(bf16[256,8,512]{0,2,1:T(8,128)(2,1)S(1)} %copy-done.57, bf16[64,112,512]{2,1,0:T(8,128)(2,1)} %reshape.767, bf16[256,8,512]{2,0,1:T(8,128)(2,1)S(1)} %get-tuple-element.90, bf16[1,256,8,512]{3,1,2,0:T(8,128)(2,1)S(1)} %get-tuple-element.51, f32[256,8]{0,1:T(8,128)S(1)} %broadcast_multiply_fusion.1, ...), kind=kOutput, calls=%fused_computation.78 | convolution fusion | flops 1096810496 | bytes 8955904 | tf_op jit(solution)/shard_map/dot_general | solution.py:20
  278.6 2.2 convolution_reduce_fusion.1
  281.3 3.2 fusion.111
  284.5 4.6 %copy.268 = bf16[256,8,512]{2,1,0:T(8,128)(2,1)} copy(bf16[256,8,512]{0,2,1:T(8,128)(2,1)} %copy-done.50) | data formatting | bytes 4194304 | tf_op jit(solution)/shard_map/convert_element_type | solution.py:52
  291.9 4.7 %convolution_bitcast_fusion.7 = f32[512,512]{1,0:T(8,128)} fusion(bf16[256,8,512]{2,1,0:T(8,128)(2,1)} %copy-done.22, bf16[256,8,512]{2,1,0:T(8,128)(2,1)} %copy.268), kind=kOutput, calls=%fused_computation.161 | convolution fusion | flops 1073741824 | bytes 5242880 | tf_op jit(solution)/shard_map/dot_general | solution.py:20
  296.6 3.5 convolution_bitcast_fusion
  300.1 5.5 %fusion.57 = (bf16[1,256,8,512]{3,1,2,0:T(8,128)(2,1)}, f32[1,256,8,512]{3,1,2,0:T(8,128)}, f32[256,512]{1,0:T(8,128)}, bf16[512,256,8]{0,1,2:T(8,128)(2,1)}) fusion(bf16[1,256,8,512]{3,1,2,0:T(8,128)(2,1)S(1)} %copy-done.20, f32[1,256,8,1536]{3,1,2,0:T(8,128)S(1)} %convolution_bitcast_fusion, f32[256,8]{0,1:T(8,128)S(1)} %broadcast_multiply_fusion.1, ...), kind=kLoop, calls=%fused_computation.88 | loop fusion | flops 13500416 | bytes 25733120 | tf_op jit(solution)/shard_map/convert_element_type | solution.py:85
  305.6 17.7 %scatter_custom_fusion.1 = f32[512,512]{1,0:T(8,128)} fusion(s32[2048]{0:T(1024)} %get-tuple-element.85, f32[1,256,8,512]{3,1,2,0:T(8,128)} %get-tuple-element.55, f32[]{:T(128)} %constant.39.clone.1), kind=kCustom, calls=%fused_computation.93 | custom fusion | flops 1048576 | bytes 5243392 | tf_op jit(solution)/shard_map/scatter-add | solution.py:87
  323.2 2.3 dot_general.205
  325.6 3.0 copy.272
  348.4 47.9 %reduce_tiles.1 = f32[58,8,128]{2,1,0:T(8,128)} custom-call(f32[4,4,4,58,8,128]{5,4,3,2,1,0:T(8,128)} %broadcast_dynamic-update-slice_fusion.src_ref), custom_call_target="tpu_custom_call" | custom-call | tf_op jit(solution)/shard_map/reduce_tiles/pallas_call | solution.py:372
  398.4 2.5 copy.383
  (350 shorter events, 89.6 us)
Async XLA Ops:
  7.2 251.2 %reduce-scatter.3.cloned.1.call-start = ((), (), s32[]{:S(2)}) async-start(), calls=%async_computation.2 | async-start | bytes 1572864 | tf_op jit(solution)/shard_map/reduce_scatter | solution.py:479
  87.4 10.6 %copy-start.10 = (bf16[1,2048,512]{2,1,0:T(8,128)(2,1)S(1)}, bf16[1,2048,512]{2,1,0:T(8,128)(2,1)}, u32[]{:S(2)}) copy-start(bf16[1,2048,512]{2,1,0:T(8,128)(2,1)} %param.24) | copy-start | bytes 6291460
  94.1 28.0 %copy-start.92 = (f32[1,1,512]{2,1,0:T(1,128)}, f32[1,1,512]{2,1,0:T(1,128)S(1)}, u32[]{:S(2)}) copy-start(f32[1,1,512]{2,1,0:T(1,128)S(1)} %get-tuple-element.84) | copy-start | bytes 6148
  94.1 33.9 %copy-start.99 = (f32[1,1,512]{2,1,0:T(1,128)}, f32[1,1,512]{2,1,0:T(1,128)S(1)}, u32[]{:S(2)}) copy-start(f32[1,1,512]{2,1,0:T(1,128)S(1)} %get-tuple-element.82) | copy-start | bytes 6148
  94.1 78.1 %copy-start.90 = (f32[1,1,512]{2,1,0:T(1,128)}, f32[1,1,512]{2,1,0:T(1,128)S(1)}, u32[]{:S(2)}) copy-start(f32[1,1,512]{2,1,0:T(1,128)S(1)} %get-tuple-element.80) | copy-start | bytes 6148
  95.5 29.5 %copy-start.54 = (f32[512,256]{1,0:T(8,128)}, f32[512,256]{1,0:T(8,128)S(1)}, u32[]{:S(2)}) copy-start(f32[512,256]{1,0:T(8,128)S(1)} %fusion.190) | copy-start | bytes 1572868
  110.3 7.4 %copy-start.22 = (bf16[256,8,512]{2,1,0:T(8,128)(2,1)}, bf16[256,8,512]{2,1,0:T(8,128)(2,1)S(1)}, u32[]{:S(2)}) copy-start(bf16[256,8,512]{2,1,0:T(8,128)(2,1)S(1)} %fusion.87) | copy-start | bytes 6291460
  123.5 8.3 %copy-start.5 = (bf16[256,8,512]{2,0,1:T(8,128)(2,1)}, bf16[256,8,512]{2,0,1:T(8,128)(2,1)S(1)}, u32[]{:S(2)}) copy-start(bf16[256,8,512]{2,0,1:T(8,128)(2,1)S(1)} %fusion.24) | copy-start | bytes 6291460
  125.0 6.8 %copy-start.73 = (bf16[256,1,512]{2,1,0:T(2,128)(2,1)}, bf16[256,1,512]{2,1,0:T(2,128)(2,1)S(1)}, u32[]{:S(2)}) copy-start(bf16[256,1,512]{2,1,0:T(2,128)(2,1)S(1)} %fusion.90) | copy-start | bytes 786436
  125.0 5.6 %copy-start.28 = (bf16[64,24,512]{2,1,0:T(8,128)(2,1)S(1)}, bf16[64,24,512]{2,1,0:T(8,128)(2,1)}, u32[]{:S(2)}) copy-start(bf16[64,24,512]{2,1,0:T(8,128)(2,1)} %get-tuple-element.65) | copy-start | bytes 4718596
  127.8 7.3 %copy-start.101 = (f32[256]{0:T(256)}, f32[256]{0:T(256)S(1)}, u32[]{:S(2)}) copy-start(f32[256]{0:T(256)S(1)} %broadcast_multiply_fusion.11) | copy-start | bytes 3076
  128.0 7.1 %copy-start.103 = (f32[256]{0:T(256)}, f32[256]{0:T(256)S(1)}, u32[]{:S(2)}) copy-start(f32[256]{0:T(256)S(1)} %add_rsqrt_fusion.3) | copy-start | bytes 3076
  128.2 6.9 %copy-start.25 = (bf16[1,256,512]{2,1,0:T(8,128)(2,1)}, bf16[1,256,512]{2,1,0:T(8,128)(2,1)S(1)}, u32[]{:S(2)}) copy-start(bf16[1,256,512]{2,1,0:T(8,128)(2,1)S(1)} %fusion.166) | copy-start | bytes 786436
  160.5 5.0 %copy-start.70 = (bf16[256,1,512]{2,1,0:T(2,128)(2,1)}, bf16[256,1,512]{2,1,0:T(2,128)(2,1)S(1)}, u32[]{:S(2)}) copy-start(bf16[256,1,512]{2,1,0:T(2,128)(2,1)S(1)} %fusion.88) | copy-start | bytes 786436
  160.9 5.4 %copy-start.35 = (bf16[64,16,512]{2,1,0:T(8,128)(2,1)S(1)}, bf16[64,16,512]{2,1,0:T(8,128)(2,1)}, u32[]{:S(2)}) copy-start(bf16[64,16,512]{2,1,0:T(8,128)(2,1)} %get-tuple-element.60) | copy-start | bytes 3145732
  176.1 6.5 %copy-start.1 = (bf16[256,8,512]{2,0,1:T(8,128)(2,1)S(1)}, bf16[256,8,512]{2,0,1:T(8,128)(2,1)}, u32[]{:S(2)}) copy-start(bf16[256,8,512]{2,0,1:T(8,128)(2,1)} %copy-done) | copy-start | bytes 6291460
  176.1 6.5 %copy-start.32 = (f32[256,8,512]{0,2,1:T(8,128)S(1)}, f32[256,8,512]{0,2,1:T(8,128)}, u32[]{:S(2)}) copy-start(f32[256,8,512]{0,2,1:T(8,128)} %copy-done.31) | copy-start | bytes 12582916
  176.1 6.5 %copy-start.69 = (f32[256,512]{0,1:T(8,128)S(1)}, f32[256,512]{0,1:T(8,128)}, u32[]{:S(2)}) copy-start(f32[256,512]{0,1:T(8,128)} %copy.250) | copy-start | bytes 1572868
  176.1 6.5 %copy-start.80 = (f32[256,8]{0,1:T(8,128)S(1)}, f32[256,8]{0,1:T(8,128)}, u32[]{:S(2)}) copy-start(f32[256,8]{0,1:T(8,128)} %copy-done.79) | copy-start | bytes 24580
  176.1 6.6 %copy-start.84 = (f32[256,8]{0,1:T(8,128)S(1)}, f32[256,8]{0,1:T(8,128)}, u32[]{:S(2)}) copy-start(f32[256,8]{0,1:T(8,128)} %copy-done.83) | copy-start | bytes 24580
  176.1 6.6 %copy-start.91 = (f32[1,1,512]{2,1,0:T(1,128)S(1)}, f32[1,1,512]{2,1,0:T(1,128)}, u32[]{:S(2)}) copy-start(f32[1,1,512]{2,1,0:T(1,128)} %copy-done.90) | copy-start | bytes 6148
  176.1 6.5 %copy-start.94 = (f32[256,8]{0,1:T(8,128)S(1)}, f32[256,8]{0,1:T(8,128)}, u32[]{:S(2)}) copy-start(f32[256,8]{0,1:T(8,128)} %copy.260) | copy-start | bytes 24580
  191.1 6.0 %copy-start.14 = (f32[1,256,8,1536]{3,1,2,0:T(8,128)}, f32[1,256,8,1536]{3,1,2,0:T(8,128)S(1)}, u32[]{:S(2)}) copy-start(f32[1,256,8,1536]{3,1,2,0:T(8,128)S(1)} %convolution_bitcast_fusion.1) | copy-start | bytes 37748740
  214.6 190.0 %reduce-scatter.5.cloned.1.call-start = ((), (), s32[]{:S(2)}) async-start(), calls=%async_computation.3 | async-start | bytes 1572864 | tf_op jit(solution)/shard_map/reduce_scatter | solution.py:479
  260.2 5.2 %copy-start.44 = (bf16[1,256,512]{2,1,0:T(8,128)(2,1)}, bf16[1,256,512]{2,1,0:T(8,128)(2,1)S(1)}, u32[]{:S(2)}) copy-start(bf16[1,256,512]{2,1,0:T(8,128)(2,1)S(1)} %get-tuple-element.52) | copy-start | bytes 786436
  260.5 5.9 %copy-start.8 = (f32[1,256,8,512]{3,2,1,0:T(8,128)S(1)}, f32[1,256,8,512]{3,2,1,0:T(8,128)}, u32[]{:S(2)}) copy-start(f32[1,256,8,512]{3,2,1,0:T(8,128)} %get-tuple-element.68) | copy-start | bytes 12582916
  260.5 5.9 %copy-start.87 = (f32[256,8]{0,1:T(8,128)S(1)}, f32[256,8]{0,1:T(8,128)}, u32[]{:S(2)}) copy-start(f32[256,8]{0,1:T(8,128)} %copy.255) | copy-start | bytes 24580
  260.5 5.8 %copy-start.93 = (f32[1,1,512]{2,1,0:T(1,128)S(1)}, f32[1,1,512]{2,1,0:T(1,128)}, u32[]{:S(2)}) copy-start(f32[1,1,512]{2,1,0:T(1,128)} %copy-done.92) | copy-start | bytes 6148
  266.4 6.3 %copy-start.57 = (bf16[256,8,512]{0,2,1:T(8,128)(2,1)S(1)}, bf16[256,8,512]{0,2,1:T(8,128)(2,1)}, u32[]{:S(2)}) copy-start(bf16[256,8,512]{0,2,1:T(8,128)(2,1)} %copy-done.56) | copy-start | bytes 6291460
  272.7 5.9 %copy-start.19 = (bf16[1,256,8,512]{3,1,2,0:T(8,128)(2,1)}, bf16[1,256,8,512]{3,1,2,0:T(8,128)(2,1)S(1)}, u32[]{:S(2)}) copy-start(bf16[1,256,8,512]{3,1,2,0:T(8,128)(2,1)S(1)} %get-tuple-element.51) | copy-start | bytes 6291460
  281.3 7.8 %copy-start.64 = (bf16[1,256,512]{2,1,0:T(8,128)(2,1)S(1)}, bf16[1,256,512]{2,1,0:T(8,128)(2,1)}, u32[]{:S(2)}) copy-start(bf16[1,256,512]{2,1,0:T(8,128)(2,1)} %copy-done.63) | copy-start | bytes 786436
  305.6 17.7 %copy-start.17 = (bf16[512,256,8]{0,1,2:T(8,128)(2,1)S(1)}, bf16[512,256,8]{0,1,2:T(8,128)(2,1)}, u32[]{:S(2)}) copy-start(bf16[512,256,8]{0,1,2:T(8,128)(2,1)} %get-tuple-element.67) | copy-start | bytes 6291460
  348.4 50.0 %copy-start.16 = (bf16[1,256,8,512]{3,1,2,0:T(8,128)(2,1)S(1)}, bf16[1,256,8,512]{3,1,2,0:T(8,128)(2,1)}, u32[]{:S(2)}) copy-start(bf16[1,256,8,512]{3,1,2,0:T(8,128)(2,1)} %get-tuple-element.54) | copy-start | bytes 6291460
  396.4 5.4 %copy-start.81 = (f32[2,8,512]{2,1,0:T(8,128)S(1)}, f32[2,8,512]{2,1,0:T(8,128)}, u32[]{:S(2)}) copy-start(f32[2,8,512]{2,1,0:T(8,128)} %param.32) | copy-start | bytes 98308
  396.4 5.4 %copy-start.95 = (f32[2,8,512]{2,1,0:T(8,128)S(1)}, f32[2,8,512]{2,1,0:T(8,128)}, u32[]{:S(2)}) copy-start(f32[2,8,512]{2,1,0:T(8,128)} %param.37) | copy-start | bytes 98308
  396.4 5.4 %copy-start.96 = (f32[2,8,512]{2,1,0:T(8,128)S(1)}, f32[2,8,512]{2,1,0:T(8,128)}, u32[]{:S(2)}) copy-start(f32[2,8,512]{2,1,0:T(8,128)} %param.42) | copy-start | bytes 98308
  396.4 6.0 %copy-start.82 = (f32[2,8,512]{2,1,0:T(8,128)S(1)}, f32[2,8,512]{2,1,0:T(8,128)}, u32[]{:S(2)}) copy-start(f32[2,8,512]{2,1,0:T(8,128)} %param.30) | copy-start | bytes 98308
  396.4 6.0 %copy-start.97 = (f32[2,8,512]{2,1,0:T(8,128)S(1)}, f32[2,8,512]{2,1,0:T(8,128)}, u32[]{:S(2)}) copy-start(f32[2,8,512]{2,1,0:T(8,128)} %param.35) | copy-start | bytes 98308
  396.4 6.0 %copy-start.98 = (f32[2,8,512]{2,1,0:T(8,128)S(1)}, f32[2,8,512]{2,1,0:T(8,128)}, u32[]{:S(2)}) copy-start(f32[2,8,512]{2,1,0:T(8,128)} %param.40) | copy-start | bytes 98308
  396.4 6.7 %copy-start.76 = (f32[2,16,512]{2,1,0:T(8,128)S(1)}, f32[2,16,512]{2,1,0:T(8,128)}, u32[]{:S(2)}) copy-start(f32[2,16,512]{2,1,0:T(8,128)} %param.31) | copy-start | bytes 196612
  396.4 6.7 %copy-start.88 = (f32[2,16,512]{2,1,0:T(8,128)S(1)}, f32[2,16,512]{2,1,0:T(8,128)}, u32[]{:S(2)}) copy-start(f32[2,16,512]{2,1,0:T(8,128)} %param.36) | copy-start | bytes 196612
  396.5 6.6 %copy-start.89 = (f32[2,16,512]{2,1,0:T(8,128)S(1)}, f32[2,16,512]{2,1,0:T(8,128)}, u32[]{:S(2)}) copy-start(f32[2,16,512]{2,1,0:T(8,128)} %param.41) | copy-start | bytes 196612
  396.5 7.3 %copy-start.75 = (f32[2,24,512]{2,1,0:T(8,128)S(1)}, f32[2,24,512]{2,1,0:T(8,128)}, u32[]{:S(2)}) copy-start(f32[2,24,512]{2,1,0:T(8,128)} %param.29) | copy-start | bytes 294916
  396.5 7.3 %copy-start.85 = (f32[2,24,512]{2,1,0:T(8,128)S(1)}, f32[2,24,512]{2,1,0:T(8,128)}, u32[]{:S(2)}) copy-start(f32[2,24,512]{2,1,0:T(8,128)} %param.34) | copy-start | bytes 294916
  396.5 7.3 %copy-start.86 = (f32[2,24,512]{2,1,0:T(8,128)S(1)}, f32[2,24,512]{2,1,0:T(8,128)}, u32[]{:S(2)}) copy-start(f32[2,24,512]{2,1,0:T(8,128)} %param.39) | copy-start | bytes 294916
  396.5 8.1 %copy-start.41 = (f32[1,256,1024]{2,1,0:T(8,128)S(1)}, f32[1,256,1024]{2,1,0:T(8,128)}, u32[]{:S(2)}) copy-start(f32[1,256,1024]{2,1,0:T(8,128)} %copy-done.40) | copy-start | bytes 3145732
  396.5 8.1 %copy-start.45 = (bf16[1,256,512]{2,1,0:T(8,128)(2,1)S(1)}, bf16[1,256,512]{2,1,0:T(8,128)(2,1)}, u32[]{:S(2)}) copy-start(bf16[1,256,512]{2,1,0:T(8,128)(2,1)} %copy-done.44) | copy-start | bytes 786436
  396.5 8.0 %copy-start.53 = (f32[256,512]{1,0:T(8,128)S(1)}, f32[256,512]{1,0:T(8,128)}, u32[]{:S(2)}) copy-start(f32[256,512]{1,0:T(8,128)} %get-tuple-element.56) | copy-start | bytes 1572868
  (65 other events, 215.1 us)
Sparse Core Ops, SparseCore 0:
  214.7 8.6 reduce-scatter.2
  323.4 8.6 reduce-scatter.4

commit v2 on v1

v2 whole, which is shorter than its diff:
```python
import functools

import jax
import jax.numpy as jnp
from jax import lax
from jax.experimental import pallas as pl
from jax.experimental.pallas import tpu as pltpu
from jax.sharding import PartitionSpec as P

NORM_EPS = 1e-5
LEARN_RATE = 1e-3
BETA_ONE = 0.9
BETA_TWO = 0.95
ADAM_EPS = 1e-8
DECAY = 0.1
STEP = 10
SHARD_ROWS = (24, 8, 16, 8)

MESH_ID = pl.DeviceIdType.MESH
ORDERS = ((0, 1, 2), (1, 2, 0), (2, 0, 1))
RING = 4


class Place:
    def __init__(self):
        chip = lax.axis_index('dp')
        self.core = lax.axis_index('sp')
        self.at = (lax.rem(chip // 16, 4), lax.rem(chip // 4, 4), lax.rem(chip, 4))

    def step(self, dim, delta):
        return lax.rem(self.at[dim] + (delta + RING), RING)

    def chip(self, dim, delta):
        pos = list(self.at)
        pos[dim] = self.step(dim, delta)
        return {'dp': pos[0] * 16 + pos[1] * 4 + pos[2]}

    def partner(self):
        return {'sp': 1 - self.core}

    def barrier(self):
        sem = pltpu.get_barrier_semaphore()
        for dim in range(3):
            for delta in (1, -1):
                pl.semaphore_signal(sem, inc=1, device_id=self.chip(dim, delta), device_id_type=MESH_ID)
        pl.semaphore_signal(sem, inc=1, device_id=self.partner(), device_id_type=MESH_ID)
        pl.semaphore_wait(sem, 7)


def split_groups(count):
    base, extra = divmod(count, 3)
    sizes = [base + (1 if g < extra else 0) for g in range(3)]
    starts = [sum(sizes[:g]) for g in range(3)]
    return list(zip(starts, sizes))


def gather_kernel(tiles, src_ref, out_ref, send_sem, recv_sem):
    place = Place()
    half = tiles // 2
    first = place.core * half
    out_ref[place.at[0], place.at[1], place.at[2]] = src_ref[...]
    place.barrier()
    pending = []
    from_partner = []
    counter = [0]

    def send(src, dst, where):
        slot = counter[0]
        counter[0] += 1
        copy = pltpu.make_async_remote_copy(src_ref=src, dst_ref=dst, send_sem=send_sem.at[slot], recv_sem=recv_sem.at[slot], device_id=where, device_id_type=MESH_ID)
        copy.start()
        pending.append(copy)
        return copy

    groups = split_groups(half)

    def region(g, phase, j, side=None):
        order = ORDERS[g]
        start, size = groups[g]
        index = list(place.at)
        for q in range(phase):
            index[order[q]] = pl.ds(0, RING)
        index[order[phase]] = j
        lo, n = start, size
        if side is not None:
            if phase == 0:
                cut = (size + 1) // 2
                lo, n = (start, cut) if side == 0 else (start + cut, size - cut)
            else:
                index[order[0]] = pl.ds(2 * side, 2)
        return out_ref.at[index[0], index[1], index[2], pl.ds(first + lo, n)]

    def share(g, phase, j, side=None):
        piece = region(g, phase, j, side)
        from_partner.append(send(piece, piece, place.partner()))

    flight = {}
    for phase in range(3):
        for g in range(3):
            dim = ORDERS[g][phase]
            piece = region(g, phase, place.at[dim])
            origin = piece
            if phase == 0:
                origin = src_ref.at[pl.ds(first + groups[g][0], groups[g][1])]
            flight[g] = (send(origin, piece, place.chip(dim, 1)), send(origin, piece, place.chip(dim, -1)))
        for g in range(3):
            dim = ORDERS[g][phase]
            from_left, from_right = flight[g]
            from_left.wait_recv()
            piece = region(g, phase, place.step(dim, -1), 0)
            onward_right = send(piece, piece, place.chip(dim, 1))
            from_right.wait_recv()
            piece = region(g, phase, place.step(dim, 1), 1)
            onward_left = send(piece, piece, place.chip(dim, -1))
            flight[g] = (onward_right, onward_left)
            share(g, phase, place.step(dim, -1))
            share(g, phase, place.step(dim, 1))
        for g in range(3):
            dim = ORDERS[g][phase]
            far = place.step(dim, 2)
            flight[g][0].wait_recv()
            flight[g][1].wait_recv()
            share(g, phase, far)
    for copy in from_partner:
        copy.wait_recv()
    for copy in pending:
        copy.wait_send()


def gather_tiles(shard, collective_id):
    tiles = shard.shape[0]
    copies = 3 * 3 * (4 + 3)
    return pl.pallas_call(
        functools.partial(gather_kernel, tiles),
        out_shape=jax.ShapeDtypeStruct((RING, RING, RING) + shard.shape, shard.dtype),
        in_specs=[pl.BlockSpec(memory_space=pltpu.VMEM)],
        out_specs=pl.BlockSpec(memory_space=pltpu.VMEM),
        scratch_shapes=[pltpu.SemaphoreType.DMA((copies,)), pltpu.SemaphoreType.DMA((copies,))],
        compiler_params=pltpu.CompilerParams(collective_id=collective_id, has_side_effects=True, vmem_limit_bytes=40 * 2 ** 20),
        name='gather_tiles',
    )(shard)


def reduce_kernel(low_ref, high_ref, norm_ref, out_ref, own, theirs, *rest):
    boxes = rest[:9]
    load_sem, send_sem, recv_sem = rest[9:]
    place = Place()
    half = 29
    groups = split_groups(half)
    pending = []
    loaded = []
    counter = [0]

    def send(src, dst, where):
        slot = counter[0]
        counter[0] += 1
        copy = pltpu.make_async_remote_copy(src_ref=src, dst_ref=dst, send_sem=send_sem.at[slot], recv_sem=recv_sem.at[slot], device_id=where, device_id_type=MESH_ID)
        copy.start()
        pending.append(copy)
        return copy

    def index_of(g, phase, j, side=None):
        order = ORDERS[g]
        start, size = groups[g]
        index = [pl.ds(0, RING)] * 3
        for q in range(phase):
            index[order[q]] = place.at[order[q]]
        index[order[phase]] = j
        lo, n = start, size
        if side is not None:
            if phase < 2:
                index[order[phase + 1]] = pl.ds(2 * side, 2)
            else:
                cut = (size + 1) // 2
                lo, n = (start, cut) if side == 0 else (start + cut, size - cut)
        return index, lo, n

    def in_own(ref, g, phase, j, side=None):
        index, lo, n = index_of(g, phase, j, side)
        return ref.at[index[0], index[1], index[2], pl.ds(lo, n)]

    def sources(g, index, core):
        lo, n = groups[g]
        pieces = []
        for ref, begin in ((low_ref, 0), (high_ref, 14)):
            start, stop = max(lo, begin), min(lo + n, begin + 14)
            if start < stop:
                pieces.append((ref.at[index[0], index[1], index[2], pl.ds(core * 14 + start - begin, stop - start)], start, stop - start))
        if lo + n == 29:
            pieces.append((norm_ref.at[index[0], index[1], index[2], pl.ds(core, 1)], 28, 1))
        return pieces

    loads = {}
    for turn, delta in enumerate((2, 1, -1, 0)):
        for g in range(3):
            j = place.step(ORDERS[g][0], delta)
            index, lo, n = index_of(g, 0, j)
            loads[turn, g] = []
            for ref, start, count in sources(g, index, place.core):
                load = pltpu.make_async_copy(ref, own.at[index[0], index[1], index[2], pl.ds(start, count)], load_sem.at[len(loaded)])
                load.start()
                loaded.append(load)
                loads[turn, g].append(load)
    place.barrier()
    swaps = {}
    for turn, delta in enumerate((2, 1, -1, 0)):
        for g in range(3):
            j = place.step(ORDERS[g][0], delta)
            index, lo, n = index_of(g, 0, j)
            swaps[turn, g] = [send(ref, theirs.at[index[0], index[1], index[2], pl.ds(start, count)], place.partner()) for ref, start, count in sources(g, index, 1 - place.core)]

    def add_into(target, addend):
        target[...] = target[...] + addend[...]

    def ready(turn, g):
        delta = (2, 1, -1, 0)[turn]
        for load in loads[turn, g]:
            load.wait()
        for swap in swaps[turn, g]:
            swap.wait_recv()
        j = place.step(ORDERS[g][0], delta)
        add_into(in_own(own, g, 0, j), in_own(theirs, g, 0, j))

    def box(g, phase, slot, side):
        ref = boxes[g * 3 + phase]
        if phase < 2:
            return ref.at[slot]
        size = groups[g][1]
        cut = (size + 1) // 2
        return ref.at[slot, pl.ds(0, cut if side == 0 else size - cut)]

    for phase in range(3):
        flight = {}
        dims = [ORDERS[g][phase] for g in range(3)]

        def start(g, name, j_delta, side, slot, toward):
            j = place.step(dims[g], j_delta)
            flight[g, name] = send(in_own(own, g, phase, j, side), box(g, phase, slot, side), place.chip(dims[g], toward))

        for g in range(3):
            if phase == 0:
                ready(0, g)
            start(g, 'far_right', 2, 0, 0, 1)
            start(g, 'far_left', 2, 1, 2, -1)
        for g in range(3):
            if phase == 0:
                ready(1, g)
            start(g, 'near_right', 1, 1, 1, 1)
            if phase == 0:
                ready(2, g)
            start(g, 'near_left', -1, 0, 3, -1)
        for g in range(3):
            flight[g, 'far_right'].wait_recv()
            add_into(in_own(own, g, phase, place.step(dims[g], 1), 0), box(g, phase, 0, 0))
            start(g, 'sum_right', 1, 0, 4, 1)
            flight[g, 'far_left'].wait_recv()
            add_into(in_own(own, g, phase, place.step(dims[g], -1), 1), box(g, phase, 2, 1))
            start(g, 'sum_left', -1, 1, 5, -1)
        if phase == 0:
            for g in range(3):
                ready(3, g)
        for g in range(3):
            here = place.at[dims[g]]
            for name, slot, side in (('near_left', 3, 0), ('near_right', 1, 1)):
                flight[g, name].wait_recv()
                add_into(in_own(own, g, phase, here, side), box(g, phase, slot, side))
            for name, slot, side in (('sum_right', 4, 0), ('sum_left', 5, 1)):
                flight[g, name].wait_recv()
                add_into(in_own(own, g, phase, here, side), box(g, phase, slot, side))
    out_ref[place.core] = own[place.at[0], place.at[1], place.at[2]]
    piece = out_ref.at[place.core]
    send(piece, piece, place.partner()).wait_recv()
    for copy in pending:
        copy.wait_send()


def reduce_tiles(grad_low, grad_high, norm_low, norm_high, collective_id):
    half = 29
    norms = jnp.stack([norm_low, norm_high], axis=1)
    grids = [array.reshape((RING, RING, RING) + array.shape[1:]) for array in (grad_low, grad_high, norms)]
    groups = split_groups(half)
    box_shapes = []
    for g in range(3):
        order = ORDERS[g]
        size = groups[g][1]
        dims = {dim: RING for dim in range(3) if dim != order[0]}
        dims[order[1]] = 2
        box_shapes.append((6,) + tuple(dims[dim] for dim in sorted(dims)) + (size, 8, 128))
        box_shapes.append((6, 2, size, 8, 128))
        box_shapes.append((6, (size + 1) // 2, 8, 128))
    copies = 20 + 3 * 3 * 6 + 1
    return pl.pallas_call(
        reduce_kernel,
        out_shape=jax.ShapeDtypeStruct((2, half, 8, 128), jnp.float32),
        in_specs=[pl.BlockSpec(memory_space=pl.ANY)] * 3,
        out_specs=pl.BlockSpec(memory_space=pltpu.VMEM),
        scratch_shapes=[pltpu.VMEM((RING, RING, RING, half, 8, 128), jnp.float32)] * 2 + [pltpu.VMEM(shape, jnp.float32) for shape in box_shapes] + [pltpu.SemaphoreType.DMA((20,)), pltpu.SemaphoreType.DMA((copies,)), pltpu.SemaphoreType.DMA((copies,))],
        compiler_params=pltpu.CompilerParams(collective_id=collective_id, has_side_effects=True, vmem_limit_bytes=56 * 2 ** 20),
        name='reduce_tiles',
    )(*grids)


TILE = 256
NODE_TILE = TILE // 8
BF16 = jnp.bfloat16
F32 = jnp.float32


def dot(left, right, left_dim=1, right_dim=0):
    return lax.dot_general(left, right, (((left_dim,), (right_dim,)), ((), ())), preferred_element_type=F32)


def split_three(values):
    high = values.astype(BF16)
    rest = values - high.astype(F32)
    mid = rest.astype(BF16)
    low = (rest - mid.astype(F32)).astype(BF16)
    return high, mid, low


def dot_wide(values, right, right_dim=0):
    high, mid, low = split_three(values)
    return dot(high, right, 1, right_dim) + dot(mid, right, 1, right_dim) + dot(low, right, 1, right_dim)


def dot_wide_rows(left, values):
    high, mid, low = split_three(values)
    return dot(left, high, 0, 0) + dot(left, mid, 0, 0) + dot(left, low, 0, 0)


def norm_stats(out_b):
    values = out_b.astype(F32)
    centered = values - jnp.mean(values, axis=-1, keepdims=True)
    inv_std = lax.rsqrt(jnp.mean(centered * centered, axis=-1, keepdims=True) + NORM_EPS)
    return centered * inv_std, inv_std


def mlp_forward(pre_act, w_two, gain, bias):
    pre_b = pre_act.astype(BF16)
    hidden = jax.nn.silu(pre_b.astype(F32)).astype(BF16)
    out_b = dot(hidden, w_two).astype(BF16)
    normed, _ = norm_stats(out_b)
    return normed * gain + bias, pre_b, out_b


def mlp_cotangents(d_branch, pre_b, out_b, w_two, gain):
    normed, inv_std = norm_stats(out_b)
    d_norm = d_branch * gain
    d_out = (inv_std * (d_norm - jnp.mean(d_norm, axis=-1, keepdims=True) - normed * jnp.mean(d_norm * normed, axis=-1, keepdims=True))).astype(BF16)
    d_act = dot(d_out, w_two, 1, 1).astype(BF16)
    pre_f = pre_b.astype(F32)
    gate = jax.nn.sigmoid(pre_f)
    hidden = (pre_f * gate).astype(BF16)
    d_pre = (d_act.astype(F32) * gate * (1.0 + pre_f * (1.0 - gate))).astype(BF16)
    d_gain = (d_branch * normed).reshape(-1, 8, d_branch.shape[-1]).sum(axis=0)
    d_bias = d_branch.reshape(-1, 8, d_branch.shape[-1]).sum(axis=0)
    return d_out, hidden, d_pre, d_gain, d_bias


def receiver_pick(copies):
    rows = lax.broadcasted_iota(jnp.int32, (TILE, copies * NODE_TILE), 0)
    cols = lax.broadcasted_iota(jnp.int32, (TILE, copies * NODE_TILE), 1)
    return lax.shift_right_logical(rows, 3) == lax.bitwise_and(cols, NODE_TILE - 1)


def as_bf16(flags):
    return jnp.where(flags, 1.0, 0.0).astype(BF16)


def unpack_weights(tiles_ref, layer, w_e1, w_e2, w_n1, w_n2, norms):
    def pair(p, carry):
        for k in range(4):
            lanes = pl.ds(128 * k, 128)
            w_e1[pl.ds(pl.multiple_of(48 * p, 16), 16), lanes] = tiles_ref[2 * p, 8 * layer + k]
            w_e1[pl.ds(pl.multiple_of(48 * p + 32, 16), 16), lanes] = tiles_ref[2 * p + 1, 8 * layer + k]
            w_n1[pl.ds(pl.multiple_of(32 * p, 16), 16), lanes] = tiles_ref[2 * p, 8 * layer + 4 + k]
            w_n1[pl.ds(pl.multiple_of(32 * p + 16, 16), 16), lanes] = tiles_ref[2 * p + 1, 8 * layer + 4 + k]
            for ref, first, tile in ((w_e1, 48 * p + 16, 16), (w_e2, 16 * p, 20), (w_n2, 16 * p, 24)):
                even = tiles_ref[2 * p, tile + k].astype(F32)[8 * layer:8 * layer + 8]
                odd = tiles_ref[2 * p + 1, tile + k].astype(F32)[8 * layer:8 * layer + 8]
                ref[pl.ds(pl.multiple_of(first, 16), 16), lanes] = jnp.concatenate([even, odd], axis=0).astype(BF16)
        return carry
    lax.fori_loop(0, 32, pair, 0)
    for k in range(4):
        total = tiles_ref[16 * k, 28].astype(F32)
        for d in range(1, 16):
            total = total + tiles_ref[16 * k + d, 28].astype(F32)
        norms[:, 128 * k:128 * k + 128] = total[8 * layer:8 * layer + 8]


def edge_forward(layer_io, edge_out, pre_out, out_out, sums_out, w_e1, w_e2, norms, recv_terms):
    node_all, node_own, edge_in, snd_col, mask_col = layer_io
    for part, term in enumerate(split_three(dot(node_own[...], w_e1[1024:1536]))):
        recv_terms[part] = term

    def tile(i, carry):
        rows = pl.ds(pl.multiple_of(i * TILE, TILE), TILE)
        nodes = pl.ds(pl.multiple_of(i * NODE_TILE, NODE_TILE), NODE_TILE)
        ids = lax.broadcasted_iota(jnp.int32, (TILE, 512), 1)
        sender = dot(as_bf16(snd_col[rows] == ids), node_all[...]).astype(BF16)
        recv = jnp.concatenate([recv_terms[0, nodes], recv_terms[1, nodes], recv_terms[2, nodes]], axis=0)
        edge = edge_in[rows]
        pre = dot(edge, w_e1[0:512]) + dot(sender, w_e1[512:1024]) + dot(as_bf16(receiver_pick(3)), recv)
        branch, pre_b, out_b = mlp_forward(pre, w_e2[...], norms[0:1], norms[1:2])
        edge_new = (edge.astype(F32) + branch).astype(BF16)
        pre_out[rows] = pre_b
        out_out[rows] = out_b
        if edge_out is not None:
            edge_out[rows] = edge_new
        picked = jnp.where(receiver_pick(1), mask_col[rows], 0.0).astype(BF16)
        sums_out[nodes] = dot(picked, edge_new, 0, 0).astype(BF16)
        return carry
    lax.fori_loop(0, edge_in.shape[0] // TILE, tile, 0)


def node_forward(node_own, sums, w_n1, w_n2, norms):
    pre = dot(node_own[...], w_n1[0:512]) + dot(sums[...], w_n1[512:1024])
    return mlp_forward(pre, w_n2[...], norms[2:3], norms[3:4])


def store_grad(grad_ref, values, first_row, shard_rows, first_tile):
    for q in range(values.shape[0] // 8):
        place = first_row // 8 + q
        per = shard_rows // 8
        for k in range(4):
            grad_ref[place // per, first_tile + place % per * 4 + k] = values[8 * q:8 * q + 8, 128 * k:128 * k + 128]


def layer_back(layer_io, d_node_new, d_edge_new, pre_e, out_e, sums, pre_n, out_n, mats, norms, snd_row, outs, scratch):
    node_all, node_own, edge_in, snd_col, mask_col = layer_io
    w_e1, w_e2, w_n1, w_n2 = mats
    grad_ref, norm_grad, d_edge, d_local, scattered = outs
    hidden_s, d_pre_s, d_out_s, d_sum_s, recv_s, gain_s = scratch
    d_out_n, hidden_n, d_pre_n, d_gain_n, d_bias_n = mlp_cotangents(d_node_new, pre_n, out_n, w_n2[...], norms[2:3])
    d_sum_s[...] = dot(d_pre_n, w_n1[512:1024], 1, 1).astype(BF16)
    d_local[...] = d_node_new + dot(d_pre_n, w_n1[0:512], 1, 1)
    store_grad(grad_ref, dot(hidden_n, d_out_n, 0, 0), 0, 8, 24)
    store_grad(grad_ref, dot(node_own[...], d_pre_n, 0, 0), 0, 16, 16)
    store_grad(grad_ref, dot(sums[...], d_pre_n, 0, 0), 512, 16, 16)
    gain_s[...] = jnp.zeros_like(gain_s)

    def tile(i, carry):
        rows = pl.ds(pl.multiple_of(i * TILE, TILE), TILE)
        nodes = pl.ds(pl.multiple_of(i * NODE_TILE, NODE_TILE), NODE_TILE)
        pick = receiver_pick(1)
        picked = jnp.where(pick, mask_col[rows], 0.0).astype(BF16)
        d_res = (d_edge_new[rows].astype(F32) + dot(picked, d_sum_s[nodes])).astype(BF16).astype(F32)
        d_out, hidden, d_pre, d_gain, d_bias = mlp_cotangents(d_res, pre_e[rows], out_e[rows], w_e2[...], norms[0:1])
        gain_s[0] = gain_s[0] + d_gain
        gain_s[1] = gain_s[1] + d_bias
        hidden_s[rows] = hidden
        d_out_s[rows] = d_out
        d_pre_s[rows] = d_pre
        d_edge[rows] = (d_res + dot(d_pre, w_e1[0:512], 1, 1)).astype(BF16)
        recv_s[nodes] = dot(as_bf16(pick), d_pre, 0, 0)
        return carry
    lax.fori_loop(0, edge_in.shape[0] // TILE, tile, 0)
    store_grad(grad_ref, dot(hidden_s[...], d_out_s[...], 0, 0), 0, 8, 12)
    store_grad(grad_ref, dot(edge_in[...], d_pre_s[...], 0, 0), 0, 24, 0)
    for block in range(4):
        ids = lax.broadcasted_iota(jnp.int32, (128, edge_in.shape[0]), 0) + 128 * block
        scattered[128 * block:128 * block + 128] = dot(as_bf16(snd_row[...] == ids), d_pre_s[...])
    store_grad(grad_ref, dot_wide_rows(node_all[...], scattered[...]), 512, 24, 0)
    store_grad(grad_ref, dot_wide_rows(node_own[...], recv_s[...]), 1024, 24, 0)
    d_local[...] = d_local[...] + dot_wide(recv_s[...], w_e1[1024:1536], 1)
    rows = [gain_s[0].sum(axis=0, keepdims=True), gain_s[1].sum(axis=0, keepdims=True), d_gain_n.sum(axis=0, keepdims=True), d_bias_n.sum(axis=0, keepdims=True)]
    full = jnp.concatenate(rows + [jnp.zeros((4, 512), F32)], axis=0)
    for d in range(64):
        k = d // 16
        norm_grad[d] = full[:, 128 * k:128 * k + 128]


def own_nodes(node_all):
    count = node_all.shape[0] // 2
    return node_all.at[pl.ds(pl.multiple_of(lax.axis_index('sp') * count, count), count)]


def forward_kernel(tiles_ref, node_all, edge_in, snd_col, mask_col, edge_out, pre_e, out_e, sums, pre_n, out_n, node_new, *rest):
    mats = (rest[0:4], rest[5:9])
    norms = (rest[4], rest[9])
    recv_terms = rest[10]
    for layer in range(2):
        unpack_weights(tiles_ref, layer, *mats[layer], norms[layer])
    node_own = own_nodes(node_all)
    w_e1, w_e2, w_n1, w_n2 = mats[0]
    edge_forward((node_all, node_own, edge_in, snd_col, mask_col), edge_out, pre_e, out_e, sums, w_e1, w_e2, norms[0], recv_terms)
    branch, pre_b, out_b = node_forward(node_own, sums, w_n1, w_n2, norms[0])
    pre_n[...] = pre_b
    out_n[...] = out_b
    node_new[...] = (node_own[...].astype(F32) + branch).astype(BF16)


def middle_kernel(node_all, edge_in, snd_col, snd_row, mask_col, node_cot, edge_cot, w_e1, w_e2, w_n1, w_n2, norms, grad_ref, norm_grad, d_edge, d_local, scattered, pre_e, out_e, sums, recv_terms, *scratch):
    node_own = own_nodes(node_all)
    layer_io = (node_all, node_own, edge_in, snd_col, mask_col)
    edge_forward(layer_io, None, pre_e, out_e, sums, w_e1, w_e2, norms, recv_terms)
    _, pre_n, out_n = node_forward(node_own, sums, w_n1, w_n2, norms)
    layer_back(layer_io, node_cot[...].astype(F32), edge_cot, pre_e, out_e, sums, pre_n, out_n, (w_e1, w_e2, w_n1, w_n2), norms, snd_row, (grad_ref, norm_grad, d_edge, d_local, scattered), scratch)


def node_cotangent(d_local, scattered, returned, w_above):
    count = d_local.shape[0]
    mine = scattered[pl.ds(pl.multiple_of(lax.axis_index('sp') * count, count), count)]
    return (d_local[...] + dot_wide(mine + returned[...], w_above[512:1024], 1)).astype(BF16)


def back_kernel(node_all, edge_in, snd_col, snd_row, mask_col, d_local_above, scattered_above, returned, w_above, d_edge_new, pre_e, out_e, sums, pre_n, out_n, w_e1, w_e2, w_n1, w_n2, norms, grad_ref, norm_grad, d_edge, d_local, scattered, *scratch):
    node_own = own_nodes(node_all)
    layer_io = (node_all, node_own, edge_in, snd_col, mask_col)
    d_node = node_cotangent(d_local_above, scattered_above, returned, w_above).astype(F32)
    layer_back(layer_io, d_node, d_edge_new, pre_e, out_e, sums, pre_n[...], out_n[...], (w_e1, w_e2, w_n1, w_n2), norms, snd_row, (grad_ref, norm_grad, d_edge, d_local, scattered), scratch)


def last_kernel(d_local, scattered, returned, w_e1, grad_node):
    grad_node[...] = node_cotangent(d_local, scattered, returned, w_e1)


def swap_kernel(src_ref, out_ref, send_sem, recv_sem):
    core = lax.axis_index('sp')
    sem = pltpu.get_barrier_semaphore()
    pl.semaphore_signal(sem, inc=1, device_id={'sp': 1 - core}, device_id_type=MESH_ID)
    pl.semaphore_wait(sem, 1)
    count = out_ref.shape[0]
    start = pl.multiple_of((1 - core) * count, count)
    copy = pltpu.make_async_remote_copy(src_ref=src_ref.at[pl.ds(start, count)], dst_ref=out_ref, send_sem=send_sem, recv_sem=recv_sem, device_id={'sp': 1 - core}, device_id_type=MESH_ID)
    copy.start()
    copy.wait()


def vmem_call(kernel, name, inputs, outputs, scratch, flops):
    spec = pl.BlockSpec(memory_space=pltpu.VMEM)
    return pl.pallas_call(
        kernel,
        out_shape=[jax.ShapeDtypeStruct(shape, dtype) for shape, dtype in outputs],
        in_specs=[spec] * len(inputs),
        out_specs=[spec] * len(outputs),
        scratch_shapes=[pltpu.VMEM(shape, dtype) for shape, dtype in scratch],
        compiler_params=pltpu.CompilerParams(vmem_limit_bytes=62 * 2 ** 20),
        cost_estimate=pl.CostEstimate(flops=flops, bytes_accessed=20 * 2 ** 20, transcendentals=0),
        name=name,
    )(*inputs)


def swap_halves(values, collective_id):
    return pl.pallas_call(
        swap_kernel,
        out_shape=jax.ShapeDtypeStruct((values.shape[0] // 2,) + values.shape[1:], values.dtype),
        in_specs=[pl.BlockSpec(memory_space=pltpu.VMEM)],
        out_specs=pl.BlockSpec(memory_space=pltpu.VMEM),
        scratch_shapes=[pltpu.SemaphoreType.DMA, pltpu.SemaphoreType.DMA],
        compiler_params=pltpu.CompilerParams(collective_id=collective_id, has_side_effects=True),
        name='swap_halves',
    )(values)


MAT_SHAPES = [((1536, 512), BF16), ((512, 512), BF16), ((1024, 512), BF16), ((512, 512), BF16), ((8, 512), F32)]
GRAD_SHAPES = [((64, 28, 8, 128), F32), ((64, 8, 128), F32), ((2048, 512), BF16), ((256, 512), F32), ((512, 512), F32)]
BACK_SCRATCH = [((2048, 512), BF16)] * 3 + [((256, 512), BF16), ((256, 512), F32), ((2, 8, 512), F32)]
EDGE = ((2048, 512), BF16)
NODE = ((256, 512), BF16)


def adamw_update(master, grad_sum, moment_one, moment_two):
    corr_one = 1.0 - BETA_ONE ** STEP
    corr_two = 1.0 - BETA_TWO ** STEP
    one_new = BETA_ONE * moment_one + (1.0 - BETA_ONE) * grad_sum
    two_new = BETA_TWO * moment_two + (1.0 - BETA_TWO) * grad_sum * grad_sum
    direction = (one_new / corr_one) / (jnp.sqrt(two_new / corr_two) + ADAM_EPS)
    return master - LEARN_RATE * (direction + DECAY * master), one_new, two_new


def update_all(masters, moments_one, moments_two, layer_grads):
    new_master = []
    new_one = []
    new_two = []
    for slot in range(len(masters)):
        grad_sum = jnp.stack([per_layer[slot] for per_layer in layer_grads], axis=0)
        master_new, one_new, two_new = adamw_update(masters[slot], grad_sum, moments_one[slot], moments_two[slot])
        new_master.append(master_new)
        new_one.append(one_new)
        new_two.append(two_new)
    return tuple(new_master) + tuple(new_one) + tuple(new_two)


def rows_to_tiles(values, sub):
    rows = values.shape[0]
    return values.reshape(rows // sub, sub, 4, 128).transpose(0, 2, 1, 3).reshape(rows // sub * 4, sub, 128)


def tiles_to_rows(tiles):
    count, sub = tiles.shape[:2]
    return tiles.reshape(count // 4, 4, sub, 128).transpose(0, 2, 1, 3).reshape(count // 4 * sub, 512)


def pack_shard(masters):
    chip = lax.axis_index('dp')
    odd = lax.rem(chip, 2) == 1
    edge_one, edge_two, node_one, node_two, norm = [master.astype(BF16) for master in masters]
    main = jnp.where(odd, edge_one[:, 8:24], edge_one[:, 0:16])
    tail = jnp.where(odd, edge_one[:, 0:8], edge_one[:, 16:24])
    rows = jnp.concatenate([main[0], node_one[0], main[1], node_one[1], tail[0], tail[1], edge_two[0], edge_two[1], node_two[0], node_two[1]], axis=0)
    wide = jnp.tile(norm, (1, 1, 16))
    lanes = lax.broadcasted_iota(jnp.int32, wide.shape, 2) // 8
    wide = jnp.where(lanes == lax.rem(chip, 16), wide, 0)
    norms = jnp.pad(wide, ((0, 0), (0, 4), (0, 0))).reshape(1, 16, 128)
    return jnp.concatenate([rows_to_tiles(rows, 16), norms, jnp.zeros_like(norms)], axis=0)


def unpack_grads(total):
    chip = lax.axis_index('dp')
    out = []
    for layer in range(2):
        tiles = jnp.concatenate([total[0, 14 * layer:14 * layer + 14], total[1, 14 * layer:14 * layer + 14]], axis=0)
        rows = tiles_to_rows(tiles)
        norm = lax.dynamic_slice(total[layer, 28], (0, lax.rem(chip, 16) * 8), (4, 8))
        mats = []
        first = 0
        for size in SHARD_ROWS:
            mats.append(rows[first:first + size])
            first += size
        out.append(tuple(mats) + (norm,))
    return out


def solution(mesh):
    lat_spec = P('dp', 'sp', None)
    edge_spec = P('sp')
    mat_spec = P(None, 'dp', None)
    norm_spec = P(None, None, 'dp')
    param_specs = (mat_spec, mat_spec, mat_spec, mat_spec, norm_spec)

    def train_step(node_lat, edge_lat, senders, edge_mask, node_cot, edge_cot, w_edge1, w_edge2, w_node1, w_node2, norm_par, mom_edge1, mom_edge2, mom_node1, mom_node2, mom_norm, vel_edge1, vel_edge2, vel_node1, vel_node2, vel_norm):
        masters = (w_edge1, w_edge2, w_node1, w_node2, norm_par)
        moments_one = (mom_edge1, mom_edge2, mom_node1, mom_node2, mom_norm)
        moments_two = (vel_edge1, vel_edge2, vel_node1, vel_node2, vel_norm)
        snd_col = senders.reshape(-1, 1)
        snd_row = senders.reshape(1, -1)
        mask_col = edge_mask.astype(F32).reshape(-1, 1)
        tiles = gather_tiles(pack_shard(masters), 1).reshape(64, 30, 16, 128)
        node_all = lax.all_gather(node_lat[0], 'sp', axis=0, tiled=True)
        outs = vmem_call(forward_kernel, 'forward_low', (tiles, node_all, edge_lat[0], snd_col, mask_col), [EDGE, EDGE, EDGE, NODE, NODE, NODE, NODE] + MAT_SHAPES + MAT_SHAPES, [((3, 256, 512), BF16)], 5 * 10 ** 9)
        edge_one, pre_e, out_e, sums, pre_n, out_n, node_one = outs[:7]
        mats_low = outs[7:12]
        mats_high = outs[12:17]
        node_all_one = lax.all_gather(node_one, 'sp', axis=0, tiled=True)
        grad_high, norm_high, d_edge_one, d_local_one, scattered_one = vmem_call(middle_kernel, 'forward_back_high', (node_all_one, edge_one, snd_col, snd_row, mask_col, node_cot[0], edge_cot[0]) + tuple(mats_high), GRAD_SHAPES, [EDGE, EDGE, NODE, ((3, 256, 512), BF16)] + BACK_SCRATCH, 13 * 10 ** 9)
        returned = swap_halves(scattered_one, 3)
        grad_low, norm_low, d_edge_zero, d_local_zero, scattered_zero = vmem_call(back_kernel, 'back_low', (node_all, edge_lat[0], snd_col, snd_row, mask_col, d_local_one, scattered_one, returned, mats_high[0], d_edge_one, pre_e, out_e, sums, pre_n, out_n) + tuple(mats_low), GRAD_SHAPES, BACK_SCRATCH, 8 * 10 ** 9)
        returned_zero = swap_halves(scattered_zero, 4)
        grad_node = vmem_call(last_kernel, 'node_grad', (d_local_zero, scattered_zero, returned_zero, mats_low[0]), [NODE], [], 4 * 10 ** 8)[0]
        total = reduce_tiles(grad_low, grad_high, norm_low, norm_high, 2)
        new_state = update_all(masters, moments_one, moments_two, unpack_grads(total))
        return new_state + (grad_node[None], d_edge_zero[None])

    return jax.shard_map(train_step, mesh=mesh, in_specs=(lat_spec, lat_spec, edge_spec, edge_spec, lat_spec, lat_spec) + param_specs + param_specs + param_specs, out_specs=param_specs + param_specs + param_specs + (lat_spec, lat_spec), check_vma=False)
```

time: 422 us -> 209 us (0.50); the launches traced: 414 us -> 208 us
  local copies, waits for them, and re-layouts: 119 us -> 8.14 us
  Pallas kernels: 87.4 us -> 181 us
  matrix products: 88.6 us -> 0 us
  other arithmetic: 97.7 us -> 9.99 us
  between operations: 16.1 us -> 1.04 us
    pallas_call x1 -> x7, Pallas kernels: 47.9 us -> 143 us  [the longest x4 86.3 us: vmem_call(): pl.pallas_call(kernel, out_shape=[jax.ShapeDtypeStruct(shape, dtype) for...]
    dot_general x38 -> x0, matrix products: 88.6 us -> none  [the longest x36 85.6 us: contract(): lax.dot_general(left_op, right_op, ((left_dims, right_dims), ((), ())), p...]
    scatter-add x2 -> x0, other arithmetic: 35.2 us -> none  [layer_backward(): jnp.zeros((batch_size, total_nodes, lat_width), jnp.float32).at[:, senders]]
    reduce_sum x10 -> x0, other arithmetic: 24.2 us -> none  [the longest x4 15.4 us: mlp_back(): d_gain = jnp.sum(d_branch * normed, axis=lead_dims)]
    unnamed x240 -> x45, local copies, waits for them, and re-layouts: 26.4 us -> 3.19 us
    dot_general x7 -> x0, local copies, waits for them, and re-layouts: 18.2 us -> none  [contract(): lax.dot_general(left_op, right_op, ((left_dims, right_dims), ((), ())), p...]
    gather x2 -> x0, local copies, waits for them, and re-layouts: 16.7 us -> none  [layer_forward(): sender_lat = jnp.take(node_all, senders, axis=1).reshape(edge_x.shape)]
    slice x10 -> x1, local copies, waits for them, and re-layouts: 17.4 us -> 0.74 us  [unpack_grads(): total[layer, 28]]
  transfers between devices with their start and end apart: 2 -> 0, of which waited for: 0 -> 0; matrix products, arithmetic and copies ran while one was open for 17% -> 0% of each run, Pallas kernels for 12% -> 0%
where the time goes in v2:
time: 209 us; the launch traced here: 208 us
  Pallas kernels  181 us (87%)
  other arithmetic  9.99 us (5%)
  blocking collectives  8.35 us (4%)
  local copies, waits for them, and re-layouts  8.14 us (4%)
    pallas_call x4, Pallas kernels, vmem_call(): pl.pallas_call(kernel, out_shape=[jax.ShapeDtypeStruct(shape, dtype) for...  86.3 us
    pallas_call x1, Pallas kernels, reduce_tiles(): pl.pallas_call(reduce_kernel, out_shape=jax.ShapeDtypeStruct((2, half, 8,...  48.5 us
    pallas_call x1, Pallas kernels, gather_tiles(): pl.pallas_call(functools.partial(gather_kernel, tiles), out_shape=jax.Sha...  38.3 us
    pallas_call x2, Pallas kernels, swap_halves(): pl.pallas_call(swap_kernel, out_shape=jax.ShapeDtypeStruct((values.shape[...  7.91 us
    all_gather x1, blocking collectives, train_step(): node_all = lax.all_gather(node_lat[0], 'sp', axis=0, tiled=True)  4.67 us

profile of v2, /device:TPU:1, one launch (start us, length us, event | category | flops | bytes accessed | tf_op | source)
XLA Modules:
  0.0 208.5 jit_solution(16019730832202708495)
XLA Ops:
  0.7 0.0 copy-start.15
  0.7 0.1 pad.23.clone
  0.8 0.7 convert_element_type.27
  1.5 0.7 convert_element_type.22
  2.2 0.8 convert_element_type.25
  2.9 0.8 convert_element_type.26
  3.7 0.1 tile.10
  3.8 0.8 convert_element_type.24
  4.7 0.9 convert_element_type.23
  5.8 0.1 maximum_maximum_fusion.src_ref
  5.9 4.7 %all-gather = bf16[1,512,512]{2,1,0:T(8,128)(2,1)} all-gather(bf16[1,256,512]{2,1,0:T(8,128)(2,1)} %param.21), channel_id=2, replica_groups=mesh['sp'=2,'dp'=64] {'sp'}, dimensions={1}, use_global_device_ids=true | all-gather | bytes 786432 | tf_op jit(solution)/shard_map/all_gather | solution.py:640
  10.5 1.4 copy.45.mask_col
  12.0 0.0 copy-done.15
  12.0 1.5 copy.44.snd_col
  13.4 38.3 %gather_tiles.1 = bf16[4,4,4,30,16,128]{5,4,3,2,1,0:T(8,128)(2,1)S(1)} custom-call(bf16[30,16,128]{2,1,0:T(8,128)(2,1)S(1)} %maximum_maximum_fusion.src_ref), custom_call_target="tpu_custom_call" | custom-call | tf_op jit(solution)/shard_map/gather_tiles/pallas_call | solution.py:133
  51.7 3.1 %copy-done = bf16[4,4,4,30,16,128]{5,4,3,2,1,0:T(8,128)(2,1)} copy-done((bf16[4,4,4,30,16,128]{5,4,3,2,1,0:T(8,128)(2,1)}, bf16[4,4,4,30,16,128]{5,4,3,2,1,0:T(8,128)(2,1)S(1)}, u32[]{:S(2)}) %copy-start) | copy-done | bytes 7864344
  54.8 22.1 %forward_low.1 = (bf16[2048,512]{1,0:T(8,128)(2,1)}, bf16[2048,512]{1,0:T(8,128)(2,1)}, bf16[2048,512]{1,0:T(8,128)(2,1)}, bf16[256,512]{1,0:T(8,128)(2,1)}, bf1...) custom-call(bf16[64,30,16,128]{3,2,1,0:T(8,128)(2,1)} %bitcast.96, ...), custom_call_target="tpu_custom_call" | custom-call | flops 5000000000 | bytes 20971520 | tf_op jit(solution)/shard_map/forward_low/pallas_call | solution.py:532
  76.9 3.7 %all_gather.7.node_all = bf16[512,512]{1,0:T(8,128)(2,1)} all-gather(bf16[256,512]{1,0:T(8,128)(2,1)} %get-tuple-element.44), channel_id=1, replica_groups=mesh['sp'=2,'dp'=64] {'sp'}, dimensions={0}, use_global_device_ids=true | all-gather | bytes 786432 | tf_op jit(solution)/shard_map/all_gather | solution.py:645
  80.6 34.6 %forward_back_high.1 = (f32[64,28,8,128]{3,2,1,0:T(8,128)}, f32[64,8,128]{2,1,0:T(8,128)}, bf16[2048,512]{1,0:T(8,128)(2,1)}, f32[256,512]{1,0:T(8,128)}, f32[512,512]{1,0:T(8,128)}) custom-call(bf16[512,512]{1,0:T(8,128)(2,1)} %all_gather.7.node_all, bf16[2048,512]{1,0:T(8,128)(2,1)} %get-tuple-element.45.edge_in, s32[2048,1]{1,0:T(8,128)} %copy.44.snd_col, ...), custom_call_target="tpu_custom_call" | custom-call | flops 12999999488 | bytes 20971520 | tf_op jit(solution)/shard_map/forward_back_high/pallas_call | solution.py:532
  115.2 3.9 %swap_halves.2.returned = f32[256,512]{1,0:T(8,128)} custom-call(f32[512,512]{1,0:T(8,128)} %get-tuple-element.52.src_ref.scattered_above), custom_call_target="tpu_custom_call" | custom-call | tf_op jit(solution)/shard_map/swap_halves/pallas_call | solution.py:545
  119.1 26.2 %back_low.1 = (f32[64,28,8,128]{3,2,1,0:T(8,128)}, f32[64,8,128]{2,1,0:T(8,128)}, bf16[2048,512]{1,0:T(8,128)(2,1)}, f32[256,512]{1,0:T(8,128)}, f32[512,512]{1,0:T(8,128)}) custom-call(bf16[512,512]{1,0:T(8,128)(2,1)} %bitcast.100, bf16[2048,512]{1,0:T(8,128)(2,1)} %bitcast.117, s32[2048,1]{1,0:T(8,128)} %copy.44.snd_col, s32[1,2048]{1,0:T(1,128)} %bitcast.113, ...), custom_call_target="tpu_custom_call" | custom-call | flops 8000000000 | bytes 20971520 | tf_op jit(solution)/shard_map/back_low/pallas_call | solution.py:532
  145.4 1.8 pad_maximum_fusion.norm_ref
  147.2 0.0 copy-start.10
  147.2 0.0 copy-start.11
  147.2 0.0 copy-start.5
  147.2 0.0 copy-start.12
  147.2 0.0 copy-start.13
  147.2 0.0 copy-start.2
  147.2 0.0 copy-start.8
  147.2 0.0 copy-start.9
  147.3 48.5 %reduce_tiles.1 = f32[2,29,8,128]{3,2,1,0:T(8,128)} custom-call(f32[4,4,4,28,8,128]{5,4,3,2,1,0:T(8,128)} %bitcast.98, f32[4,4,4,28,8,128]{5,4,3,2,1,0:T(8,128)} %bitcast.97, f32[4,4,4,2,8,128]{5,4,3,2,1,0:T(8,128)} %pad_maximum_fusion.norm_ref), custom_call_target="tpu_custom_call" | custom-call | tf_op jit(solution)/shard_map/reduce_tiles/pallas_call | solution.py:292
  195.8 0.0 copy-start.1
  195.8 0.0 copy-start.6
  195.8 0.0 copy-start.7
  195.8 0.7 fusion.11
  196.5 0.9 slice_bitcast_fusion.3
  197.5 0.1 dynamic-slice_bitcast_fusion.1
  197.6 0.1 dynamic-slice_bitcast_fusion
  197.6 0.0 copy-done.14
  197.6 0.6 multiply_subtract_fusion.4
  198.4 0.7 multiply_subtract_fusion.2
  199.0 0.0 copy-done.5
  199.0 0.7 multiply_subtract_fusion.3
  199.7 0.0 copy-done.8
  199.7 0.7 multiply_subtract_fusion.1
  200.4 0.7 multiply_subtract_fusion
  201.2 4.0 %swap_halves.3.returned = f32[256,512]{1,0:T(8,128)} custom-call(f32[512,512]{1,0:T(8,128)} %get-tuple-element.69.src_ref.scattered), custom_call_target="tpu_custom_call" | custom-call | tf_op jit(solution)/shard_map/swap_halves/pallas_call | solution.py:545
  205.1 3.4 %node_grad.1 = bf16[256,512]{1,0:T(8,128)(2,1)} custom-call(f32[256,512]{1,0:T(8,128)} %get-tuple-element.68.d_local, f32[512,512]{1,0:T(8,128)} %get-tuple-element.69.src_ref.scattered, f32[256,512]{1,0:T(8,128)} %swap_halves.3.returned, bf16[1536,512]{1,0:T(8,128)(2,1)} %get-tuple-element.59.w_e1), custom_call_target="tpu_custom_call" | custom-call | flops 400000000 | bytes 20971520 | tf_op jit(solution)/shard_map/node_grad/pallas_call | solution.py:532
  (46 shorter events, 0.2 us)
Async XLA Ops:
  0.7 11.3 %copy-start.15 = (s32[2048]{0:T(1024)S(1)}, s32[2048]{0:T(1024)}, u32[]{:S(2)}) copy-start(s32[2048]{0:T(1024)} %param.23) | copy-start | bytes 24580
  51.7 3.1 %copy-start = (bf16[4,4,4,30,16,128]{5,4,3,2,1,0:T(8,128)(2,1)}, bf16[4,4,4,30,16,128]{5,4,3,2,1,0:T(8,128)(2,1)S(1)}, u32[]{:S(2)}) copy-start(bf16[4,4,4,30,16,128]{5,4,3,2,1,0:T(8,128)(2,1)S(1)} %gather_tiles.1) | copy-start | bytes 23592964
  119.1 26.2 %copy-start.3 = (f32[64,8,128]{2,1,0:T(8,128)S(1)}, f32[64,8,128]{2,1,0:T(8,128)}, u32[]{:S(2)}) copy-start(f32[64,8,128]{2,1,0:T(8,128)} %get-tuple-element.67) | copy-start | bytes 786436
  147.1 50.5 %copy-start.14 = (f32[2,4,8]{2,1,0:T(4,128)S(1)}, f32[2,4,8]{2,1,0:T(4,128)}, u32[]{:S(2)}) copy-start(f32[2,4,8]{2,1,0:T(4,128)} %param.31) | copy-start | bytes 772
  147.2 50.5 %copy-start.16 = (f32[2,4,8]{2,1,0:T(4,128)S(1)}, f32[2,4,8]{2,1,0:T(4,128)}, u32[]{:S(2)}) copy-start(f32[2,4,8]{2,1,0:T(4,128)} %param.36) | copy-start | bytes 772
  147.2 50.5 %copy-start.17 = (f32[2,4,8]{2,1,0:T(4,128)S(1)}, f32[2,4,8]{2,1,0:T(4,128)}, u32[]{:S(2)}) copy-start(f32[2,4,8]{2,1,0:T(4,128)} %param.41) | copy-start | bytes 772
  147.2 51.2 %copy-start.4 = (f32[2,8,512]{2,1,0:T(8,128)S(1)}, f32[2,8,512]{2,1,0:T(8,128)}, u32[]{:S(2)}) copy-start(f32[2,8,512]{2,1,0:T(8,128)} %param.30) | copy-start | bytes 98308
  147.2 51.2 %copy-start.10 = (f32[2,8,512]{2,1,0:T(8,128)S(1)}, f32[2,8,512]{2,1,0:T(8,128)}, u32[]{:S(2)}) copy-start(f32[2,8,512]{2,1,0:T(8,128)} %param.35) | copy-start | bytes 98308
  147.2 51.2 %copy-start.11 = (f32[2,8,512]{2,1,0:T(8,128)S(1)}, f32[2,8,512]{2,1,0:T(8,128)}, u32[]{:S(2)}) copy-start(f32[2,8,512]{2,1,0:T(8,128)} %param.40) | copy-start | bytes 98308
  147.2 51.8 %copy-start.5 = (f32[2,8,512]{2,1,0:T(8,128)S(1)}, f32[2,8,512]{2,1,0:T(8,128)}, u32[]{:S(2)}) copy-start(f32[2,8,512]{2,1,0:T(8,128)} %param.28) | copy-start | bytes 98308
  147.2 51.8 %copy-start.12 = (f32[2,8,512]{2,1,0:T(8,128)S(1)}, f32[2,8,512]{2,1,0:T(8,128)}, u32[]{:S(2)}) copy-start(f32[2,8,512]{2,1,0:T(8,128)} %param.33) | copy-start | bytes 98308
  147.2 51.8 %copy-start.13 = (f32[2,8,512]{2,1,0:T(8,128)S(1)}, f32[2,8,512]{2,1,0:T(8,128)}, u32[]{:S(2)}) copy-start(f32[2,8,512]{2,1,0:T(8,128)} %param.38) | copy-start | bytes 98308
  147.2 52.5 %copy-start.2 = (f32[2,16,512]{2,1,0:T(8,128)S(1)}, f32[2,16,512]{2,1,0:T(8,128)}, u32[]{:S(2)}) copy-start(f32[2,16,512]{2,1,0:T(8,128)} %param.29) | copy-start | bytes 196612
  147.2 52.5 %copy-start.8 = (f32[2,16,512]{2,1,0:T(8,128)S(1)}, f32[2,16,512]{2,1,0:T(8,128)}, u32[]{:S(2)}) copy-start(f32[2,16,512]{2,1,0:T(8,128)} %param.34) | copy-start | bytes 196612
  147.2 52.4 %copy-start.9 = (f32[2,16,512]{2,1,0:T(8,128)S(1)}, f32[2,16,512]{2,1,0:T(8,128)}, u32[]{:S(2)}) copy-start(f32[2,16,512]{2,1,0:T(8,128)} %param.39) | copy-start | bytes 196612
  195.8 4.6 %copy-start.1 = (f32[2,24,512]{2,1,0:T(8,128)S(1)}, f32[2,24,512]{2,1,0:T(8,128)}, u32[]{:S(2)}) copy-start(f32[2,24,512]{2,1,0:T(8,128)} %param.27) | copy-start | bytes 294916
  195.8 4.6 %copy-start.6 = (f32[2,24,512]{2,1,0:T(8,128)S(1)}, f32[2,24,512]{2,1,0:T(8,128)}, u32[]{:S(2)}) copy-start(f32[2,24,512]{2,1,0:T(8,128)} %param.32) | copy-start | bytes 294916
  195.8 4.6 %copy-start.7 = (f32[2,24,512]{2,1,0:T(8,128)S(1)}, f32[2,24,512]{2,1,0:T(8,128)}, u32[]{:S(2)}) copy-start(f32[2,24,512]{2,1,0:T(8,128)} %param.37) | copy-start | bytes 294916

commit v3 on v0

v3 whole, which is shorter than its diff:
```python
import functools

import jax
import jax.numpy as jnp
from jax import lax
from jax.experimental import pallas as pl
from jax.experimental.pallas import tpu as pltpu
from jax.sharding import PartitionSpec as P

NORM_EPS = 1e-5
LEARN_RATE = 1e-3
BETA_ONE = 0.9
BETA_TWO = 0.95
ADAM_EPS = 1e-8
DECAY = 0.1
STEP = 10

MESH_ID = pl.DeviceIdType.MESH
ORDERS = ((0, 1, 2), (1, 2, 0), (2, 0, 1))
RING = 4
HOPS = (1, -1, 2)


class Place:
    def __init__(self):
        chip = lax.axis_index('dp')
        self.core = lax.axis_index('sp')
        self.at = (lax.rem(chip // 16, 4), lax.rem(chip // 4, 4), lax.rem(chip, 4))

    def step(self, dim, delta):
        return lax.rem(self.at[dim] + (delta + RING), RING)

    def chip(self, dim, delta):
        pos = list(self.at)
        pos[dim] = self.step(dim, delta)
        return {'dp': pos[0] * 16 + pos[1] * 4 + pos[2]}

    def partner(self):
        return {'sp': 1 - self.core}

    def barrier(self, ring=True):
        sem = pltpu.get_barrier_semaphore()
        peers = [self.partner()]
        if ring:
            peers += [self.chip(dim, delta) for dim in range(3) for delta in HOPS]
        for peer in peers:
            pl.semaphore_signal(sem, inc=1, device_id=peer, device_id_type=MESH_ID)
        pl.semaphore_wait(sem, len(peers))


class Wire:
    def __init__(self, send_sem, recv_sem):
        self.sems = (send_sem, recv_sem)
        self.slots = {}
        self.parts = {}

    def describe(self, key):
        source, target, where = self.parts[key]
        slot = self.slots.setdefault(key, len(self.slots))
        return pltpu.make_async_remote_copy(src_ref=source(), dst_ref=target(), send_sem=self.sems[0].at[slot], recv_sem=self.sems[1].at[slot], device_id=where(), device_id_type=MESH_ID)

    def start(self, key, source, target, where):
        self.parts[key] = (source, target, where)
        self.describe(key).start()

    def wait_recv(self, key):
        self.describe(key).wait_recv()

    def finish(self):
        for key in list(self.parts):
            self.describe(key).wait_send()


def split_groups(count):
    base, extra = divmod(count, 3)
    sizes = [base + (1 if g < extra else 0) for g in range(3)]
    starts = [sum(sizes[:g]) for g in range(3)]
    return list(zip(starts, sizes))


class Gather:
    def __init__(self, name, place, wire, src_ref, grid_ref):
        self.name, self.place, self.wire = name, place, wire
        self.src, self.grid = src_ref, grid_ref
        self.half = src_ref.shape[0] // 2
        self.first = place.core * self.half
        self.groups = split_groups(self.half)
        self.shared = []

    def region(self, g, phase, delta, side=None):
        order = ORDERS[g]
        start, size = self.groups[g]
        index = list(self.place.at)
        for q in range(phase):
            index[order[q]] = pl.ds(0, RING)
        index[order[phase]] = self.place.step(order[phase], delta)
        if side is not None:
            index[order[0]] = pl.ds(2 * side, 2)
        return self.grid.at[index[0], index[1], index[2], pl.ds(self.first + start, size)]

    def send(self, g, phase, delta, toward, tag, side=None):
        dim = ORDERS[g][phase]
        piece = functools.partial(self.region, g, phase, delta, side)
        origin = piece
        if phase == 0:
            start, size = self.groups[g]
            origin = lambda: self.src.at[pl.ds(self.first + start, size)]
        self.wire.start((self.name, g, phase, tag), origin, piece, lambda: self.place.chip(dim, toward))

    def share(self, g, phase, delta):
        key = (self.name, g, phase, 'share', delta)
        self.shared.append(key)
        piece = functools.partial(self.region, g, phase, delta)
        self.wire.start(key, piece, piece, self.place.partner)

    def begin(self, phase):
        for g in range(3):
            for toward in (HOPS if phase < 2 else (1, -1)):
                self.send(g, phase, 0, toward, toward)

    def arrived(self, g, phase, tag):
        self.wire.wait_recv((self.name, g, phase, tag))

    def stage(self, number):
        if number == 0:
            self.begin(0)
        elif number in (1, 2):
            for g in range(3):
                for toward in HOPS:
                    self.arrived(g, number - 1, toward)
            self.begin(number)
            for g in range(3):
                for toward in HOPS:
                    self.share(g, number - 1, -toward)
        elif number == 3:
            for g in range(3):
                self.arrived(g, 2, 1)
                self.send(g, 2, -1, 1, 'on_right', 0)
                self.arrived(g, 2, -1)
                self.send(g, 2, 1, -1, 'on_left', 1)
            for g in range(3):
                self.share(g, 2, -1)
                self.share(g, 2, 1)
        elif number == 4:
            for g in range(3):
                self.arrived(g, 2, 'on_right')
                self.arrived(g, 2, 'on_left')
                self.share(g, 2, 2)
        else:
            for key in self.shared:
                self.wire.wait_recv(key)


GATHER_COPIES = 3 * (3 + 3 + 4 + 3 + 3 + 3)


class Reduce:
    def __init__(self, name, place, wire, sources, own, theirs, boxes, out_ref, out_first, load_sem=None):
        self.name, self.place, self.wire = name, place, wire
        self.sources, self.own, self.theirs, self.boxes = sources, own, theirs, boxes
        self.out, self.out_first, self.load_sem = out_ref, out_first, load_sem
        self.count = own.shape[3]
        self.groups = split_groups(self.count)
        self.turns = (2, 1, -1, 0)

    def index_of(self, g, phase, delta, side=None):
        order = ORDERS[g]
        index = [pl.ds(0, RING)] * 3
        for q in range(phase):
            index[order[q]] = self.place.at[order[q]]
        index[order[phase]] = self.place.step(order[phase], delta)
        if side is not None:
            index[order[phase + 1]] = pl.ds(2 * side, 2)
        return index

    def kept(self, ref, g, phase, delta, side=None):
        index = self.index_of(g, phase, delta, side)
        return ref.at[index[0], index[1], index[2], pl.ds(*self.groups[g])]

    def pieces(self, g, delta, core):
        index = self.index_of(g, 0, delta)
        lo, n = self.groups[g]
        begin = 0
        out = []
        for ref, first, count in self.sources:
            part = count // 2
            start, stop = max(lo, begin), min(lo + n, begin + part)
            if start < stop:
                out.append((ref.at[index[0], index[1], index[2], pl.ds(first + core * part + start - begin, stop - start)], start, stop - start))
            begin += part
        return out

    def slot(self, ref, g, delta, start, count):
        index = self.index_of(g, 0, delta)
        return ref.at[index[0], index[1], index[2], pl.ds(start, count)]

    def loads(self):
        out = []
        for delta in self.turns:
            for g in range(3):
                for ref, start, count in self.pieces(g, delta, self.place.core):
                    out.append((delta, g, functools.partial(pltpu.make_async_copy, ref, self.slot(self.own, g, delta, start, count), self.load_sem.at[len(out)])))
        return out

    def ready(self, g, delta):
        here = self.pieces(g, delta, self.place.core)
        if self.load_sem is not None:
            for turn, group, load in self.loads():
                if turn == delta and group == g:
                    load().wait()
        for n, (ref, start, count) in enumerate(here):
            self.wire.wait_recv((self.name, 'swap', g, delta, n))
            target = self.slot(self.own, g, delta, start, count)
            mine = target if self.load_sem is not None else ref
            target[...] = mine[...] + self.slot(self.theirs, g, delta, start, count)[...]

    def box(self, g, phase, number):
        return self.boxes[g * 3 + phase].at[number]

    def send(self, g, phase, tag, delta, side, number, toward):
        dim = ORDERS[g][phase]
        self.wire.start((self.name, g, phase, tag), functools.partial(self.kept, self.own, g, phase, delta, side), functools.partial(self.box, g, phase, number), lambda: self.place.chip(dim, toward))

    def absorb(self, g, phase, tag, delta, side, number):
        self.wire.wait_recv((self.name, g, phase, tag))
        target = self.kept(self.own, g, phase, delta, side)
        target[...] = target[...] + self.box(g, phase, number)[...]

    def far(self, g, phase):
        self.send(g, phase, 'far_right', 2, 0, 0, 1)
        self.send(g, phase, 'far_left', 2, 1, 2, -1)

    def near(self, g, phase):
        self.send(g, phase, 'near_right', 1, 1, 1, 1)
        self.send(g, phase, 'near_left', -1, 0, 3, -1)

    def onward(self, g, phase):
        self.absorb(g, phase, 'far_right', 1, 0, 0)
        self.send(g, phase, 'sum_right', 1, 0, 4, 1)
        self.absorb(g, phase, 'far_left', -1, 1, 2)
        self.send(g, phase, 'sum_left', -1, 1, 5, -1)

    def settle(self, g, phase):
        for tag, number, side in (('near_left', 3, 0), ('near_right', 1, 1), ('sum_right', 4, 0), ('sum_left', 5, 1)):
            self.absorb(g, phase, tag, 0, side, number)

    def stage(self, number):
        if number == 0:
            if self.load_sem is not None:
                for _, _, load in self.loads():
                    load().start()
            for delta in self.turns:
                for g in range(3):
                    for n, (_, start, count) in enumerate(self.pieces(g, delta, 1 - self.place.core)):
                        self.wire.start((self.name, 'swap', g, delta, n), lambda g=g, delta=delta, n=n: self.pieces(g, delta, 1 - self.place.core)[n][0], functools.partial(self.slot, self.theirs, g, delta, start, count), self.place.partner)
        elif number == 1:
            for g in range(3):
                self.ready(g, 2)
                self.far(g, 0)
            for g in range(3):
                self.ready(g, 1)
                self.ready(g, -1)
                self.near(g, 0)
        elif number == 2:
            for g in range(3):
                self.onward(g, 0)
            for g in range(3):
                self.ready(g, 0)
        elif number == 3:
            for g in range(3):
                self.settle(g, 0)
                self.far(g, 1)
                self.near(g, 1)
        elif number == 4:
            for g in range(3):
                self.onward(g, 1)
        elif number == 5:
            for g in range(3):
                self.settle(g, 1)
                for n, toward in enumerate(HOPS):
                    self.send(g, 2, toward, toward, None, n, toward)
        elif number == 6:
            for g in range(3):
                for n, toward in enumerate(HOPS):
                    self.absorb(g, 2, toward, 0, None, n)
            span = lambda: self.out.at[self.place.core, pl.ds(self.out_first, self.count)]
            span()[...] = self.own[self.place.at[0], self.place.at[1], self.place.at[2]]
            self.wire.start((self.name, 'result'), span, span, self.place.partner)
        else:
            self.wire.wait_recv((self.name, 'result'))


def box_shapes(count):
    out = []
    for g, (_, size) in enumerate(split_groups(count)):
        order = ORDERS[g]
        dims = {dim: RING for dim in range(3) if dim != order[0]}
        dims[order[1]] = 2
        out.append((6,) + tuple(dims[dim] for dim in sorted(dims)) + (size, 8, 128))
        out.append((6, 2, size, 8, 128))
        out.append((3, size, 8, 128))
    return out


def reduce_scratch(count):
    grid = pltpu.VMEM((RING, RING, RING, count, 8, 128), jnp.float32)
    return [grid, grid] + [pltpu.VMEM(shape, jnp.float32) for shape in box_shapes(count)]


TILE = 256
NODE_TILE = TILE // 8
BF16 = jnp.bfloat16
F32 = jnp.float32


def dot(left, right, left_dim=1, right_dim=0):
    return lax.dot_general(left, right, (((left_dim,), (right_dim,)), ((), ())), preferred_element_type=F32)


def split_three(values):
    high = values.astype(BF16)
    rest = values - high.astype(F32)
    mid = rest.astype(BF16)
    low = (rest - mid.astype(F32)).astype(BF16)
    return high, mid, low


def dot_wide(values, right, right_dim=0):
    high, mid, low = split_three(values)
    return dot(high, right, 1, right_dim) + dot(mid, right, 1, right_dim) + dot(low, right, 1, right_dim)


def dot_wide_rows(left, values):
    high, mid, low = split_three(values)
    return dot(left, high, 0, 0) + dot(left, mid, 0, 0) + dot(left, low, 0, 0)


def norm_stats(out_b):
    values = out_b.astype(F32)
    centered = values - jnp.mean(values, axis=-1, keepdims=True)
    inv_std = lax.rsqrt(jnp.mean(centered * centered, axis=-1, keepdims=True) + NORM_EPS)
    return centered * inv_std, inv_std


def mlp_forward(pre_act, w_two, gain, bias):
    pre_b = pre_act.astype(BF16)
    hidden = jax.nn.silu(pre_b.astype(F32)).astype(BF16)
    out_b = dot(hidden, w_two).astype(BF16)
    normed, _ = norm_stats(out_b)
    return normed * gain + bias, pre_b, out_b


def mlp_cotangents(d_branch, pre_b, out_b, w_two, gain):
    normed, inv_std = norm_stats(out_b)
    d_norm = d_branch * gain
    d_out = (inv_std * (d_norm - jnp.mean(d_norm, axis=-1, keepdims=True) - normed * jnp.mean(d_norm * normed, axis=-1, keepdims=True))).astype(BF16)
    d_act = dot(d_out, w_two, 1, 1).astype(BF16)
    pre_f = pre_b.astype(F32)
    gate = jax.nn.sigmoid(pre_f)
    hidden = (pre_f * gate).astype(BF16)
    d_pre = (d_act.astype(F32) * gate * (1.0 + pre_f * (1.0 - gate))).astype(BF16)
    d_gain = (d_branch * normed).reshape(-1, 8, d_branch.shape[-1]).sum(axis=0)
    d_bias = d_branch.reshape(-1, 8, d_branch.shape[-1]).sum(axis=0)
    return d_out, hidden, d_pre, d_gain, d_bias


def receiver_pick(copies):
    rows = lax.broadcasted_iota(jnp.int32, (TILE, copies * NODE_TILE), 0)
    cols = lax.broadcasted_iota(jnp.int32, (TILE, copies * NODE_TILE), 1)
    return lax.shift_right_logical(rows, 3) == lax.bitwise_and(cols, NODE_TILE - 1)


def as_bf16(flags):
    return jnp.where(flags, 1.0, 0.0).astype(BF16)


def unpack_weights(grid, w_e1, w_e2, w_n1, w_n2, norms):
    def pair(p, carry):
        at = (p // 8, lax.rem(p // 2, 4))
        x = lax.rem(p, 2) * 2
        for k in range(4):
            lanes = pl.ds(128 * k, 128)
            for dev in range(2):
                w_e1[pl.ds(pl.multiple_of(48 * p + 32 * dev, 16), 16), lanes] = grid[at[0], at[1], x + dev, k]
                w_n1[pl.ds(pl.multiple_of(32 * p + 16 * dev, 16), 16), lanes] = grid[at[0], at[1], x + dev, 4 + k]
            for ref, first, tile, top in ((w_e1, 48 * p + 16, 8, 0), (w_e2, 16 * p, 8, 8), (w_n2, 16 * p, 12, 0)):
                even = grid[at[0], at[1], x, tile + k].astype(F32)[top:top + 8]
                odd = grid[at[0], at[1], x + 1, tile + k].astype(F32)[top:top + 8]
                ref[pl.ds(pl.multiple_of(first, 16), 16), lanes] = jnp.concatenate([even, odd], axis=0).astype(BF16)
        return carry
    lax.fori_loop(0, 32, pair, 0)
    for k in range(4):
        total = grid[k, 0, 0, 12].astype(F32)
        for d in range(1, 16):
            total = total + grid[k, d // 4, d % 4, 12].astype(F32)
        norms[:, 128 * k:128 * k + 128] = total[8:16]


def fill_columns(snd_rows, mask_rows, snd_col, mask_col):
    for rows, col in ((snd_rows, snd_col), (mask_rows, mask_col)):
        turned = rows[...].astype(F32).T
        for n in range(rows.shape[0]):
            col[128 * n:128 * n + 128, :] = turned[:, n:n + 1]


def edge_forward(layer_io, hook, edge_out, pre_out, out_out, sums_out, w_e1, w_e2, norms, recv_terms):
    node_all, node_own, edge_in, snd_col, mask_col = layer_io
    for part, term in enumerate(split_three(dot(node_own[...], w_e1[1024:1536]))):
        recv_terms[part] = term

    def tile(i, carry):
        rows = pl.ds(pl.multiple_of(i * TILE, TILE), TILE)
        nodes = pl.ds(pl.multiple_of(i * NODE_TILE, NODE_TILE), NODE_TILE)
        ids = lax.broadcasted_iota(jnp.int32, (TILE, 512), 1)
        sender = dot(as_bf16(snd_col[rows].astype(jnp.int32) == ids), node_all[...]).astype(BF16)
        recv = jnp.concatenate([recv_terms[0, nodes], recv_terms[1, nodes], recv_terms[2, nodes]], axis=0)
        edge = edge_in[rows]
        pre = dot(edge, w_e1[0:512]) + dot(sender, w_e1[512:1024]) + dot(as_bf16(receiver_pick(3)), recv)
        branch, pre_b, out_b = mlp_forward(pre, w_e2[...], norms[0:1], norms[1:2])
        edge_new = (edge.astype(F32) + branch).astype(BF16)
        pre_out[rows] = pre_b
        out_out[rows] = out_b
        if edge_out is not None:
            edge_out[rows] = edge_new
        picked = jnp.where(receiver_pick(1), mask_col[rows], 0.0).astype(BF16)
        sums_out[nodes] = dot(picked, edge_new, 0, 0).astype(BF16)
        hook(i)
        return carry
    lax.fori_loop(0, edge_in.shape[0] // TILE, tile, 0)


def node_forward(node_own, sums, w_n1, w_n2, norms):
    pre = dot(node_own[...], w_n1[0:512]) + dot(sums[...], w_n1[512:1024])
    return mlp_forward(pre, w_n2[...], norms[2:3], norms[3:4])


def store_grad(grad_ref, values, first_row, shard_rows, first_tile):
    for q in range(values.shape[0] // 8):
        place = first_row // 8 + q
        per = shard_rows // 8
        for k in range(4):
            dev = place // per
            grad_ref[dev // 16, dev // 4 % 4, dev % 4, first_tile + place % per * 4 + k] = values[8 * q:8 * q + 8, 128 * k:128 * k + 128]


def layer_back(layer_io, d_node_new, d_edge_new, pre_e, out_e, sums, pre_n, out_n, mats, norms, snd_rows, outs, scratch, after_nodes, hook, pass_on):
    node_all, node_own, edge_in, snd_col, mask_col = layer_io
    w_e1, w_e2, w_n1, w_n2 = mats
    grad_ref, norm_grad, d_edge, d_local, scattered = outs
    hidden_s, d_pre_s, d_out_s, d_sum_s, recv_s, gain_s = scratch
    d_out_n, hidden_n, d_pre_n, d_gain_n, d_bias_n = mlp_cotangents(d_node_new, pre_n, out_n, w_n2[...], norms[2:3])
    d_sum_s[...] = dot(d_pre_n, w_n1[512:1024], 1, 1).astype(BF16)
    d_local[...] = d_node_new + dot(d_pre_n, w_n1[0:512], 1, 1)
    store_grad(grad_ref, dot(hidden_n, d_out_n, 0, 0), 0, 8, 24)
    store_grad(grad_ref, dot(node_own[...], d_pre_n, 0, 0), 0, 16, 16)
    store_grad(grad_ref, dot(sums[...], d_pre_n, 0, 0), 512, 16, 16)
    after_nodes()
    gain_s[...] = jnp.zeros_like(gain_s)

    def tile(i, carry):
        rows = pl.ds(pl.multiple_of(i * TILE, TILE), TILE)
        nodes = pl.ds(pl.multiple_of(i * NODE_TILE, NODE_TILE), NODE_TILE)
        pick = receiver_pick(1)
        picked = jnp.where(pick, mask_col[rows], 0.0).astype(BF16)
        d_res = (d_edge_new[rows].astype(F32) + dot(picked, d_sum_s[nodes])).astype(BF16).astype(F32)
        d_out, hidden, d_pre, d_gain, d_bias = mlp_cotangents(d_res, pre_e[rows], out_e[rows], w_e2[...], norms[0:1])
        gain_s[0] = gain_s[0] + d_gain
        gain_s[1] = gain_s[1] + d_bias
        hidden_s[rows] = hidden
        d_out_s[rows] = d_out
        d_pre_s[rows] = d_pre
        d_edge[rows] = (d_res + dot(d_pre, w_e1[0:512], 1, 1)).astype(BF16)
        recv_s[nodes] = dot(as_bf16(pick), d_pre, 0, 0)
        hook(i)
        return carry
    lax.fori_loop(0, edge_in.shape[0] // TILE, tile, 0)
    store_grad(grad_ref, dot(hidden_s[...], d_out_s[...], 0, 0), 0, 8, 12)
    store_grad(grad_ref, dot(edge_in[...], d_pre_s[...], 0, 0), 0, 24, 0)
    snd_row = jnp.concatenate([snd_rows[n:n + 1] for n in range(snd_rows.shape[0])], axis=1)
    for block in range(4):
        ids = lax.broadcasted_iota(jnp.int32, (128, edge_in.shape[0]), 0) + 128 * block
        scattered[128 * block:128 * block + 128] = dot(as_bf16(snd_row == ids), d_pre_s[...])
    pass_on()
    store_grad(grad_ref, dot_wide_rows(node_all[...], scattered[...]), 512, 24, 0)
    store_grad(grad_ref, dot_wide_rows(node_own[...], recv_s[...]), 1024, 24, 0)
    d_local[...] = d_local[...] + dot_wide(recv_s[...], w_e1[1024:1536], 1)
    for part, (gain, bias) in enumerate(((gain_s[0], gain_s[1]), (d_gain_n, d_bias_n))):
        full = jnp.concatenate([gain.sum(axis=0, keepdims=True), bias.sum(axis=0, keepdims=True), jnp.zeros((6, 512), F32)], axis=0)
        for d in range(64):
            k = d // 16
            norm_grad[k, d // 4 % 4, d % 4, part] = full[:, 128 * k:128 * k + 128]


def half_of(ref, core):
    count = ref.shape[0] // 2
    return ref.at[pl.ds(pl.multiple_of(core * count, count), count)]


def no_hook(i):
    return None


def at_tile(plan):
    def hook(i):
        for tile, stages in plan.items():
            @pl.when(i == tile)
            def _():
                for plan_of, number in stages:
                    plan_of.stage(number)
    return hook


def forward_kernel(shard_low, shard_high, node_in, edge_in, snd_rows, mask_rows, node_all, node_all_one, edge_out, pre_e, out_e, sums, pre_n, out_n, *rest):
    mats = (rest[0:4], rest[5:9])
    norms = (rest[4], rest[9])
    recv_terms, grid_low, grid_high, snd_col, mask_col, send_sem, recv_sem = rest[10:]
    place = Place()
    wire = Wire(send_sem, recv_sem)
    low = Gather('low', place, wire, shard_low, grid_low)
    high = Gather('high', place, wire, shard_high, grid_high)
    node_own = half_of(node_all, place.core)
    grid_low[place.at[0], place.at[1], place.at[2]] = shard_low[...]
    grid_high[place.at[0], place.at[1], place.at[2]] = shard_high[...]
    node_own[...] = node_in[...]
    place.barrier()
    low.stage(0)
    high.stage(0)
    wire.start('node', lambda: node_in, lambda: half_of(node_all, place.core), place.partner)
    fill_columns(snd_rows, mask_rows, snd_col, mask_col)
    low.stage(1)
    high.stage(1)
    low.stage(2)
    low.stage(3)
    high.stage(2)
    low.stage(4)
    low.stage(5)
    unpack_weights(grid_low, *mats[0], norms[0])
    wire.wait_recv('node')
    w_e1, w_e2, w_n1, w_n2 = mats[0]
    hook = at_tile({1: [(high, 3)], 4: [(high, 4)]})
    edge_forward((node_all, node_own, edge_in, snd_col, mask_col), hook, edge_out, pre_e, out_e, sums, w_e1, w_e2, norms[0], recv_terms)
    branch, pre_b, out_b = node_forward(node_own, sums, w_n1, w_n2, norms[0])
    pre_n[...] = pre_b
    out_n[...] = out_b
    half_of(node_all_one, place.core)[...] = (node_own[...].astype(F32) + branch).astype(BF16)
    piece = lambda: half_of(node_all_one, place.core)
    wire.start('node_one', piece, piece, place.partner)
    high.stage(5)
    unpack_weights(grid_high, *mats[1], norms[1])
    wire.wait_recv('node_one')
    wire.finish()


def middle_kernel(node_all, edge_in, snd_rows, mask_rows, node_cot, edge_cot, w_e1, w_e2, w_n1, w_n2, norms, grad_ref, norm_grad, d_edge, d_local, scattered, returned, pre_e, out_e, sums, recv_terms, snd_col, mask_col, *rest):
    scratch = rest[:-2]
    place = Place()
    wire = Wire(*rest[-2:])
    place.barrier(ring=False)
    node_own = half_of(node_all, place.core)
    fill_columns(snd_rows, mask_rows, snd_col, mask_col)
    layer_io = (node_all, node_own, edge_in, snd_col, mask_col)
    edge_forward(layer_io, no_hook, None, pre_e, out_e, sums, w_e1, w_e2, norms, recv_terms)
    _, pre_n, out_n = node_forward(node_own, sums, w_n1, w_n2, norms)

    def pass_on():
        wire.start('scattered', lambda: half_of(scattered, 1 - place.core), lambda: returned, place.partner)
    layer_back(layer_io, node_cot[...].astype(F32), edge_cot, pre_e, out_e, sums, pre_n, out_n, (w_e1, w_e2, w_n1, w_n2), norms, snd_rows, (grad_ref, norm_grad, d_edge, d_local, scattered), scratch, lambda: None, no_hook, pass_on)
    wire.wait_recv('scattered')
    wire.finish()


def node_cotangent(d_local, scattered, returned, w_above, core):
    return (d_local[...] + dot_wide(half_of(scattered, core)[...] + returned[...], w_above[512:1024], 1)).astype(BF16)


def back_kernel(node_all, edge_in, snd_rows, mask_rows, d_local_above, scattered_above, returned_above, w_above, d_edge_new, pre_e, out_e, sums, pre_n, out_n, w_e1, w_e2, w_n1, w_n2, norms, grad_high, norm_high, grad_node, d_edge, total, grad_ref, norm_grad, d_local, scattered, returned, mask_col, snd_col, *rest):
    scratch, rest = rest[:6], rest[6:]
    load_sem, send_sem, recv_sem = rest[-3:]
    place = Place()
    wire = Wire(send_sem, recv_sem)
    plans = []
    for n, (name, sources, count, first, sem) in enumerate((
            ('high', [(grad_high, 0, 28), (norm_high, 0, 2)], 15, 0, load_sem),
            ('node', [(grad_ref, 16, 12)], 6, 15, None),
            ('edge', [(grad_ref, 0, 16), (norm_grad, 0, 2)], 9, 21, None))):
        own, theirs = rest[11 * n:11 * n + 2]
        plans.append(Reduce(name, place, wire, sources, own, theirs, rest[11 * n + 2:11 * n + 11], total, first, sem))
    high, node, edge = plans
    place.barrier()
    high.stage(0)
    node_own = half_of(node_all, place.core)
    fill_columns(snd_rows, mask_rows, snd_col, mask_col)
    layer_io = (node_all, node_own, edge_in, snd_col, mask_col)
    d_node = node_cotangent(d_local_above, scattered_above, returned_above, w_above, place.core).astype(F32)

    def after_nodes():
        node.stage(0)
        high.stage(1)

    def pass_on():
        wire.start('scattered', lambda: half_of(scattered, 1 - place.core), lambda: returned, place.partner)
    hook = at_tile({0: [(node, 1)], 3: [(high, 2)], 4: [(node, 2)], 6: [(high, 3)]})
    layer_back(layer_io, d_node, d_edge_new, pre_e, out_e, sums, pre_n[...], out_n[...], (w_e1, w_e2, w_n1, w_n2), norms, snd_rows, (grad_ref, norm_grad, d_edge, d_local, scattered), scratch, after_nodes, hook, pass_on)
    edge.stage(0)
    node.stage(3)
    edge.stage(1)
    high.stage(4)
    node.stage(4)
    wire.wait_recv('scattered')
    grad_node[...] = node_cotangent(d_local, scattered, returned, w_e1, place.core)
    high.stage(5)
    node.stage(5)
    edge.stage(2)
    edge.stage(3)
    high.stage(6)
    node.stage(6)
    for number in (4, 5, 6):
        edge.stage(number)
    for plan in (high, node, edge):
        plan.stage(7)
    wire.finish()


def vmem_call(kernel, name, inputs, outputs, scratch, flops, collective_id, copies, in_hbm=()):
    spec = pl.BlockSpec(memory_space=pltpu.VMEM)
    anywhere = pl.BlockSpec(memory_space=pl.ANY)
    return pl.pallas_call(
        kernel,
        out_shape=[jax.ShapeDtypeStruct(shape, dtype) for shape, dtype in outputs],
        in_specs=[spec] * len(inputs) + [anywhere] * len(in_hbm),
        out_specs=[spec] * len(outputs),
        scratch_shapes=[pltpu.VMEM(*entry) if isinstance(entry, tuple) else entry for entry in scratch] + [pltpu.SemaphoreType.DMA((copies,))] * 2,
        compiler_params=pltpu.CompilerParams(collective_id=collective_id, has_side_effects=True, vmem_limit_bytes=63 * 2 ** 20),
        cost_estimate=pl.CostEstimate(flops=flops, bytes_accessed=20 * 2 ** 20, transcendentals=0),
        name=name,
    )(*inputs, *in_hbm)


MAT_SHAPES = [((1536, 512), BF16), ((512, 512), BF16), ((1024, 512), BF16), ((512, 512), BF16), ((8, 512), F32)]
GRADS = [((4, 4, 4, 28, 8, 128), F32), ((4, 4, 4, 2, 8, 128), F32)]
BACK_SCRATCH = [((2048, 512), BF16)] * 3 + [((256, 512), BF16), ((256, 512), F32), ((2, 8, 512), F32)]
EDGE = ((2048, 512), BF16)
NODE = ((256, 512), BF16)
NODES = ((512, 512), BF16)
NODE_F32 = ((256, 512), F32)
NODES_F32 = ((512, 512), F32)
COLUMN = ((2048, 1), F32)
RECV_TERMS = ((3, 256, 512), BF16)


def adamw_update(master, grad_sum, moment_one, moment_two):
    corr_one = 1.0 - BETA_ONE ** STEP
    corr_two = 1.0 - BETA_TWO ** STEP
    one_new = BETA_ONE * moment_one + (1.0 - BETA_ONE) * grad_sum
    two_new = BETA_TWO * moment_two + (1.0 - BETA_TWO) * grad_sum * grad_sum
    direction = (one_new / corr_one) / (jnp.sqrt(two_new / corr_two) + ADAM_EPS)
    return master - LEARN_RATE * (direction + DECAY * master), one_new, two_new


def update_all(masters, moments_one, moments_two, layer_grads):
    new_master = []
    new_one = []
    new_two = []
    for slot in range(len(masters)):
        grad_sum = jnp.stack([per_layer[slot] for per_layer in layer_grads], axis=0)
        master_new, one_new, two_new = adamw_update(masters[slot], grad_sum, moments_one[slot], moments_two[slot])
        new_master.append(master_new)
        new_one.append(one_new)
        new_two.append(two_new)
    return tuple(new_master) + tuple(new_one) + tuple(new_two)


def rows_to_tiles(values, sub):
    rows = values.shape[0]
    return values.reshape(rows // sub, sub, 4, 128).transpose(0, 2, 1, 3).reshape(rows // sub * 4, sub, 128)


def tiles_to_rows(tiles):
    count, sub = tiles.shape[:2]
    return tiles.reshape(count // 4, 4, sub, 128).transpose(0, 2, 1, 3).reshape(count // 4 * sub, 512)


def pack_shards(masters):
    chip = lax.axis_index('dp')
    odd = lax.rem(chip, 2) == 1
    edge_one, edge_two, node_one, node_two, norm = [master.astype(BF16) for master in masters]
    main = jnp.where(odd, edge_one[:, 8:24], edge_one[:, 0:16])
    tail = jnp.where(odd, edge_one[:, 0:8], edge_one[:, 16:24])
    wide = jnp.tile(norm, (1, 1, 16))
    lanes = lax.broadcasted_iota(jnp.int32, wide.shape, 2) // 8
    norms = jnp.pad(jnp.where(lanes == lax.rem(chip, 16), wide, 0), ((0, 0), (0, 4), (0, 384)))
    return [rows_to_tiles(jnp.concatenate([main[n], node_one[n], tail[n], edge_two[n], node_two[n], norms[n]], axis=0), 16) for n in range(2)]


def unpack_grads(total):
    chip = lax.axis_index('dp')
    tiles_high = jnp.concatenate([total[0, 0:14], total[1, 0:14]], axis=0)
    tiles_low = jnp.concatenate([total[0, 21:29], total[1, 21:29], total[0, 15:21], total[1, 15:21]], axis=0)
    out = []
    for tiles, norm_at in ((tiles_low, 29), (tiles_high, 14)):
        rows = tiles_to_rows(tiles)
        norm = lax.dynamic_slice(total[:, norm_at, 0:2], (0, 0, lax.rem(chip, 16) * 8), (2, 2, 8)).reshape(4, 8)
        mats = []
        first = 0
        for size in (24, 8, 16, 8):
            mats.append(rows[first:first + size])
            first += size
        out.append(tuple(mats) + (norm,))
    return out


def solution(mesh):
    lat_spec = P('dp', 'sp', None)
    edge_spec = P('sp')
    mat_spec = P(None, 'dp', None)
    norm_spec = P(None, None, 'dp')
    param_specs = (mat_spec, mat_spec, mat_spec, mat_spec, norm_spec)

    def train_step(node_lat, edge_lat, senders, edge_mask, node_cot, edge_cot, w_edge1, w_edge2, w_node1, w_node2, norm_par, mom_edge1, mom_edge2, mom_node1, mom_node2, mom_norm, vel_edge1, vel_edge2, vel_node1, vel_node2, vel_norm):
        masters = (w_edge1, w_edge2, w_node1, w_node2, norm_par)
        moments_one = (mom_edge1, mom_edge2, mom_node1, mom_node2, mom_norm)
        moments_two = (vel_edge1, vel_edge2, vel_node1, vel_node2, vel_norm)
        snd_rows = senders.reshape(-1, 128)
        mask_rows = edge_mask.reshape(-1, 128)
        shard_low, shard_high = pack_shards(masters)
        grid = pltpu.VMEM((RING, RING, RING) + shard_low.shape, BF16)
        outs = vmem_call(forward_kernel, 'gather_forward', (shard_low, shard_high, node_lat[0], edge_lat[0], snd_rows, mask_rows), [NODES, NODES, EDGE, EDGE, EDGE, NODE, NODE, NODE] + MAT_SHAPES + MAT_SHAPES, [RECV_TERMS, grid, grid, COLUMN, COLUMN], 5 * 10 ** 9, 1, 2 * GATHER_COPIES + 2)
        node_all, node_all_one, edge_one, pre_e, out_e, sums, pre_n, out_n = outs[:8]
        mats_low = outs[8:13]
        mats_high = outs[13:18]
        grad_high, norm_high, d_edge_one, d_local_one, scattered_one, returned_one = vmem_call(middle_kernel, 'forward_back_high', (node_all_one, edge_one, snd_rows, mask_rows, node_cot[0], edge_cot[0]) + tuple(mats_high), GRADS + [EDGE, NODE_F32, NODES_F32, NODE_F32], [EDGE, EDGE, NODE, RECV_TERMS, COLUMN, COLUMN] + BACK_SCRATCH, 13 * 10 ** 9, 2, 1)
        reduce_bufs = reduce_scratch(15) + reduce_scratch(6) + reduce_scratch(9)
        inputs = (node_all, edge_lat[0], snd_rows, mask_rows, d_local_one, scattered_one, returned_one, mats_high[0], d_edge_one, pre_e, out_e, sums, pre_n, out_n) + tuple(mats_low)
        grad_node, d_edge_zero, total = vmem_call(back_kernel, 'back_low_reduce', inputs, [NODE, EDGE, ((2, 30, 8, 128), F32)], GRADS + [NODE_F32, NODES_F32, NODE_F32, COLUMN, COLUMN] + BACK_SCRATCH + reduce_bufs + [pltpu.SemaphoreType.DMA((16,))], 8 * 10 ** 9, 3, 200, (grad_high, norm_high))
        new_state = update_all(masters, moments_one, moments_two, unpack_grads(total))
        return new_state + (grad_node[None], d_edge_zero[None])

    return jax.shard_map(train_step, mesh=mesh, in_specs=(lat_spec, lat_spec, edge_spec, edge_spec, lat_spec, lat_spec) + param_specs + param_specs + param_specs, out_specs=param_specs + param_specs + param_specs + (lat_spec, lat_spec), check_vma=False)
```

time: 3840 us -> 170 us (0.04)
  waiting for transfers between devices: 2210 us -> 0 us
  blocking collectives: 1340 us -> 0 us
  Pallas kernels: 0 us -> 154 us
  other arithmetic: 109 us -> 7.4 us
  matrix products: 84.4 us -> 0 us
  local copies, waits for them, and re-layouts: 64.2 us -> 7.02 us
    reduce_scatter x10 -> x0, waiting for transfers between devices: 2190 us -> none  [the longest x8 2170 us: reduce_grads(): lax.psum_scatter(grad_full, 'dp', scatter_dimension=0, tiled=True)]
    all_gather x8 -> x0, blocking collectives: 1050 us -> none  [the longest x4 582 us: gather_weights(): lax.all_gather(master[layer_idx].astype(jnp.bfloat16), 'dp', axis=0, tile...]
    unnamed x1 -> x0, blocking collectives: 292 us -> none
    pallas_call x0 -> x3, Pallas kernels: none -> 154 us  [vmem_call(): pl.pallas_call(kernel, out_shape=[jax.ShapeDtypeStruct(shape, dtype) for...]
    dot_general x38 -> x0, matrix products: 84.4 us -> none  [the longest x36 81.5 us: contract(): lax.dot_general(left_op, right_op, ((left_dims, right_dims), ((), ())), p...]
  transfers between devices with their start and end apart: 15 -> 0, of which waited for: 9 -> 0; matrix products, arithmetic and copies ran while one was open for 5% -> 0% of each run, Pallas kernels for 0% -> 0%
where the time goes in v3:
time: 170 us
  Pallas kernels  154 us (91%)
  other arithmetic  7.4 us (4%)
  local copies, waits for them, and re-layouts  7.02 us (4%)
    pallas_call x3, Pallas kernels, vmem_call(): pl.pallas_call(kernel, out_shape=[jax.ShapeDtypeStruct(shape, dtype) for...  154 us
    convert_element_type x5, other arithmetic, pack_shards(): master.astype(BF16)  3.96 us

profile of v3, /device:TPU:1, one launch (start us, length us, event | category | flops | bytes accessed | tf_op | source)
XLA Modules:
  0.0 169.7 jit_solution(10570772705640806631)
XLA Ops:
  0.7 0.7 convert_element_type.23
  1.4 0.8 convert_element_type.21
  2.1 0.8 convert_element_type.22
  2.9 0.1 tile.10
  3.0 0.8 convert_element_type.20
  3.9 0.9 convert_element_type.19
  4.9 0.6 copy.41
  5.6 0.6 copy.40
  6.2 52.5 %gather_forward.1 = (bf16[512,512]{1,0:T(8,128)(2,1)}, bf16[512,512]{1,0:T(8,128)(2,1)}, bf16[2048,512]{1,0:T(8,128)(2,1)}, bf16[2048,512]{1,0:T(8,128)(2,1)}, b...) custom-call(bf16[16,16,128]{2,1,0:T(8,128)(2,1)} %bitcast.109, ...), custom_call_target="tpu_custom_call" | custom-call | flops 5000000000 | bytes 20971520 | tf_op jit(solution)/shard_map/gather_forward/pallas_call | solution.py:627
  58.7 35.6 %forward_back_high.1 = (f32[4,4,4,28,8,128]{5,4,3,2,1,0:T(8,128)}, f32[4,4,4,2,8,128]{5,4,3,2,1,0:T(8,128)}, bf16[2048,512]{1,0:T(8,128)(2,1)}, f32[256,512]{1,0...) custom-call(bf16[512,512]{1,0:T(8,128)(2,1)} %get-tuple-element.45.node_all, ...), custom_call_target="tpu_custom_call" | custom-call | flops 12999999488 | bytes 20971520 | tf_op jit(solution)/shard_map/forward_back_high/pallas_call | solution.py:627
  94.3 0.0 copy-start.14
  94.4 0.0 copy-start.15
  94.4 0.0 copy-start.16
  94.4 0.0 copy-start.4
  94.4 0.0 copy-start.10
  94.4 0.0 copy-start.11
  94.4 0.0 copy-start.5
  94.4 0.0 copy-start.12
  94.4 0.0 copy-start.13
  94.4 0.0 copy-start.2
  94.5 0.0 copy-start.8
  94.5 0.0 copy-start.9
  94.5 0.0 copy-start.6
  94.5 0.0 copy-start.7
  94.5 66.1 %back_low_reduce.1 = (bf16[256,512]{1,0:T(8,128)(2,1)}, bf16[2048,512]{1,0:T(8,128)(2,1)}, f32[2,30,8,128]{3,2,1,0:T(8,128)}) custom-call(bf16[512,512]{1,0:T(8,128)(2,1)} %get-tuple-element.44.node_all, bf16[2048,512]{1,0:T(8,128)(2,1)} %bitcast.114, s32[16,128]{1,0:T(8,128)} %bitcast.119, s32[16,128]{1,0:T(8,128)} %bitcast.122, ...), custom_call_target="tpu_custom_call" | custom-call | flops 8000000000 | bytes 20971520 | tf_op jit(solution)/shard_map/back_low_reduce/pallas_call | solution.py:627
  160.6 0.0 copy-start.1
  160.6 0.0 copy-start.3
  160.6 0.0 copy-start
  160.6 0.9 fusion.13
  161.5 0.1 constant_dynamic-slice_fusion.1
  161.6 0.1 constant_dynamic-slice_fusion
  161.7 0.0 copy-done.14
  161.7 0.0 copy-done.15
  161.7 0.0 copy-done.16
  161.7 0.6 multiply_subtract_fusion.4
  162.3 0.8 slice_bitcast_fusion.9
  163.1 0.8 slice_bitcast_fusion.7
  163.8 0.9 slice_bitcast_fusion.1
  164.8 0.0 copy-done.4
  164.8 0.7 multiply_subtract_fusion.2
  165.5 0.0 copy-done.12
  165.5 0.7 multiply_subtract_fusion.3
  166.2 0.0 copy-done.2
  166.2 0.7 multiply_subtract_fusion.1
  166.9 0.0 copy-done.6
  166.9 0.8 multiply_subtract_fusion
  167.6 0.7 copy.54
  168.3 1.3 copy.55
  (32 shorter events, 0.2 us)
Async XLA Ops:
  94.3 67.3 %copy-start.14 = (f32[2,4,8]{2,1,0:T(4,128)S(1)}, f32[2,4,8]{2,1,0:T(4,128)}, u32[]{:S(2)}) copy-start(f32[2,4,8]{2,1,0:T(4,128)} %param.31) | copy-start | bytes 772
  94.4 67.3 %copy-start.15 = (f32[2,4,8]{2,1,0:T(4,128)S(1)}, f32[2,4,8]{2,1,0:T(4,128)}, u32[]{:S(2)}) copy-start(f32[2,4,8]{2,1,0:T(4,128)} %param.36) | copy-start | bytes 772
  94.4 67.3 %copy-start.16 = (f32[2,4,8]{2,1,0:T(4,128)S(1)}, f32[2,4,8]{2,1,0:T(4,128)}, u32[]{:S(2)}) copy-start(f32[2,4,8]{2,1,0:T(4,128)} %param.41) | copy-start | bytes 772
  94.4 70.4 %copy-start.4 = (f32[2,8,512]{2,1,0:T(8,128)S(1)}, f32[2,8,512]{2,1,0:T(8,128)}, u32[]{:S(2)}) copy-start(f32[2,8,512]{2,1,0:T(8,128)} %param.30) | copy-start | bytes 98308
  94.4 70.4 %copy-start.10 = (f32[2,8,512]{2,1,0:T(8,128)S(1)}, f32[2,8,512]{2,1,0:T(8,128)}, u32[]{:S(2)}) copy-start(f32[2,8,512]{2,1,0:T(8,128)} %param.35) | copy-start | bytes 98308
  94.4 70.4 %copy-start.11 = (f32[2,8,512]{2,1,0:T(8,128)S(1)}, f32[2,8,512]{2,1,0:T(8,128)}, u32[]{:S(2)}) copy-start(f32[2,8,512]{2,1,0:T(8,128)} %param.40) | copy-start | bytes 98308
  94.4 71.1 %copy-start.5 = (f32[2,8,512]{2,1,0:T(8,128)S(1)}, f32[2,8,512]{2,1,0:T(8,128)}, u32[]{:S(2)}) copy-start(f32[2,8,512]{2,1,0:T(8,128)} %param.28) | copy-start | bytes 98308
  94.4 71.1 %copy-start.12 = (f32[2,8,512]{2,1,0:T(8,128)S(1)}, f32[2,8,512]{2,1,0:T(8,128)}, u32[]{:S(2)}) copy-start(f32[2,8,512]{2,1,0:T(8,128)} %param.33) | copy-start | bytes 98308
  94.4 71.1 %copy-start.13 = (f32[2,8,512]{2,1,0:T(8,128)S(1)}, f32[2,8,512]{2,1,0:T(8,128)}, u32[]{:S(2)}) copy-start(f32[2,8,512]{2,1,0:T(8,128)} %param.38) | copy-start | bytes 98308
  94.4 71.7 %copy-start.2 = (f32[2,16,512]{2,1,0:T(8,128)S(1)}, f32[2,16,512]{2,1,0:T(8,128)}, u32[]{:S(2)}) copy-start(f32[2,16,512]{2,1,0:T(8,128)} %param.29) | copy-start | bytes 196612
  94.5 71.7 %copy-start.8 = (f32[2,16,512]{2,1,0:T(8,128)S(1)}, f32[2,16,512]{2,1,0:T(8,128)}, u32[]{:S(2)}) copy-start(f32[2,16,512]{2,1,0:T(8,128)} %param.34) | copy-start | bytes 196612
  94.5 71.7 %copy-start.9 = (f32[2,16,512]{2,1,0:T(8,128)S(1)}, f32[2,16,512]{2,1,0:T(8,128)}, u32[]{:S(2)}) copy-start(f32[2,16,512]{2,1,0:T(8,128)} %param.39) | copy-start | bytes 196612
  94.5 72.4 %copy-start.6 = (f32[2,24,512]{2,1,0:T(8,128)S(1)}, f32[2,24,512]{2,1,0:T(8,128)}, u32[]{:S(2)}) copy-start(f32[2,24,512]{2,1,0:T(8,128)} %param.32) | copy-start | bytes 294916
  94.5 72.4 %copy-start.7 = (f32[2,24,512]{2,1,0:T(8,128)S(1)}, f32[2,24,512]{2,1,0:T(8,128)}, u32[]{:S(2)}) copy-start(f32[2,24,512]{2,1,0:T(8,128)} %param.37) | copy-start | bytes 294916
  160.6 6.3 %copy-start.1 = (f32[2,24,512]{2,1,0:T(8,128)S(1)}, f32[2,24,512]{2,1,0:T(8,128)}, u32[]{:S(2)}) copy-start(f32[2,24,512]{2,1,0:T(8,128)} %param.27) | copy-start | bytes 294916
  160.6 7.0 %copy-start.3 = (bf16[256,512]{1,0:T(8,128)(2,1)S(1)}, bf16[256,512]{1,0:T(8,128)(2,1)}, u32[]{:S(2)}) copy-start(bf16[256,512]{1,0:T(8,128)(2,1)} %get-tuple-element.69) | copy-start | bytes 786436
  160.6 7.7 %copy-start = (bf16[2048,512]{1,0:T(8,128)(2,1)S(1)}, bf16[2048,512]{1,0:T(8,128)(2,1)}, u32[]{:S(2)}) copy-start(bf16[2048,512]{1,0:T(8,128)(2,1)} %get-tuple-element.70) | copy-start | bytes 6291460

commit v4 on v3

v4 whole, which is shorter than its diff:
```python
import functools

import jax
import jax.numpy as jnp
from jax import lax
from jax.experimental import pallas as pl
from jax.experimental.pallas import tpu as pltpu
from jax.sharding import PartitionSpec as P

NORM_EPS = 1e-5
LEARN_RATE = 1e-3
BETA_ONE = 0.9
BETA_TWO = 0.95
ADAM_EPS = 1e-8
DECAY = 0.1
STEP = 10

MESH_ID = pl.DeviceIdType.MESH
ORDERS = ((0, 1, 2), (1, 2, 0), (2, 0, 1))
RING = 4
HOPS = (1, -1, 2)


class Place:
    def __init__(self):
        chip = lax.axis_index('dp')
        self.core = lax.axis_index('sp')
        self.at = (lax.rem(chip // 16, 4), lax.rem(chip // 4, 4), lax.rem(chip, 4))

    def step(self, dim, delta):
        return lax.rem(self.at[dim] + (delta + RING), RING)

    def chip(self, dim, delta):
        pos = list(self.at)
        pos[dim] = self.step(dim, delta)
        return {'dp': pos[0] * 16 + pos[1] * 4 + pos[2]}

    def partner(self):
        return {'sp': 1 - self.core}

    def peers(self):
        return [self.partner()] + [self.chip(dim, delta) for dim in range(3) for delta in HOPS]

    def barrier(self):
        sem = pltpu.get_barrier_semaphore()
        peers = self.peers()
        for peer in peers:
            pl.semaphore_signal(sem, inc=1, device_id=peer, device_id_type=MESH_ID)
        pl.semaphore_wait(sem, len(peers))


class Wire:
    def __init__(self, send_sem, recv_sem):
        self.sems = (send_sem, recv_sem)
        self.slots = {}
        self.parts = {}

    def describe(self, key):
        source, target, where = self.parts[key]
        slot = self.slots.setdefault(key, len(self.slots))
        return pltpu.make_async_remote_copy(src_ref=source(), dst_ref=target(), send_sem=self.sems[0].at[slot], recv_sem=self.sems[1].at[slot], device_id=where(), device_id_type=MESH_ID)

    def start(self, key, source, target, where):
        self.parts[key] = (source, target, where)
        self.describe(key).start()

    def wait_recv(self, key):
        self.describe(key).wait_recv()

    def finish(self):
        for key in list(self.parts):
            self.describe(key).wait_send()


class Credit:
    def __init__(self, place, sem):
        self.place, self.sem = place, sem

    def stage(self, number):
        pl.semaphore_signal(self.sem, inc=1, device_id=self.place.partner(), device_id_type=MESH_ID)


def split_groups(count):
    base, extra = divmod(count, 3)
    sizes = [base + (1 if g < extra else 0) for g in range(3)]
    starts = [sum(sizes[:g]) for g in range(3)]
    return list(zip(starts, sizes))


class Gather:
    def __init__(self, name, place, wire, src_ref, grid_ref):
        self.name, self.place, self.wire = name, place, wire
        self.src, self.grid = src_ref, grid_ref
        self.half = src_ref.shape[0] // 2
        self.first = place.core * self.half
        self.groups = split_groups(self.half)
        self.shared = []

    def region(self, g, phase, delta, side=None):
        order = ORDERS[g]
        start, size = self.groups[g]
        index = list(self.place.at)
        for q in range(phase):
            index[order[q]] = pl.ds(0, RING)
        index[order[phase]] = self.place.step(order[phase], delta)
        if side is not None:
            index[order[0]] = pl.ds(2 * side, 2)
        return self.grid.at[index[0], index[1], index[2], pl.ds(self.first + start, size)]

    def send(self, g, phase, delta, toward, tag, side=None):
        dim = ORDERS[g][phase]
        piece = functools.partial(self.region, g, phase, delta, side)
        origin = piece
        if phase == 0:
            start, size = self.groups[g]
            origin = lambda: self.src.at[pl.ds(self.first + start, size)]
        self.wire.start((self.name, g, phase, tag), origin, piece, lambda: self.place.chip(dim, toward))

    def share(self, g, phase, delta):
        key = (self.name, g, phase, 'share', delta)
        self.shared.append(key)
        piece = functools.partial(self.region, g, phase, delta)
        self.wire.start(key, piece, piece, self.place.partner)

    def begin(self, phase):
        for g in range(3):
            for toward in (HOPS if phase < 2 else (1, -1)):
                self.send(g, phase, 0, toward, toward)

    def arrived(self, g, phase, tag):
        self.wire.wait_recv((self.name, g, phase, tag))

    def stage(self, number):
        if number == 0:
            self.begin(0)
        elif number in (1, 2):
            for g in range(3):
                for toward in HOPS:
                    self.arrived(g, number - 1, toward)
            self.begin(number)
            for g in range(3):
                for toward in HOPS:
                    self.share(g, number - 1, -toward)
        elif number == 3:
            for g in range(3):
                self.arrived(g, 2, 1)
                self.send(g, 2, -1, 1, 'on_right', 0)
                self.arrived(g, 2, -1)
                self.send(g, 2, 1, -1, 'on_left', 1)
            for g in range(3):
                self.share(g, 2, -1)
                self.share(g, 2, 1)
        elif number == 4:
            for g in range(3):
                self.arrived(g, 2, 'on_right')
                self.arrived(g, 2, 'on_left')
                self.share(g, 2, 2)
        else:
            for key in self.shared:
                self.wire.wait_recv(key)


GATHER_COPIES = 3 * (3 + 3 + 4 + 3 + 3 + 3)


class Reduce:
    def __init__(self, name, place, wire, source, first, count, bufs, out_ref, out_first, own=None, load_sem=None):
        self.name, self.place, self.wire = name, place, wire
        self.source, self.first, self.count = source, first, count // 2
        self.theirs, self.boxes = bufs[0], bufs[1:10]
        self.out, self.out_first, self.load_sem = out_ref, out_first, load_sem
        self.own, self.base = (source, first + place.core * self.count) if own is None else (own, 0)
        self.groups = split_groups(self.count)
        self.turns = (2, 1, -1, 0)

    def index_of(self, g, phase, delta, side=None):
        order = ORDERS[g]
        index = [pl.ds(0, RING)] * 3
        for q in range(phase):
            index[order[q]] = self.place.at[order[q]]
        index[order[phase]] = self.place.step(order[phase], delta)
        if side is not None:
            index[order[phase + 1]] = pl.ds(2 * side, 2)
        return index

    def kept(self, g, phase, delta, side=None):
        index = self.index_of(g, phase, delta, side)
        start, size = self.groups[g]
        return self.own.at[index[0], index[1], index[2], pl.ds(self.base + start, size)]

    def piece(self, g, delta, core):
        index = self.index_of(g, 0, delta)
        start, size = self.groups[g]
        return self.source.at[index[0], index[1], index[2], pl.ds(self.first + core * self.count + start, size)]

    def slot(self, g, delta):
        index = self.index_of(g, 0, delta)
        return self.theirs.at[index[0], index[1], index[2], pl.ds(*self.groups[g])]

    def load(self, g, delta):
        return pltpu.make_async_copy(self.piece(g, delta, self.place.core), self.kept(g, 0, delta), self.load_sem.at[self.turns.index(delta) * 3 + g])

    def ready(self, g, delta):
        if self.load_sem is not None:
            self.load(g, delta).wait()
        self.wire.wait_recv((self.name, 'swap', g, delta))
        target = self.kept(g, 0, delta)
        target[...] = target[...] + self.slot(g, delta)[...]

    def box(self, g, phase, number):
        return self.boxes[g * 3 + phase].at[number]

    def send(self, g, phase, tag, delta, side, number, toward):
        dim = ORDERS[g][phase]
        self.wire.start((self.name, g, phase, tag), functools.partial(self.kept, g, phase, delta, side), functools.partial(self.box, g, phase, number), lambda: self.place.chip(dim, toward))

    def absorb(self, g, phase, tag, delta, side, number):
        self.wire.wait_recv((self.name, g, phase, tag))
        target = self.kept(g, phase, delta, side)
        target[...] = target[...] + self.box(g, phase, number)[...]

    def far(self, g, phase):
        self.send(g, phase, 'far_right', 2, 0, 0, 1)
        self.send(g, phase, 'far_left', 2, 1, 2, -1)

    def near(self, g, phase):
        self.send(g, phase, 'near_right', 1, 1, 1, 1)
        self.send(g, phase, 'near_left', -1, 0, 3, -1)

    def onward(self, g, phase):
        self.absorb(g, phase, 'far_right', 1, 0, 0)
        self.send(g, phase, 'sum_right', 1, 0, 4, 1)
        self.absorb(g, phase, 'far_left', -1, 1, 2)
        self.send(g, phase, 'sum_left', -1, 1, 5, -1)

    def settle(self, g, phase):
        for tag, number, side in (('near_left', 3, 0), ('near_right', 1, 1), ('sum_right', 4, 0), ('sum_left', 5, 1)):
            self.absorb(g, phase, tag, 0, side, number)

    def stage(self, number):
        if number == 0:
            for delta in self.turns:
                for g in range(3):
                    if self.load_sem is not None:
                        self.load(g, delta).start()
                    self.wire.start((self.name, 'swap', g, delta), functools.partial(self.piece, g, delta, 1 - self.place.core), functools.partial(self.slot, g, delta), self.place.partner)
        elif number == 1:
            for g in range(3):
                self.ready(g, 2)
                self.far(g, 0)
            for g in range(3):
                self.ready(g, 1)
                self.ready(g, -1)
                self.near(g, 0)
        elif number == 2:
            for g in range(3):
                self.onward(g, 0)
            for g in range(3):
                self.ready(g, 0)
        elif number == 3:
            for g in range(3):
                self.settle(g, 0)
                self.far(g, 1)
                self.near(g, 1)
        elif number == 4:
            for g in range(3):
                self.onward(g, 1)
        elif number == 5:
            for g in range(3):
                self.settle(g, 1)
                for n, toward in enumerate(HOPS):
                    self.send(g, 2, toward, toward, None, n, toward)
        elif number == 6:
            for g in range(3):
                for n, toward in enumerate(HOPS):
                    self.absorb(g, 2, toward, 0, None, n)
            span = lambda: self.out.at[self.place.core, pl.ds(self.out_first, self.count)]
            span()[...] = self.own[self.place.at[0], self.place.at[1], self.place.at[2], pl.ds(self.base, self.count)]
            self.wire.start((self.name, 'result'), span, span, self.place.partner)
        else:
            self.wire.wait_recv((self.name, 'result'))


def box_shapes(count):
    out = []
    for g, (_, size) in enumerate(split_groups(count)):
        order = ORDERS[g]
        dims = {dim: RING for dim in range(3) if dim != order[0]}
        dims[order[1]] = 2
        out.append((6,) + tuple(dims[dim] for dim in sorted(dims)) + (size, 8, 128))
        out.append((6, 2, size, 8, 128))
        out.append((3, size, 8, 128))
    return out


def reduce_scratch(count):
    grid = pltpu.VMEM((RING, RING, RING, count, 8, 128), jnp.float32)
    return [grid] + [pltpu.VMEM(shape, jnp.float32) for shape in box_shapes(count)]


REDUCE_COPIES = 12 + 3 * 15 + 1


TILE = 256
NODE_TILE = TILE // 8
BF16 = jnp.bfloat16
F32 = jnp.float32


def dot(left, right, left_dim=1, right_dim=0):
    return lax.dot_general(left, right, (((left_dim,), (right_dim,)), ((), ())), preferred_element_type=F32)


def split_three(values):
    high = values.astype(BF16)
    rest = values - high.astype(F32)
    mid = rest.astype(BF16)
    low = (rest - mid.astype(F32)).astype(BF16)
    return high, mid, low


def dot_wide(values, right, right_dim=0):
    high, mid, low = split_three(values)
    return dot(high, right, 1, right_dim) + dot(mid, right, 1, right_dim) + dot(low, right, 1, right_dim)


def dot_wide_rows(left, values):
    high, mid, low = split_three(values)
    return dot(left, high, 0, 0) + dot(left, mid, 0, 0) + dot(left, low, 0, 0)


def norm_stats(out_b):
    values = out_b.astype(F32)
    centered = values - jnp.mean(values, axis=-1, keepdims=True)
    inv_std = lax.rsqrt(jnp.mean(centered * centered, axis=-1, keepdims=True) + NORM_EPS)
    return centered * inv_std, inv_std


def mlp_forward(pre_act, w_two, gain, bias):
    pre_b = pre_act.astype(BF16)
    hidden = jax.nn.silu(pre_b.astype(F32)).astype(BF16)
    out_b = dot(hidden, w_two).astype(BF16)
    normed, _ = norm_stats(out_b)
    return normed * gain + bias, pre_b, out_b


def mlp_cotangents(d_branch, pre_b, out_b, w_two, gain):
    normed, inv_std = norm_stats(out_b)
    d_norm = d_branch * gain
    d_out = (inv_std * (d_norm - jnp.mean(d_norm, axis=-1, keepdims=True) - normed * jnp.mean(d_norm * normed, axis=-1, keepdims=True))).astype(BF16)
    d_act = dot(d_out, w_two, 1, 1).astype(BF16)
    pre_f = pre_b.astype(F32)
    gate = jax.nn.sigmoid(pre_f)
    hidden = (pre_f * gate).astype(BF16)
    d_pre = (d_act.astype(F32) * gate * (1.0 + pre_f * (1.0 - gate))).astype(BF16)
    d_gain = (d_branch * normed).reshape(-1, 8, d_branch.shape[-1]).sum(axis=0)
    d_bias = d_branch.reshape(-1, 8, d_branch.shape[-1]).sum(axis=0)
    return d_out, hidden, d_pre, d_gain, d_bias


def receiver_pick(copies):
    rows = lax.broadcasted_iota(jnp.int32, (TILE, copies * NODE_TILE), 0)
    cols = lax.broadcasted_iota(jnp.int32, (TILE, copies * NODE_TILE), 1)
    return lax.shift_right_logical(rows, 3) == lax.bitwise_and(cols, NODE_TILE - 1)


def as_bf16(flags):
    return jnp.where(flags, 1.0, 0.0).astype(BF16)


def unpack_weights(grid, w_e1, w_e2, w_n1, w_n2, norms):
    def pair(p, carry):
        at = (p // 8, lax.rem(p // 2, 4))
        x = lax.rem(p, 2) * 2
        for k in range(4):
            lanes = pl.ds(128 * k, 128)
            for dev in range(2):
                w_e1[pl.ds(pl.multiple_of(48 * p + 32 * dev, 16), 16), lanes] = grid[at[0], at[1], x + dev, k]
                w_n1[pl.ds(pl.multiple_of(32 * p + 16 * dev, 16), 16), lanes] = grid[at[0], at[1], x + dev, 4 + k]
            for ref, first, tile, top in ((w_e1, 48 * p + 16, 8, 0), (w_e2, 16 * p, 8, 8), (w_n2, 16 * p, 12, 0)):
                even = grid[at[0], at[1], x, tile + k].astype(F32)[top:top + 8]
                odd = grid[at[0], at[1], x + 1, tile + k].astype(F32)[top:top + 8]
                ref[pl.ds(pl.multiple_of(first, 16), 16), lanes] = jnp.concatenate([even, odd], axis=0).astype(BF16)
        return carry
    lax.fori_loop(0, 32, pair, 0)
    for k in range(4):
        total = grid[k, 0, 0, 12].astype(F32)
        for d in range(1, 16):
            total = total + grid[k, d // 4, d % 4, 12].astype(F32)
        norms[:, 128 * k:128 * k + 128] = total[8:16]


def fill_columns(snd_rows, mask_rows, snd_col, mask_col):
    for rows, col in ((snd_rows, snd_col), (mask_rows, mask_col)):
        turned = rows[...].astype(F32).T
        for n in range(rows.shape[0]):
            col[128 * n:128 * n + 128, :] = turned[:, n:n + 1]


def edge_forward(layer_io, hook, edge_out, pre_out, out_out, sums_out, w_e1, w_e2, norms, recv_terms):
    node_all, node_own, edge_in, snd_col, mask_col = layer_io
    for part, term in enumerate(split_three(dot(node_own[...], w_e1[1024:1536]))):
        recv_terms[part] = term

    def tile(i, carry):
        rows = pl.ds(pl.multiple_of(i * TILE, TILE), TILE)
        nodes = pl.ds(pl.multiple_of(i * NODE_TILE, NODE_TILE), NODE_TILE)
        ids = lax.broadcasted_iota(jnp.int32, (TILE, 512), 1)
        sender = dot(as_bf16(snd_col[rows].astype(jnp.int32) == ids), node_all[...]).astype(BF16)
        recv = jnp.concatenate([recv_terms[0, nodes], recv_terms[1, nodes], recv_terms[2, nodes]], axis=0)
        edge = edge_in[rows]
        pre = dot(edge, w_e1[0:512]) + dot(sender, w_e1[512:1024]) + dot(as_bf16(receiver_pick(3)), recv)
        branch, pre_b, out_b = mlp_forward(pre, w_e2[...], norms[0:1], norms[1:2])
        edge_new = (edge.astype(F32) + branch).astype(BF16)
        pre_out[rows] = pre_b
        out_out[rows] = out_b
        if edge_out is not None:
            edge_out[rows] = edge_new
        picked = jnp.where(receiver_pick(1), mask_col[rows], 0.0).astype(BF16)
        sums_out[nodes] = dot(picked, edge_new, 0, 0).astype(BF16)
        hook(i)
        return carry
    lax.fori_loop(0, edge_in.shape[0] // TILE, tile, 0)


def node_forward(node_own, sums, w_n1, w_n2, norms):
    pre = dot(node_own[...], w_n1[0:512]) + dot(sums[...], w_n1[512:1024])
    return mlp_forward(pre, w_n2[...], norms[2:3], norms[3:4])


def lane_tiles(values):
    return [values[:, 128 * k:128 * k + 128].reshape(-1, 8, 128) for k in range(4)]


def tile_at(tile):
    return tile + tile // 8 if tile < 16 else tile + 2


def store_square(grad_ref, values, first_tile):
    for k, tiles in enumerate(lane_tiles(values)):
        grad_ref[:, :, :, tile_at(first_tile + k)] = tiles.reshape(4, 4, 4, 8, 128)


def store_double(grad_ref, values, first_tile, part):
    for k, tiles in enumerate(lane_tiles(values)):
        tiles = tiles.reshape(2, 4, 4, 2, 8, 128)
        for r in range(2):
            grad_ref[2 * part:2 * part + 2, :, :, tile_at(first_tile + 4 * r + k)] = tiles[:, :, :, r]


def store_triple(grad_ref, values, first_pair):
    for n in range(values.shape[0] // 96):
        pair = first_pair + n
        for k, tiles in enumerate(lane_tiles(values[96 * n:96 * n + 96])):
            tiles = tiles.reshape(4, 3, 8, 128)
            for r in range(3):
                grad_ref[pair // 4, pair % 4, :, tile_at(4 * r + k)] = tiles[:, r]


def layer_back(layer_io, d_node_new, d_edge_new, pre_e, out_e, sums, pre_n, out_n, mats, norms, snd_rows, outs, scratch, after_nodes, hook, pass_on):
    node_all, node_own, edge_in, snd_col, mask_col = layer_io
    w_e1, w_e2, w_n1, w_n2 = mats
    grad_ref, d_edge, d_local, scattered = outs
    hidden_s, d_pre_s, d_out_s, d_sum_s, recv_s, gain_s = scratch
    d_out_n, hidden_n, d_pre_n, d_gain_n, d_bias_n = mlp_cotangents(d_node_new, pre_n, out_n, w_n2[...], norms[2:3])
    d_sum_s[...] = dot(d_pre_n, w_n1[512:1024], 1, 1).astype(BF16)
    d_local[...] = d_node_new + dot(d_pre_n, w_n1[0:512], 1, 1)
    store_square(grad_ref, dot(hidden_n, d_out_n, 0, 0), 24)
    store_double(grad_ref, dot(node_own[...], d_pre_n, 0, 0), 16, 0)
    store_double(grad_ref, dot(sums[...], d_pre_n, 0, 0), 16, 1)
    after_nodes()
    gain_s[...] = jnp.zeros_like(gain_s)

    def tile(i, carry):
        rows = pl.ds(pl.multiple_of(i * TILE, TILE), TILE)
        nodes = pl.ds(pl.multiple_of(i * NODE_TILE, NODE_TILE), NODE_TILE)
        pick = receiver_pick(1)
        picked = jnp.where(pick, mask_col[rows], 0.0).astype(BF16)
        d_res = (d_edge_new[rows].astype(F32) + dot(picked, d_sum_s[nodes])).astype(BF16).astype(F32)
        d_out, hidden, d_pre, d_gain, d_bias = mlp_cotangents(d_res, pre_e[rows], out_e[rows], w_e2[...], norms[0:1])
        gain_s[0] = gain_s[0] + d_gain
        gain_s[1] = gain_s[1] + d_bias
        hidden_s[rows] = hidden
        d_out_s[rows] = d_out
        d_pre_s[rows] = d_pre
        d_edge[rows] = d_res.astype(BF16)
        recv_s[nodes] = dot(as_bf16(pick), d_pre, 0, 0)
        hook(i)
        return carry
    lax.fori_loop(0, edge_in.shape[0] // TILE, tile, 0)
    store_square(grad_ref, dot(hidden_s[...], d_out_s[...], 0, 0), 12)
    upper = dot(edge_in[...], d_pre_s[...], 0, 0)
    store_triple(grad_ref, upper[0:480], 0)
    snd_row = jnp.concatenate([snd_rows[n:n + 1] for n in range(snd_rows.shape[0])], axis=1)
    for block in range(4):
        ids = lax.broadcasted_iota(jnp.int32, (128, edge_in.shape[0]), 0) + 128 * block
        scattered[128 * block:128 * block + 128] = dot(as_bf16(snd_row == ids), d_pre_s[...])
    pass_on()
    middle = dot_wide_rows(node_all[...], scattered[...])
    store_triple(grad_ref, jnp.concatenate([upper[480:512], middle[0:448]], axis=0), 5)
    lower = dot_wide_rows(node_own[...], recv_s[...])
    store_triple(grad_ref, jnp.concatenate([middle[448:512], lower], axis=0), 10)
    for part, (gain, bias) in enumerate(((gain_s[0], gain_s[1]), (d_gain_n, d_bias_n))):
        full = jnp.concatenate([gain.sum(axis=0, keepdims=True), bias.sum(axis=0, keepdims=True), jnp.zeros((6, 512), F32)], axis=0)
        for k in range(4):
            grad_ref[k, :, :, 8 + 9 * part] = jnp.broadcast_to(full[:, 128 * k:128 * k + 128], (4, 4, 8, 128))


def layer_back_late(w_e1, d_edge, d_local, scratch):
    d_pre_s, recv_s = scratch[1], scratch[4]

    def tile(i, carry):
        rows = pl.ds(pl.multiple_of(i * TILE, TILE), TILE)
        d_edge[rows] = (d_edge[rows].astype(F32) + dot(d_pre_s[rows], w_e1[0:512], 1, 1)).astype(BF16)
        return carry
    lax.fori_loop(0, d_edge.shape[0] // TILE, tile, 0)
    d_local[...] = d_local[...] + dot_wide(recv_s[...], w_e1[1024:1536], 1)


def half_of(ref, core):
    count = ref.shape[0] // 2
    return ref.at[pl.ds(pl.multiple_of(core * count, count), count)]


def no_hook(i):
    return None


def at_tile(plan):
    def hook(i):
        for tile, stages in plan.items():
            @pl.when(i == tile)
            def _():
                for plan_of, number in stages:
                    plan_of.stage(number)
    return hook


def pack_shard(layer, masters, shard, norm_pad):
    edge_one, edge_two, node_one, node_two, norm_rows = masters
    chip = lax.axis_index('dp')
    odd = lax.rem(chip, 2) == 1
    norm_pad[...] = jnp.zeros_like(norm_pad)
    norm_pad[0:4, 0:8] = norm_rows[layer]
    placed = pltpu.roll(norm_pad[...], lax.rem(chip, 16) * 8, 1)
    for k in range(4):
        lanes = slice(128 * k, 128 * k + 128)
        first, mid, last = edge_one[layer, 0:8, lanes], edge_one[layer, 8:16, lanes], edge_one[layer, 16:24, lanes]
        shard[k] = jnp.concatenate([jnp.where(odd, mid, first), jnp.where(odd, last, mid)], axis=0).astype(BF16)
        shard[4 + k] = node_one[layer, :, lanes].astype(BF16)
        shard[8 + k] = jnp.concatenate([jnp.where(odd, first, last), edge_two[layer, :, lanes]], axis=0).astype(BF16)
        shard[12 + k] = jnp.concatenate([node_two[layer, :, lanes], placed if k == 0 else jnp.zeros_like(placed)], axis=0).astype(BF16)


def node_cotangent(d_local, scattered, returned, w_above, core):
    return (d_local[...] + dot_wide(half_of(scattered, core)[...] + returned[...], w_above[512:1024], 1)).astype(BF16)


def pack_kernel(edge_one, edge_two, node_one, node_two, norm_rows, shard_low, shard_high, norm_pad):
    for layer, shard in enumerate((shard_low, shard_high)):
        pack_shard(layer, (edge_one, edge_two, node_one, node_two, norm_rows), shard, norm_pad)


def pack_call(masters):
    spec = pl.BlockSpec(memory_space=pltpu.VMEM)
    shard = jax.ShapeDtypeStruct((16, 16, 128), BF16)
    return pl.pallas_call(pack_kernel, out_shape=[shard, shard], in_specs=[spec] * 5, out_specs=[spec] * 2, scratch_shapes=[pltpu.VMEM((8, 128), F32)], compiler_params=pltpu.CompilerParams(vmem_limit_bytes=67043328), name='pack')(*masters)


def step_kernel(shard_low, shard_high, node_in, snd_rows, mask_rows, node_cot, edge_lat, edge_cot, grad_node, d_edge, total, node_all, node_all_one, edge_in, pre_low, out_low, pre_high, out_high, d_pre, snd_col, mask_col, sums_low, sums_high, pre_node, out_node, recv_terms, d_sum, recv_sum, gain_sum, d_local, scattered_high, scattered_low, returned_high, returned_low, *rest):
    mats_low, norms_low, mats_high, norms_high = rest[0:4], rest[4], rest[5:9], rest[9]
    load_sem, credit_sem, peer_sem, send_sem, recv_sem = rest[10:]
    wire = Wire(send_sem, recv_sem)
    load_edge = lambda n: pltpu.make_async_copy(edge_lat, edge_in, load_sem.at[n])
    load_cot = lambda: pltpu.make_async_copy(edge_cot, d_edge, load_sem.at[1])
    load_edge(0).start()
    load_cot().start()

    def begin():
        place = Place()
        node_own = half_of(node_all, place.core)
        node_own_one = half_of(node_all_one, place.core)
        return place, (node_all, node_own, edge_in, snd_col, mask_col), (node_all_one, node_own_one, edge_in, snd_col, mask_col)

    def gather_and_first(grid_low, grid_high):
        place, low_io, high_io = begin()
        node_own, node_own_one = low_io[1], high_io[1]
        for shard, grid in ((shard_low, grid_low), (shard_high, grid_high)):
            grid[place.at[0], place.at[1], place.at[2]] = shard[...]
        node_own[...] = node_in[...]
        place.barrier()
        low = Gather('low', place, wire, shard_low, grid_low)
        high = Gather('high', place, wire, shard_high, grid_high)
        low.stage(0)
        high.stage(0)
        wire.start('node', lambda: node_in, lambda: half_of(node_all, place.core), place.partner)
        fill_columns(snd_rows, mask_rows, snd_col, mask_col)
        low.stage(1)
        high.stage(1)
        low.stage(2)
        low.stage(3)
        high.stage(2)
        low.stage(4)
        low.stage(5)
        unpack_weights(grid_low, *mats_low, norms_low)
        wire.wait_recv('node')
        load_edge(0).wait()
        hook = at_tile({1: [(high, 3)], 4: [(high, 4)]})
        edge_forward(low_io, hook, edge_in, pre_low, out_low, sums_low, mats_low[0], mats_low[1], norms_low, recv_terms)
        branch, pre_b, out_b = node_forward(node_own, sums_low, mats_low[2], mats_low[3], norms_low)
        pre_node[...] = pre_b
        out_node[...] = out_b
        node_own_one[...] = (node_own[...].astype(F32) + branch).astype(BF16)
        piece = lambda: half_of(node_all_one, place.core)
        wire.start('node_one', piece, piece, place.partner)
        high.stage(5)
        unpack_weights(grid_high, *mats_high, norms_high)
        wire.wait_recv('node_one')
        wire.finish()
        wire.parts.clear()

    def second_and_back(grad_high, grad_low, theirs_edge, theirs_node, *boxes):
        place, low_io, high_io = begin()
        node_own_one = high_io[1]
        peers = place.peers()
        for peer in peers:
            pl.semaphore_signal(peer_sem, inc=1, device_id=peer, device_id_type=MESH_ID)
        high_node = Reduce('high_node', place, wire, grad_high, 18, 12, (theirs_node,) + boxes[0:9], total, 24)
        high_edge = Reduce('high_edge', place, wire, grad_high, 0, 18, (theirs_edge,) + boxes[9:18], total, 0)
        low_node = Reduce('low_node', place, wire, grad_low, 18, 12, (theirs_node,) + boxes[18:27], total, 9)
        low_edge = Reduce('low_edge', place, wire, grad_low, 0, 18, (theirs_edge,) + boxes[27:36], total, 15)
        edge_forward(high_io, no_hook, None, pre_high, out_high, sums_high, mats_high[0], mats_high[1], norms_high, recv_terms)
        _, pre_n, out_n = node_forward(node_own_one, sums_high, mats_high[2], mats_high[3], norms_high)
        load_cot().wait()

        def pass_on_high():
            wire.start('scattered_high', lambda: half_of(scattered_high, 1 - place.core), lambda: returned_high, place.partner)

        def after_nodes_high():
            pl.semaphore_wait(peer_sem, len(peers))
            high_node.stage(0)
        hook = at_tile({1: [(high_node, 1)], 3: [(high_node, 2), (Credit(place, credit_sem.at[0]), 0)], 5: [(high_node, 3)], 7: [(high_node, 4)]})
        scratch = (pre_high, d_pre, out_high, d_sum, recv_sum, gain_sum)
        layer_back(high_io, node_cot[...].astype(F32), d_edge, pre_high, out_high, sums_high, pre_n, out_n, mats_high, norms_high, snd_rows, (grad_high, d_edge, d_local, scattered_high), scratch, after_nodes_high, hook, pass_on_high)
        load_edge(2).start()
        high_edge.stage(0)
        high_node.stage(5)
        layer_back_late(mats_high[0], d_edge, d_local, scratch)
        wire.wait_recv('scattered_high')
        d_node = node_cotangent(d_local, scattered_high, returned_high, mats_high[0], place.core).astype(F32)
        load_edge(2).wait()

        def pass_on_low():
            wire.start('scattered_low', lambda: half_of(scattered_low, 1 - place.core), lambda: returned_low, place.partner)

        def after_nodes_low():
            high_edge.stage(1)
            pl.semaphore_wait(credit_sem.at[0], 1)
            low_node.stage(0)
        hook = at_tile({0: [(high_node, 6)], 1: [(low_node, 1)], 2: [(high_edge, 2), (Credit(place, credit_sem.at[1]), 0)], 3: [(low_node, 2)], 4: [(high_edge, 3)], 5: [(low_node, 3)], 6: [(high_edge, 4)], 7: [(low_node, 4)]})
        scratch = (pre_low, d_pre, out_low, d_sum, recv_sum, gain_sum)
        layer_back(low_io, d_node, d_edge, pre_low, out_low, sums_low, pre_node[...], out_node[...], mats_low, norms_low, snd_rows, (grad_low, d_edge, d_local, scattered_low), scratch, after_nodes_low, hook, pass_on_low)
        pl.semaphore_wait(credit_sem.at[1], 1)
        low_edge.stage(0)
        high_edge.stage(5)
        low_node.stage(5)
        low_edge.stage(1)
        layer_back_late(mats_low[0], d_edge, d_local, scratch)
        high_edge.stage(6)
        low_node.stage(6)
        low_edge.stage(2)
        wire.wait_recv('scattered_low')
        grad_node[...] = node_cotangent(d_local, scattered_low, returned_low, mats_low[0], place.core)
        for number in (3, 4, 5, 6):
            low_edge.stage(number)
        for plan in (high_node, high_edge, low_node, low_edge):
            plan.stage(7)
        wire.finish()

    grid = pltpu.VMEM((RING, RING, RING, 16, 16, 128), BF16)
    pl.run_scoped(gather_and_first, grid, grid)
    grad = pltpu.VMEM((RING, RING, RING, 30, 8, 128), F32)
    theirs = [pltpu.VMEM((RING, RING, RING, count, 8, 128), F32) for count in (9, 6)]
    boxes = [pltpu.VMEM(shape, F32) for count in (6, 9, 6, 9) for shape in box_shapes(count)]
    pl.run_scoped(second_and_back, grad, grad, *theirs, *boxes)


def step_call(vmem_inputs, hbm_inputs):
    spec = pl.BlockSpec(memory_space=pltpu.VMEM)
    anywhere = pl.BlockSpec(memory_space=pl.ANY)
    edge = ((2048, 512), BF16)
    node = ((256, 512), BF16)
    nodes = ((512, 512), BF16)
    column = ((2048, 1), F32)
    node_wide = ((256, 512), F32)
    nodes_wide = ((512, 512), F32)
    mats = [((1536, 512), BF16), ((512, 512), BF16), ((1024, 512), BF16), ((512, 512), BF16), ((8, 512), F32)]
    scratch = [nodes, nodes, edge, edge, edge, edge, edge, edge, column, column, node, node, node, node, ((3, 256, 512), BF16), node, node_wide, ((2, 8, 512), F32), node_wide, nodes_wide, nodes_wide, node_wide, node_wide] + mats + mats
    copies = 2 * GATHER_COPIES + 4 * REDUCE_COPIES + 4
    return pl.pallas_call(
        step_kernel,
        out_shape=[jax.ShapeDtypeStruct(*node), jax.ShapeDtypeStruct(*edge), jax.ShapeDtypeStruct((2, 30, 8, 128), F32)],
        in_specs=[spec] * len(vmem_inputs) + [anywhere] * len(hbm_inputs),
        out_specs=[spec] * 3,
        scratch_shapes=[pltpu.VMEM(*entry) for entry in scratch] + [pltpu.SemaphoreType.DMA((3,)), pltpu.SemaphoreType.REGULAR((2,)), pltpu.SemaphoreType.REGULAR, pltpu.SemaphoreType.DMA((copies,)), pltpu.SemaphoreType.DMA((copies,))],
        compiler_params=pltpu.CompilerParams(collective_id=1, has_side_effects=True, vmem_limit_bytes=67043328),
        cost_estimate=pl.CostEstimate(flops=27 * 10 ** 9, bytes_accessed=20 * 2 ** 20, transcendentals=0),
        name='train_step',
    )(*vmem_inputs, *hbm_inputs)


def update_kernel(total, node_in, edge_in, *refs):
    refs[-2][...] = node_in[...]
    refs[-1][...] = edge_in[...]
    masters, ones, twos, new_masters, new_ones, new_twos = [refs[5 * n:5 * n + 5] for n in range(6)]

    def apply(slot, index, grad):
        master, one, two = adamw_update(masters[slot][index], grad, ones[slot][index], twos[slot][index])
        new_masters[slot][index] = master
        new_ones[slot][index] = one
        new_twos[slot][index] = two

    shift = lax.rem(16 - lax.rem(lax.axis_index('dp'), 16), 16) * 8
    for layer in range(2):
        edge_first = 15 if layer == 0 else 0
        for slot, (first, rows) in enumerate(((0, 3), (12, 1), (16, 2), (24, 1))):
            for r in range(rows):
                for k in range(4):
                    tile = first + 4 * r + k
                    if tile < 16:
                        grad = total[tile // 8, edge_first + tile % 8]
                    else:
                        grad = total[(tile - 16) // 6, 9 + 15 * layer + (tile - 16) % 6]
                    apply(slot, (layer, slice(8 * r, 8 * r + 8), slice(128 * k, 128 * k + 128)), grad)
        for part in range(2):
            turned = pltpu.roll(total[part, edge_first + 8], shift, 1)
            apply(4, (layer, slice(2 * part, 2 * part + 2), slice(0, 8)), turned[0:2, 0:8])


def update_call(total, grad_node, grad_edge, masters, ones, twos):
    spec = pl.BlockSpec(memory_space=pltpu.VMEM)
    shapes = [jax.ShapeDtypeStruct(array.shape, array.dtype) for array in masters + ones + twos + (grad_node, grad_edge)]
    return tuple(pl.pallas_call(update_kernel, out_shape=shapes, in_specs=[spec] * 18, out_specs=[spec] * 17, compiler_params=pltpu.CompilerParams(vmem_limit_bytes=67043328), name='update')(total, grad_node, grad_edge, *masters, *ones, *twos))


def adamw_update(master, grad_sum, moment_one, moment_two):
    corr_one = 1.0 - BETA_ONE ** STEP
    corr_two = 1.0 - BETA_TWO ** STEP
    one_new = BETA_ONE * moment_one + (1.0 - BETA_ONE) * grad_sum
    two_new = BETA_TWO * moment_two + (1.0 - BETA_TWO) * grad_sum * grad_sum
    direction = (one_new / corr_one) / (jnp.sqrt(two_new / corr_two) + ADAM_EPS)
    return master - LEARN_RATE * (direction + DECAY * master), one_new, two_new


def solution(mesh):
    lat_spec = P('dp', 'sp', None)
    edge_spec = P('sp')
    mat_spec = P(None, 'dp', None)
    norm_spec = P(None, None, 'dp')
    param_specs = (mat_spec, mat_spec, mat_spec, mat_spec, norm_spec)

    def train_step(node_lat, edge_lat, senders, edge_mask, node_cot, edge_cot, *params):
        masters, ones, twos = params[0:5], params[5:10], params[10:15]
        snd_rows = senders.reshape(-1, 128)
        mask_rows = edge_mask.reshape(-1, 128)
        grad_node, grad_edge, total = step_call(tuple(pack_call(masters)) + (node_lat[0], snd_rows, mask_rows, node_cot[0]), (edge_lat[0], edge_cot[0]))
        outs = update_call(total, grad_node, grad_edge, masters, ones, twos)
        return outs[:15] + (outs[15][None], outs[16][None])

    return jax.shard_map(train_step, mesh=mesh, in_specs=(lat_spec, lat_spec, edge_spec, edge_spec, lat_spec, lat_spec) + param_specs + param_specs + param_specs, out_specs=param_specs + param_specs + param_specs + (lat_spec, lat_spec), check_vma=False)
```

time: 170 us -> 139 us (0.82)
  Pallas kernels: 154 us -> 138 us
  other arithmetic: 7.4 us -> 0 us
  local copies, waits for them, and re-layouts: 7.02 us -> 0 us
    pallas_call x3, Pallas kernels: 154 us -> 138 us  [the longest x1 133 us: step_call(): pl.pallas_call(step_kernel, out_shape=[jax.ShapeDtypeStruct(*node), jax.S...]
    convert_element_type x5 -> x0, other arithmetic: 3.96 us -> none  [pack_shards(): master.astype(BF16)]
    sub x5 -> x0, other arithmetic: 3.38 us -> none  [adamw_update(): master - LEARN_RATE * (direction + DECAY * master)]
    squeeze x3 -> x0, local copies, waits for them, and re-layouts: 2.39 us -> none  [the longest x1 0.85 us: unpack_grads(): tiles_high = jnp.concatenate([total[0, 0:14], total[1, 0:14]], axis=0)]
    unnamed x41 -> x0, local copies, waits for them, and re-layouts: 2.15 us -> none
where the time goes in v4:
time: 139 us
  Pallas kernels  138 us (99%)
    pallas_call x1, Pallas kernels, step_call(): pl.pallas_call(step_kernel, out_shape=[jax.ShapeDtypeStruct(*node), jax.S...  133 us
    pallas_call x1, Pallas kernels, update_call(): pl.pallas_call(update_kernel, out_shape=shapes, in_specs=[spec] * 18, out...  3.78 us

profile of v4, /device:TPU:1, one launch (start us, length us, event | category | flops | bytes accessed | tf_op | source)
XLA Modules:
  0.0 139.3 jit_solution(14527593305251843345)
XLA Ops:
  0.7 1.7 %pack.1 = (bf16[16,16,128]{2,1,0:T(8,128)(2,1)}, bf16[16,16,128]{2,1,0:T(8,128)(2,1)}) custom-call(f32[2,24,512]{2,1,0:T(8,128)} %refs_0_.1, f32[2,8,512]{2,1,0:T(8,128)} %refs_1_.1, f32[2,16,512]{2,1,0:T(8,128)} %refs_2_.1, f32[2,8,512]{2,1,0:T(8,128)} %refs_3_.1, f32[2,4,8]{2,1,0:T(4,128)} %refs_4_.1), custom_call_target="tpu_custom_call" | custom-call | tf_op jit(solution)/shard_map/pack/pallas_call | solution.py:567
  2.3 133.0 %train_step.1 = (bf16[256,512]{1,0:T(8,128)(2,1)}, bf16[2048,512]{1,0:T(8,128)(2,1)}, f32[2,30,8,128]{3,2,1,0:T(8,128)}) custom-call(bf16[16,16,128]{2,1,0:T(8,128)(2,1)} %get-tuple-element.39.shard_low, bf16[16,16,128]{2,1,0:T(8,128)(2,1)} %get-tuple-element.40.shard_high, bf16[256,512]{1,0:T(8,128)(2,1)} %bitcast.11, s32[16,128]{1,0:T(8,128)} %bitcast.14, ...), custom_call_target="tpu_custom_call" | custom-call | flops 27000000512 | bytes 20971520 | tf_op jit(solution)/shard_map/train_step/pallas_call | solution.py:700
  135.3 3.8 %update.1 = (f32[2,24,512]{2,1,0:T(8,128)}, f32[2,8,512]{2,1,0:T(8,128)}, f32[2,16,512]{2,1,0:T(8,128)}, f32[2,8,512]{2,1,0:T(8,128)}, f32[2,4,8]{2,1,0:T(4,128)...) custom-call(f32[2,30,8,128]{3,2,1,0:T(8,128)} %get-tuple-element.41., ...), custom_call_target="tpu_custom_call" | custom-call | tf_op jit(solution)/shard_map/update/pallas_call | solution.py:743

commit v5 on v4

--- a/solution.py
+++ b/solution.py
@@ -233,6 +233,14 @@
         self.absorb(g, phase, 'far_left', -1, 1, 2)
         self.send(g, phase, 'sum_left', -1, 1, 5, -1)
 
+    def direct(self, g, phase):
+        for n, toward in enumerate(HOPS):
+            self.send(g, phase, toward, toward, None, n, toward)
+
+    def collect(self, g, phase):
+        for n, toward in enumerate(HOPS):
+            self.absorb(g, phase, toward, 0, None, n)
+
     def settle(self, g, phase):
         for tag, number, side in (('near_left', 3, 0), ('near_right', 1, 1), ('sum_right', 4, 0), ('sum_left', 5, 1)):
             self.absorb(g, phase, tag, 0, side, number)
@@ -260,20 +268,16 @@
         elif number == 3:
             for g in range(3):
                 self.settle(g, 0)
-                self.far(g, 1)
-                self.near(g, 1)
+                self.direct(g, 1)
         elif number == 4:
-            for g in range(3):
-                self.onward(g, 1)
+            return
         elif number == 5:
             for g in range(3):
-                self.settle(g, 1)
-                for n, toward in enumerate(HOPS):
-                    self.send(g, 2, toward, toward, None, n, toward)
+                self.collect(g, 1)
+                self.direct(g, 2)
         elif number == 6:
             for g in range(3):
-                for n, toward in enumerate(HOPS):
-                    self.absorb(g, 2, toward, 0, None, n)
+                self.collect(g, 2)
             span = lambda: self.out.at[self.place.core, pl.ds(self.out_first, self.count)]
             span()[...] = self.own[self.place.at[0], self.place.at[1], self.place.at[2], pl.ds(self.base, self.count)]
             self.wire.start((self.name, 'result'), span, span, self.place.partner)
@@ -288,7 +292,7 @@
         dims = {dim: RING for dim in range(3) if dim != order[0]}
         dims[order[1]] = 2
         out.append((6,) + tuple(dims[dim] for dim in sorted(dims)) + (size, 8, 128))
-        out.append((6, 2, size, 8, 128))
+        out.append((3, RING, size, 8, 128))
         out.append((3, size, 8, 128))
     return out
 
@@ -298,10 +302,10 @@
     return [grid] + [pltpu.VMEM(shape, jnp.float32) for shape in box_shapes(count)]
 
 
-REDUCE_COPIES = 12 + 3 * 15 + 1
-
-
-TILE = 256
+REDUCE_COPIES = 12 + 3 * 12 + 1
+
+
+TILE = 512
 NODE_TILE = TILE // 8
 BF16 = jnp.bfloat16
 F32 = jnp.float32
@@ -369,20 +373,20 @@
 
 
 def unpack_weights(grid, w_e1, w_e2, w_n1, w_n2, norms):
-    def pair(p, carry):
-        at = (p // 8, lax.rem(p // 2, 4))
-        x = lax.rem(p, 2) * 2
-        for k in range(4):
-            lanes = pl.ds(128 * k, 128)
-            for dev in range(2):
-                w_e1[pl.ds(pl.multiple_of(48 * p + 32 * dev, 16), 16), lanes] = grid[at[0], at[1], x + dev, k]
-                w_n1[pl.ds(pl.multiple_of(32 * p + 16 * dev, 16), 16), lanes] = grid[at[0], at[1], x + dev, 4 + k]
-            for ref, first, tile, top in ((w_e1, 48 * p + 16, 8, 0), (w_e2, 16 * p, 8, 8), (w_n2, 16 * p, 12, 0)):
-                even = grid[at[0], at[1], x, tile + k].astype(F32)[top:top + 8]
-                odd = grid[at[0], at[1], x + 1, tile + k].astype(F32)[top:top + 8]
-                ref[pl.ds(pl.multiple_of(first, 16), 16), lanes] = jnp.concatenate([even, odd], axis=0).astype(BF16)
+    def row(p, carry):
+        at = (p // 4, lax.rem(p, 4))
+        for x in range(0, 4, 2):
+            for k in range(4):
+                lanes = pl.ds(128 * k, 128)
+                for dev in range(2):
+                    w_e1[pl.ds(pl.multiple_of(96 * p, 32) + (24 * x + 32 * dev), 16), lanes] = grid[at[0], at[1], x + dev, k]
+                    w_n1[pl.ds(pl.multiple_of(64 * p, 64) + 16 * (x + dev), 16), lanes] = grid[at[0], at[1], x + dev, 4 + k]
+                for ref, first, tile, top in ((w_e1, pl.multiple_of(96 * p, 32) + (24 * x + 16), 8, 0), (w_e2, pl.multiple_of(32 * p, 32) + 8 * x, 8, 8), (w_n2, pl.multiple_of(32 * p, 32) + 8 * x, 12, 0)):
+                    even = grid[at[0], at[1], x, tile + k].astype(F32)[top:top + 8]
+                    odd = grid[at[0], at[1], x + 1, tile + k].astype(F32)[top:top + 8]
+                    ref[pl.ds(first, 16), lanes] = jnp.concatenate([even, odd], axis=0).astype(BF16)
         return carry
-    lax.fori_loop(0, 32, pair, 0)
+    lax.fori_loop(0, 16, row, 0)
     for k in range(4):
         total = grid[k, 0, 0, 12].astype(F32)
         for d in range(1, 16):
@@ -397,7 +401,20 @@
             col[128 * n:128 * n + 128, :] = turned[:, n:n + 1]
 
 
-def edge_forward(layer_io, hook, edge_out, pre_out, out_out, sums_out, w_e1, w_e2, norms, recv_terms):
+def pick_senders(snd_col, node_all, rows):
+    ids = lax.broadcasted_iota(jnp.int32, (TILE, 512), 1)
+    return dot(as_bf16(snd_col[rows].astype(jnp.int32) == ids), node_all[...]).astype(BF16)
+
+
+def all_senders(snd_col, node_all, out):
+    def tile(i, carry):
+        rows = pl.ds(pl.multiple_of(i * TILE, TILE), TILE)
+        out[rows] = pick_senders(snd_col, node_all, rows)
+        return carry
+    lax.fori_loop(0, out.shape[0] // TILE, tile, 0)
+
+
+def edge_forward(layer_io, senders, hook, edge_out, pre_out, out_out, sums_out, w_e1, w_e2, norms, recv_terms):
     node_all, node_own, edge_in, snd_col, mask_col = layer_io
     for part, term in enumerate(split_three(dot(node_own[...], w_e1[1024:1536]))):
         recv_terms[part] = term
@@ -405,8 +422,7 @@
     def tile(i, carry):
         rows = pl.ds(pl.multiple_of(i * TILE, TILE), TILE)
         nodes = pl.ds(pl.multiple_of(i * NODE_TILE, NODE_TILE), NODE_TILE)
-        ids = lax.broadcasted_iota(jnp.int32, (TILE, 512), 1)
-        sender = dot(as_bf16(snd_col[rows].astype(jnp.int32) == ids), node_all[...]).astype(BF16)
+        sender = pick_senders(snd_col, node_all, rows) if senders is None else senders[rows]
         recv = jnp.concatenate([recv_terms[0, nodes], recv_terms[1, nodes], recv_terms[2, nodes]], axis=0)
         edge = edge_in[rows]
         pre = dot(edge, w_e1[0:512]) + dot(sender, w_e1[512:1024]) + dot(as_bf16(receiver_pick(3)), recv)
@@ -598,15 +614,16 @@
         low.stage(1)
         high.stage(1)
         low.stage(2)
+        wire.wait_recv('node')
+        all_senders(snd_col, node_all, d_pre)
         low.stage(3)
         high.stage(2)
         low.stage(4)
         low.stage(5)
         unpack_weights(grid_low, *mats_low, norms_low)
-        wire.wait_recv('node')
         load_edge(0).wait()
-        hook = at_tile({1: [(high, 3)], 4: [(high, 4)]})
-        edge_forward(low_io, hook, edge_in, pre_low, out_low, sums_low, mats_low[0], mats_low[1], norms_low, recv_terms)
+        hook = at_tile({0: [(high, 3)], 2: [(high, 4)]})
+        edge_forward(low_io, d_pre, hook, edge_in, pre_low, out_low, sums_low, mats_low[0], mats_low[1], norms_low, recv_terms)
         branch, pre_b, out_b = node_forward(node_own, sums_low, mats_low[2], mats_low[3], norms_low)
         pre_node[...] = pre_b
         out_node[...] = out_b
@@ -629,7 +646,7 @@
         high_edge = Reduce('high_edge', place, wire, grad_high, 0, 18, (theirs_edge,) + boxes[9:18], total, 0)
         low_node = Reduce('low_node', place, wire, grad_low, 18, 12, (theirs_node,) + boxes[18:27], total, 9)
         low_edge = Reduce('low_edge', place, wire, grad_low, 0, 18, (theirs_edge,) + boxes[27:36], total, 15)
-        edge_forward(high_io, no_hook, None, pre_high, out_high, sums_high, mats_high[0], mats_high[1], norms_high, recv_terms)
+        edge_forward(high_io, None, no_hook, None, pre_high, out_high, sums_high, mats_high[0], mats_high[1], norms_high, recv_terms)
         _, pre_n, out_n = node_forward(node_own_one, sums_high, mats_high[2], mats_high[3], norms_high)
         load_cot().wait()
 
@@ -639,13 +656,14 @@
         def after_nodes_high():
             pl.semaphore_wait(peer_sem, len(peers))
             high_node.stage(0)
-        hook = at_tile({1: [(high_node, 1)], 3: [(high_node, 2), (Credit(place, credit_sem.at[0]), 0)], 5: [(high_node, 3)], 7: [(high_node, 4)]})
+        hook = at_tile({1: [(high_node, 1)], 2: [(high_node, 2), (Credit(place, credit_sem.at[0]), 0)], 3: [(high_node, 3)]})
         scratch = (pre_high, d_pre, out_high, d_sum, recv_sum, gain_sum)
         layer_back(high_io, node_cot[...].astype(F32), d_edge, pre_high, out_high, sums_high, pre_n, out_n, mats_high, norms_high, snd_rows, (grad_high, d_edge, d_local, scattered_high), scratch, after_nodes_high, hook, pass_on_high)
         load_edge(2).start()
         high_edge.stage(0)
+        high_node.stage(4)
+        layer_back_late(mats_high[0], d_edge, d_local, scratch)
         high_node.stage(5)
-        layer_back_late(mats_high[0], d_edge, d_local, scratch)
         wire.wait_recv('scattered_high')
         d_node = node_cotangent(d_local, scattered_high, returned_high, mats_high[0], place.core).astype(F32)
         load_edge(2).wait()
@@ -657,22 +675,29 @@
             high_edge.stage(1)
             pl.semaphore_wait(credit_sem.at[0], 1)
             low_node.stage(0)
-        hook = at_tile({0: [(high_node, 6)], 1: [(low_node, 1)], 2: [(high_edge, 2), (Credit(place, credit_sem.at[1]), 0)], 3: [(low_node, 2)], 4: [(high_edge, 3)], 5: [(low_node, 3)], 6: [(high_edge, 4)], 7: [(low_node, 4)]})
+        hook = at_tile({0: [(high_node, 6)], 1: [(low_node, 1)], 2: [(high_edge, 2), (Credit(place, credit_sem.at[1]), 0)]})
         scratch = (pre_low, d_pre, out_low, d_sum, recv_sum, gain_sum)
         layer_back(low_io, d_node, d_edge, pre_low, out_low, sums_low, pre_node[...], out_node[...], mats_low, norms_low, snd_rows, (grad_low, d_edge, d_local, scattered_low), scratch, after_nodes_low, hook, pass_on_low)
         pl.semaphore_wait(credit_sem.at[1], 1)
         low_edge.stage(0)
-        high_edge.stage(5)
-        low_node.stage(5)
+        high_edge.stage(3)
+        low_node.stage(2)
         low_edge.stage(1)
         layer_back_late(mats_low[0], d_edge, d_local, scratch)
-        high_edge.stage(6)
-        low_node.stage(6)
-        low_edge.stage(2)
+        high_edge.stage(4)
+        low_node.stage(3)
         wire.wait_recv('scattered_low')
         grad_node[...] = node_cotangent(d_local, scattered_low, returned_low, mats_low[0], place.core)
-        for number in (3, 4, 5, 6):
-            low_edge.stage(number)
+        low_edge.stage(2)
+        high_edge.stage(5)
+        low_node.stage(4)
+        low_edge.stage(3)
+        low_node.stage(5)
+        high_edge.stage(6)
+        low_edge.stage(4)
+        low_node.stage(6)
+        low_edge.stage(5)
+        low_edge.stage(6)
         for plan in (high_node, high_edge, low_node, low_edge):
             plan.stage(7)
         wire.finish()

time: 139 us -> 122 us (0.88)
  Pallas kernels: 138 us -> 121 us
    pallas_call x1, Pallas kernels: 133 us -> 116 us  [step_call(): pl.pallas_call(step_kernel, out_shape=[jax.ShapeDtypeStruct(*node), jax.S...]
where the time goes in v5:
time: 122 us
  Pallas kernels  121 us (99%)
    pallas_call x1, Pallas kernels, step_call(): pl.pallas_call(step_kernel, out_shape=[jax.ShapeDtypeStruct(*node), jax.S...  116 us
    pallas_call x1, Pallas kernels, update_call(): pl.pallas_call(update_kernel, out_shape=shapes, in_specs=[spec] * 18, out...  3.78 us

profile of v5, /device:TPU:1, one launch (start us, length us, event | category | flops | bytes accessed | tf_op | source)
XLA Modules:
  0.0 122.0 jit_solution(3744371016499613856)
XLA Ops:
  0.7 1.7 %pack.1 = (bf16[16,16,128]{2,1,0:T(8,128)(2,1)}, bf16[16,16,128]{2,1,0:T(8,128)(2,1)}) custom-call(f32[2,24,512]{2,1,0:T(8,128)} %refs_0_.1, f32[2,8,512]{2,1,0:T(8,128)} %refs_1_.1, f32[2,16,512]{2,1,0:T(8,128)} %refs_2_.1, f32[2,8,512]{2,1,0:T(8,128)} %refs_3_.1, f32[2,4,8]{2,1,0:T(4,128)} %refs_4_.1), custom_call_target="tpu_custom_call" | custom-call | tf_op jit(solution)/shard_map/pack/pallas_call | solution.py:583
  2.3 115.7 %train_step.1 = (bf16[256,512]{1,0:T(8,128)(2,1)}, bf16[2048,512]{1,0:T(8,128)(2,1)}, f32[2,30,8,128]{3,2,1,0:T(8,128)}) custom-call(bf16[16,16,128]{2,1,0:T(8,128)(2,1)} %get-tuple-element.39.shard_low, bf16[16,16,128]{2,1,0:T(8,128)(2,1)} %get-tuple-element.40.shard_high, bf16[256,512]{1,0:T(8,128)(2,1)} %bitcast.11, s32[16,128]{1,0:T(8,128)} %bitcast.14, ...), custom_call_target="tpu_custom_call" | custom-call | flops 27000000512 | bytes 20971520 | tf_op jit(solution)/shard_map/train_step/pallas_call | solution.py:725
  118.0 3.8 %update.1 = (f32[2,24,512]{2,1,0:T(8,128)}, f32[2,8,512]{2,1,0:T(8,128)}, f32[2,16,512]{2,1,0:T(8,128)}, f32[2,8,512]{2,1,0:T(8,128)}, f32[2,4,8]{2,1,0:T(4,128)...) custom-call(f32[2,30,8,128]{3,2,1,0:T(8,128)} %get-tuple-element.41., ...), custom_call_target="tpu_custom_call" | custom-call | tf_op jit(solution)/shard_map/update/pallas_call | solution.py:768

commit v6 on v5

--- a/solution.py
+++ b/solution.py
@@ -583,12 +583,13 @@
     return pl.pallas_call(pack_kernel, out_shape=[shard, shard], in_specs=[spec] * 5, out_specs=[spec] * 2, scratch_shapes=[pltpu.VMEM((8, 128), F32)], compiler_params=pltpu.CompilerParams(vmem_limit_bytes=67043328), name='pack')(*masters)
 
 
-def step_kernel(shard_low, shard_high, node_in, snd_rows, mask_rows, node_cot, edge_lat, edge_cot, grad_node, d_edge, total, node_all, node_all_one, edge_in, pre_low, out_low, pre_high, out_high, d_pre, snd_col, mask_col, sums_low, sums_high, pre_node, out_node, recv_terms, d_sum, recv_sum, gain_sum, d_local, scattered_high, scattered_low, returned_high, returned_low, *rest):
+def step_kernel(shard_low, shard_high, node_in, snd_rows, mask_rows, node_cot, edge_lat, edge_cot, grad_node, edge_out, total, d_edge, node_all, node_all_one, edge_in, pre_low, out_low, pre_high, out_high, d_pre, snd_col, mask_col, sums_low, sums_high, pre_node, out_node, recv_terms, d_sum, recv_sum, gain_sum, d_local, scattered_high, scattered_low, returned_high, returned_low, *rest):
     mats_low, norms_low, mats_high, norms_high = rest[0:4], rest[4], rest[5:9], rest[9]
     load_sem, credit_sem, peer_sem, send_sem, recv_sem = rest[10:]
     wire = Wire(send_sem, recv_sem)
     load_edge = lambda n: pltpu.make_async_copy(edge_lat, edge_in, load_sem.at[n])
     load_cot = lambda: pltpu.make_async_copy(edge_cot, d_edge, load_sem.at[1])
+    store_edge = lambda: pltpu.make_async_copy(d_edge, edge_out, load_sem.at[3])
     load_edge(0).start()
     load_cot().start()
 
@@ -656,12 +657,12 @@
         def after_nodes_high():
             pl.semaphore_wait(peer_sem, len(peers))
             high_node.stage(0)
-        hook = at_tile({1: [(high_node, 1)], 2: [(high_node, 2), (Credit(place, credit_sem.at[0]), 0)], 3: [(high_node, 3)]})
+        hook = at_tile({1: [(high_node, 1)], 2: [(high_node, 2), (Credit(place, credit_sem.at[0]), 0)]})
         scratch = (pre_high, d_pre, out_high, d_sum, recv_sum, gain_sum)
         layer_back(high_io, node_cot[...].astype(F32), d_edge, pre_high, out_high, sums_high, pre_n, out_n, mats_high, norms_high, snd_rows, (grad_high, d_edge, d_local, scattered_high), scratch, after_nodes_high, hook, pass_on_high)
         load_edge(2).start()
         high_edge.stage(0)
-        high_node.stage(4)
+        high_node.stage(3)
         layer_back_late(mats_high[0], d_edge, d_local, scratch)
         high_node.stage(5)
         wire.wait_recv('scattered_high')
@@ -684,6 +685,7 @@
         low_node.stage(2)
         low_edge.stage(1)
         layer_back_late(mats_low[0], d_edge, d_local, scratch)
+        store_edge().start()
         high_edge.stage(4)
         low_node.stage(3)
         wire.wait_recv('scattered_low')
@@ -700,6 +702,7 @@
         low_edge.stage(6)
         for plan in (high_node, high_edge, low_node, low_edge):
             plan.stage(7)
+        store_edge().wait()
         wire.finish()
 
     grid = pltpu.VMEM((RING, RING, RING, 16, 16, 128), BF16)
@@ -720,14 +723,14 @@
     node_wide = ((256, 512), F32)
     nodes_wide = ((512, 512), F32)
     mats = [((1536, 512), BF16), ((512, 512), BF16), ((1024, 512), BF16), ((512, 512), BF16), ((8, 512), F32)]
-    scratch = [nodes, nodes, edge, edge, edge, edge, edge, edge, column, column, node, node, node, node, ((3, 256, 512), BF16), node, node_wide, ((2, 8, 512), F32), node_wide, nodes_wide, nodes_wide, node_wide, node_wide] + mats + mats
+    scratch = [edge, nodes, nodes, edge, edge, edge, edge, edge, edge, column, column, node, node, node, node, ((3, 256, 512), BF16), node, node_wide, ((2, 8, 512), F32), node_wide, nodes_wide, nodes_wide, node_wide, node_wide] + mats + mats
     copies = 2 * GATHER_COPIES + 4 * REDUCE_COPIES + 4
     return pl.pallas_call(
         step_kernel,
         out_shape=[jax.ShapeDtypeStruct(*node), jax.ShapeDtypeStruct(*edge), jax.ShapeDtypeStruct((2, 30, 8, 128), F32)],
         in_specs=[spec] * len(vmem_inputs) + [anywhere] * len(hbm_inputs),
-        out_specs=[spec] * 3,
-        scratch_shapes=[pltpu.VMEM(*entry) for entry in scratch] + [pltpu.SemaphoreType.DMA((3,)), pltpu.SemaphoreType.REGULAR((2,)), pltpu.SemaphoreType.REGULAR, pltpu.SemaphoreType.DMA((copies,)), pltpu.SemaphoreType.DMA((copies,))],
+        out_specs=[spec, anywhere, spec],
+        scratch_shapes=[pltpu.VMEM(*entry) for entry in scratch] + [pltpu.SemaphoreType.DMA((4,)), pltpu.SemaphoreType.REGULAR((2,)), pltpu.SemaphoreType.REGULAR, pltpu.SemaphoreType.DMA((copies,)), pltpu.SemaphoreType.DMA((copies,))],
         compiler_params=pltpu.CompilerParams(collective_id=1, has_side_effects=True, vmem_limit_bytes=67043328),
         cost_estimate=pl.CostEstimate(flops=27 * 10 ** 9, bytes_accessed=20 * 2 ** 20, transcendentals=0),
         name='train_step',

time: 122 us -> 121 us (level)
  no operation moved by 1% of the time
where the time goes in v6:
time: 121 us
  Pallas kernels  120 us (99%)
    pallas_call x1, Pallas kernels, step_call(): pl.pallas_call(step_kernel, out_shape=[jax.ShapeDtypeStruct(*node), jax.S...  114 us
    pallas_call x1, Pallas kernels, update_call(): pl.pallas_call(update_kernel, out_shape=shapes, in_specs=[spec] * 18, out...  3.78 us

profile of v6, /device:TPU:1, one launch (start us, length us, event | category | flops | bytes accessed | tf_op | source)
XLA Modules:
  0.0 120.8 jit_solution(16431788415652178740)
XLA Ops:
  0.7 1.7 %pack.1 = (bf16[16,16,128]{2,1,0:T(8,128)(2,1)}, bf16[16,16,128]{2,1,0:T(8,128)(2,1)}) custom-call(f32[2,24,512]{2,1,0:T(8,128)} %refs_0_.1, f32[2,8,512]{2,1,0:T(8,128)} %refs_1_.1, f32[2,16,512]{2,1,0:T(8,128)} %refs_2_.1, f32[2,8,512]{2,1,0:T(8,128)} %refs_3_.1, f32[2,4,8]{2,1,0:T(4,128)} %refs_4_.1), custom_call_target="tpu_custom_call" | custom-call | tf_op jit(solution)/shard_map/pack/pallas_call | solution.py:583
  2.3 114.5 %train_step.1 = (bf16[256,512]{1,0:T(8,128)(2,1)}, bf16[2048,512]{1,0:T(8,128)(2,1)}, f32[2,30,8,128]{3,2,1,0:T(8,128)}) custom-call(bf16[16,16,128]{2,1,0:T(8,128)(2,1)} %get-tuple-element.39.shard_low, bf16[16,16,128]{2,1,0:T(8,128)(2,1)} %get-tuple-element.40.shard_high, bf16[256,512]{1,0:T(8,128)(2,1)} %bitcast.11, s32[16,128]{1,0:T(8,128)} %bitcast.14, ...), custom_call_target="tpu_custom_call" | custom-call | flops 27000000512 | bytes 20971520 | tf_op jit(solution)/shard_map/train_step/pallas_call | solution.py:728
  116.8 3.8 %update.1 = (f32[2,24,512]{2,1,0:T(8,128)}, f32[2,8,512]{2,1,0:T(8,128)}, f32[2,16,512]{2,1,0:T(8,128)}, f32[2,8,512]{2,1,0:T(8,128)}, f32[2,4,8]{2,1,0:T(4,128)...) custom-call(f32[2,30,8,128]{3,2,1,0:T(8,128)} %get-tuple-element.41., ...), custom_call_target="tpu_custom_call" | custom-call | tf_op jit(solution)/shard_map/update/pallas_call | solution.py:771
